TPU v7x, 128 devices: a whole 4x4x4 slice. The times are simulated.
128 devices in a mesh: cells: 16 (over y, x), mem: 8 (over z, core).
Axes of the slice: x: 4, y: 4, z: 4, core: 2. Of those that a mesh axis runs over, the one named last changes fastest.
Arguments:
- background_realisations: bfloat16 [128, 4096, 128], P('mem', 'cells'), may hold values from -6 to 6
- reading_figures: float32 [4096, 128], P('cells'), may hold values from -6 to 6
- reading_error_spread: float32 [4096, 128], P('cells'), may hold values from 0.5 to 4
- footprint_grid_point: int32 [4096, 128], P('cells'), may hold values from 0 to 31
- active_reading_number: int32 [4096], P('cells'), may hold values from 0 to 128, as said below
- bordering_patches: int32 [4096, 4], P('cells'), may hold values from 0 to 4095, as said below
Outputs:
- analysis: bfloat16 [128, 4096, 128], P('mem', 'cells')
Inputs may be any that keep to these rules, and one draw needn't show every extreme that they name: The live observations of tile t fill its first active_reading_number[t] slots; in every draw some tile has all 128 slots live; counts differ strongly between runs of 32 tiles. `bordering_patches`: each row lists 4 different tiles, never the row's own tile, each at circular distance 1 to 128 from it along the order of the 4096 tiles.
All inputs are finite; a program needn't handle non-finite values.
Results may differ from a plain program's by a relative error of at most 0.01.
Values may be sent and summed in bfloat16 or wider, within the bound.
No kernel may reach another device: no remote copies, remote signals or barrier semaphores. Data moves between devices by JAX's collectives and lax.ppermute only.
A program may use at most 128 MiB of HBM per device.

v0:
```python
import jax
import jax.numpy as jnp
from jax import lax
from jax.experimental import pallas as pl
from jax.experimental.pallas import tpu as pltpu
from jax.sharding import Mesh
from jax.sharding import PartitionSpec as P

F32 = jnp.float32
BF16 = jnp.bfloat16
MEM = ("z", "k")
PACK = 4
UNROLL = 16


def lane_id(rows):
    return lax.broadcasted_iota(jnp.int32, (rows, 128), 1)


def sense_kernel(info, bg, sg, *refs):
    states, buf = refs[:8], refs[8]
    members, tiles, _ = bg.shape
    z, k = info[0], info[1]
    pitch = tiles + 1
    for m in range(members):
        buf[pl.ds(m * pitch, tiles), :] = bg[m].astype(F32)
    quarter = lane_id(members) >> 5
    chunk = tiles // 8
    for n, xd in enumerate(states):
        zone = 2 * ((z + n) % 4) + (k if n < 4 else 1 - k)

        def group(i, carry, xd=xd, zone=zone):
            row = None
            for q in range(PACK):
                x = buf[pl.ds(chunk * zone + PACK * i + q, members, stride=pitch), :]
                xd[PACK * i + q] = x.astype(BF16)
                s = x + 0.5 * pltpu.roll(x, 96, 1)
                s = s if q == 0 else pltpu.roll(s, 32 * q, 1)
                row = s if q == 0 else jnp.where(quarter == q, s, row)
            sg[(chunk // PACK) * zone + i] = row.astype(BF16)
            return carry

        lax.fori_loop(0, chunk // PACK, group, 0, unroll=4)


def window_kernel(info, sg, left, right, *outs):
    half = left.shape[0]
    z = info[0]
    for d, w in enumerate(outs):
        zz = (z + d) % 4

        @pl.when(zz < 2)
        def _():
            for i in range(16):
                w[i] = left[16 * zz + i]
            for j in range(4):
                src = 16 * zz + 16 * (j + 1) - half

                @pl.when(src < 0)
                def _():
                    for i in range(16):
                        w[16 * (j + 1) + i] = left[src + half + i]

                @pl.when(src >= 0)
                def _():
                    for i in range(16):
                        w[16 * (j + 1) + i] = sg[src + i]

        @pl.when(zz >= 2)
        def _():
            for j in range(5):
                src = 16 * zz + 16 * j - half

                @pl.when(src < 2 * half)
                def _():
                    for i in range(16):
                        w[16 * j + i] = sg[src + i]

                @pl.when(src >= 2 * half)
                def _():
                    for i in range(16):
                        w[16 * j + i] = right[src - 2 * half + i]


def cell_kernel(info, pix, w2, y, nbr, out, near, own_nbr):
    groups = pix.shape[0] // PACK

    def packed(ref, p):
        parts = [ref[pl.ds(2 * p + h, groups, stride=PACK), :] for h in range(2)]
        return jnp.concatenate(parts, axis=0).astype(F32).T

    cols = [[], []]
    for p in range(2):
        pt = packed(pix, p)
        wt = packed(w2, p)
        yt = packed(y, p) * wt
        d, e = [], []
        for c in range(32):
            hit = pt == float(c)
            d.append(jnp.sum(jnp.where(hit, wt, 0.0), axis=0, keepdims=True))
            e.append(jnp.sum(jnp.where(hit, yt, 0.0), axis=0, keepdims=True))
        for i, rows in enumerate((d, e)):
            block = jnp.concatenate(rows, axis=0)
            cols[i] += [block, pltpu.roll(block, 64, 1)]
    own_nbr[...] = nbr[pl.ds(pl.multiple_of(64 * info[0] + 32 * info[1], 32), 32), :]
    at = pl.multiple_of(jnp.where(info[0] < 2, 32, 0), 32)
    for i in range(2):
        out[i] = jnp.concatenate(cols[i], axis=0).T[:groups]
        near[i] = out[i, pl.ds(at, 32), :]


def pair_dot(left, right):
    zero = jnp.zeros((128, 128), BF16)
    top = jnp.concatenate([right[:, :128], zero], axis=1)
    low = jnp.concatenate([zero, right[:, 128:]], axis=1)
    both = jnp.concatenate([top, low], axis=0)
    return jnp.dot(left, both, preferred_element_type=F32)


def each(f, *lists):
    return [f(*a) for a in zip(*lists)]


def narrow(a):
    return a.astype(BF16)


def solve_kernel(info, nbr, *refs):
    parts, (de, dn, out, gt, lt, ks) = refs[:8], refs[8:]
    z, k, first, total = info[0], info[1], info[2], info[3]
    reach = 128
    start = 16 * z - 32 + 8 * k
    low = z < 2
    n_end = jnp.where(low, -start, start + 8)
    end_at = jnp.where(low, 32 + start, 0)
    end_to = jnp.where(low, 0, 64 - start)
    own_at = jnp.where(low, 0, start)
    own_to = jnp.where(low, -start, 0)
    mine = lax.broadcasted_iota(jnp.int32, (8, 128), 0) == (lane_id(8) >> 5)

    def center(table, b, g):
        x = jnp.concatenate([r[8 * k + g] for r in parts], axis=0).astype(F32)
        mean = jnp.sum(x, axis=0, keepdims=True) * (1.0 / 128.0)
        d = table[0, pl.ds(b, 1), :]
        e = table[1, pl.ds(b, 1), :] - d * mean
        a = x - mean
        turned = a.astype(BF16).T
        gt[g] = turned
        lt[g] = (a * d).astype(BF16).T
        ks[pl.ds(8 * g, 8), :] = jnp.dot(
            jnp.where(mine, e, 0.0).astype(BF16), turned, preferred_element_type=F32
        )

    def own_eight(j, carry):
        for i in range(8):
            center(de, own_at + 8 * j + i, own_to + 8 * j + i)
        return carry

    def end_eight(j, carry):
        for i in range(8):
            center(dn, end_at + 8 * j + i, end_to + 8 * j + i)
        return carry

    lax.fori_loop(0, (gt.shape[0] - n_end) // 8, own_eight, 0)
    lax.fori_loop(0, n_end // 8, end_eight, 0)
    eye = lax.broadcasted_iota(jnp.int32, (128, 128), 0) == lane_id(128)

    def gather(t):
        lhs, rhs, cross = [], [], None
        for n in range(5):
            if n == 0:
                loc, tap = t + reach, None
            else:
                gap = nbr[t, n - 1] - (first + t)
                gap = jnp.where(gap < 0, gap + total, gap)
                gap = jnp.where(gap > total // 2, gap - total, gap)
                loc = t + reach + gap
                tap = 1.0 - jnp.abs(gap).astype(F32) * (1.0 / (reach + 1.0))
            g = loc // PACK
            at = pl.multiple_of(32 * (loc % PACK), 32)
            rhs.append(gt[g, pl.ds(at, 32), :])
            v = lt[g, pl.ds(at, 32), :]
            c = ks[pl.ds(8 * g + loc % PACK, 1), :]
            lhs.append(v if tap is None else (v.astype(F32) * tap).astype(BF16))
            cross = c if n == 0 else cross + tap * c
        cat = lambda v: jnp.concatenate(v, axis=0)
        dims = (((0,), (0,)), ((), ()))
        gram = lax.dot_general(cat(lhs), cat(rhs), dims, preferred_element_type=F32)
        return gram, cross

    def prepare(t):
        gram, cross = gather(t)
        total_sq = lambda a: jnp.sum(jnp.sum(a, axis=0, keepdims=True), axis=1, keepdims=True)
        diag = jnp.where(eye, gram, 0.0)
        system = gram + jnp.where(eye, 127.0, 0.0)
        inv = lax.rsqrt(total_sq(system * system))
        mid = 127.0 + total_sq(diag) * (1.0 / 128.0)
        rest = (system - jnp.where(eye, mid, 0.0)) * inv
        wide = lambda v: jnp.broadcast_to(v, (1, 128))
        return rest, wide(mid * inv), wide(inv), cross

    unit = jnp.where(eye, 1.0, 0.0)
    unit = narrow(jnp.concatenate([unit, unit], axis=1))

    def tiles(b, carry):
        ts = [b * UNROLL + u for u in range(UNROLL)]
        ready = [prepare(t) for t in ts]
        pairs = range(UNROLL // 2)
        wide = lambda j: [
            jnp.concatenate([ready[2 * p][j], ready[2 * p + 1][j]], axis=1) for p in pairs
        ]
        v, al = wide(0), wide(1)
        root = rho = None
        for step in range(3):
            vs = each(narrow, v)
            sq = each(pair_dot, vs, vs)
            be = each(lambda a: a * (0.0625 * a - 0.5625), al)
            cx = each(lambda a, c: 1.6875 + c + 0.0625 * a * a, al, be)
            c1 = each(lambda a, c: 2.0 * a * c - 2.4375 - 0.5625 * a * a, al, cx)
            ga = each(lambda a, c: 2.25 + a * (1.6875 * a - 2.4375) + a * a * c, al, be)
            xs, ys, lin = [], [], []
            for m, p, a, i, j in zip(v, sq, al, c1, cx):
                n = narrow(m)
                x = narrow(2.0 * a) * n + narrow(p)
                xs.append(x)
                ys.append(0.0625 * x - 0.5625 * n)
                lin.append(i * m + j * p)
            high = each(pair_dot, xs, ys)
            q = each(lambda m, h: m + h, lin, high)
            qs = each(narrow, q)

            def times(m, a):
                prod = each(lambda i, c, r: pair_dot(narrow(i) + unit * narrow(c), r), m, a, qs)
                rest = each(lambda g, j, d: g * j + d, ga, m, prod)
                return rest, each(lambda i, g: i * g, a, ga)

            root, rho = (q, ga) if root is None else times(root, rho)
            if step < 2:
                v, al = times(*times(v, al))
        for u, t in enumerate(ts):
            _, _, inv, cross = ready[u]
            at = 128 * (u % 2)
            r = root[u // 2][:, at : at + 128]
            r = r + jnp.where(eye, rho[u // 2][:, at : at + 128], 0.0)
            col = jnp.sum(r * cross, axis=1, keepdims=True)
            row = jnp.sum(r * col, axis=0, keepdims=True) * inv
            out[t] = (r * jnp.sqrt(127.0 * inv) + row).astype(BF16)
        return carry

    lax.fori_loop(0, out.shape[0] // UNROLL, tiles, 0)


def update_kernel(info, tr, *refs):
    parts, outs = refs[:8], refs[8:]

    def tile(t, carry):
        x = jnp.concatenate([r[t] for r in parts], axis=0).astype(F32)
        mean = jnp.sum(x, axis=0, keepdims=True) * (1.0 / 128.0)
        anomaly = (x - mean).astype(BF16)
        new = jnp.dot(tr[t], anomaly, preferred_element_type=F32) + mean
        new = new.astype(BF16)
        for i, o in enumerate(outs):
            o[t] = new[16 * i : 16 * i + 16]
        return carry

    lax.fori_loop(0, tr.shape[0], tile, 0, unroll=8)


def place_kernel(info, *refs):
    pieces, out, buf = refs[:8], refs[8], refs[9]
    z, k = info[0], info[1]
    for i, piece in enumerate(pieces):
        d, o = i % 4, i // 4
        zz = (z + d) % 4
        kk = k if o == 0 else 1 - k
        at = pl.multiple_of(64 * zz + 32 * kk, 32)
        for t in range(32):
            buf[i % 2, pl.ds(t, 16, stride=33), :] = piece[t].astype(F32)
        for m in range(16):
            out[m, pl.ds(at, 32), :] = buf[i % 2, 33 * m : 33 * m + 32, :].astype(BF16)


def vmem():
    return pl.BlockSpec(memory_space=pltpu.VMEM)


def smem():
    return pl.BlockSpec(memory_space=pltpu.SMEM)


def call(kernel, n_smem, args, outs, scratch=(), mib=12):
    return pl.pallas_call(
        kernel,
        in_specs=[smem()] * n_smem + [vmem()] * (len(args) - n_smem),
        out_specs=jax.tree.map(lambda _: vmem(), outs),
        out_shape=outs,
        scratch_shapes=list(scratch),
        compiler_params=pltpu.CompilerParams(vmem_limit_bytes=mib * 1024 * 1024),
    )(*args)


def to_z(x, by):
    return lax.ppermute(x, "z", [(i, (i + by) % 4) for i in range(4)])


def to_core(x):
    return lax.ppermute(x, "k", [(0, 1), (1, 0)])


def to_cells(x, by):
    n = lax.axis_size("cells")
    return lax.ppermute(x, "cells", [(i, (i + by) % n) for i in range(n)])


def to_side(x, d):
    n = lax.axis_size("cells")
    pairs = []
    for c in range(n):
        for z in range(4):
            zz = (z + d) % 4
            cc = (c + 1) % n if zz < 2 else (c - 1) % n
            pairs += [(8 * c + 2 * z + k, 8 * cc + 2 * zz + k) for k in range(2)]
    return lax.ppermute(x, ("cells", "z", "k"), pairs)


def away(x, d, o):
    pairs = [(2 * z + k, 2 * ((z + d) % 4) + (k ^ o)) for z in range(4) for k in range(2)]
    return lax.ppermute(x, MEM, pairs)


def home(x, d, o):
    pairs = [(2 * z + k, 2 * ((z - d) % 4) + (k ^ o)) for z in range(4) for k in range(2)]
    return lax.ppermute(x, MEM, pairs)


def analysis(bg, figures, spread, pixel, active, nbr):
    members, tiles, width = bg.shape
    groups = tiles // PACK
    z, k = lax.axis_index("z"), lax.axis_index("k")
    first = lax.axis_index("cells") * tiles + 64 * z + 32 * k
    info = jnp.stack([z, k, first, tiles * lax.axis_size("cells")]).astype(jnp.int32)
    half = groups // 2
    shape = lambda n: jax.ShapeDtypeStruct((n, members, width), BF16)
    sg, *rest = call(
        sense_kernel,
        1,
        (info, bg),
        (shape(groups),) + (shape(tiles // 8),) * 8,
        [pltpu.VMEM((members * (tiles + 1) + 7, width), F32)],
    )
    left = to_cells(sg[half:], 1)
    right = to_cells(sg[:half], -1)
    windows = call(window_kernel, 1, (info, sg, left, right), (shape(80),) * 4)
    own = [windows[0]] + [to_z(windows[d], d) for d in (1, 2, 3)]
    state = [rest[i] if i == 0 else away(rest[i], i % 4, i // 4) for i in range(8)]
    live = jnp.arange(128, dtype=jnp.int32)[None, :] < active[:, None]
    w2 = jnp.where(live, 1.0 / spread, 0.0)
    de, near, own_nbr = call(
        cell_kernel,
        1,
        (info, pixel, w2, figures, nbr),
        (
            jax.ShapeDtypeStruct((2, groups, 128), F32),
            jax.ShapeDtypeStruct((2, half, 128), F32),
            jax.ShapeDtypeStruct((32, 4), jnp.int32),
        ),
    )
    dn = to_side(near, 0)
    own += [to_core(r) for r in own]
    transform = call(
        solve_kernel,
        2,
        (info, own_nbr, *own, de, dn),
        jax.ShapeDtypeStruct((32, 128, 128), BF16),
        [
            pltpu.VMEM((72, 128, 128), BF16),
            pltpu.VMEM((72, 128, 128), BF16),
            pltpu.VMEM((8 * 72, 128), F32),
        ],
        40,
    )
    outs = call(update_kernel, 1, (info, transform, *state), (shape(32),) * 8)
    back = [
        outs[i] if i == 0 else home(outs[i], i % 4, i // 4) for i in range(8)
    ]
    return call(
        place_kernel,
        1,
        (info, *back),
        jax.ShapeDtypeStruct((members, tiles, width), BF16),
        [pltpu.VMEM((2, 16 * 33, 128), F32)],
    )


def solution(mesh):
    finer = Mesh(mesh.devices.reshape(mesh.shape["cells"], 4, 2), ("cells", "z", "k"))
    placed = (
        P(MEM, "cells", None),
        P("cells", None),
        P("cells", None),
        P("cells", None),
        P("cells"),
        P("cells", None),
    )
    return jax.shard_map(
        analysis, mesh=finer, in_specs=placed, out_specs=P(MEM, "cells", None), check_vma=False
    )
```

profile of v0, /device:TPU:1, one launch (start us, length us, event | category | flops | bytes accessed | tf_op | source)
XLA Modules:
  0.0 99.6 jit_solution(1404678198264271613)
XLA Ops:
  0.1 1.2 %copy-done = bf16[16,256,128]{2,1,0:T(8,128)(2,1)S(1)} copy-done((bf16[16,256,128]{2,1,0:T(8,128)(2,1)S(1)}, bf16[16,256,128]{2,1,0:T(8,128)(2,1)}, u32[]{:S(2)}) %copy-start) | copy-done | bytes 1048600
  1.3 3.3 %shard_map.65 = (bf16[64,16,128]{2,1,0:T(8,128)(2,1)S(1)}, bf16[32,16,128]{2,1,0:T(8,128)(2,1)S(1)}, bf16[32,16,128]{2,1,0:T(8,128)(2,1)S(1)}, bf16[32,16,128]{2...) custom-call(s32[4]{0:T(128)S(1)} %pad_add_fusion.info, ...), custom_call_target="tpu_custom_call" | custom-call | tf_op jit(solution)/shard_map/pallas_call | solution.py:292
  6.1 5.7 %collective-permute-start.1 = (bf16[32,16,128]{2,1,0:T(8,128)(2,1)S(1)}, bf16[32,16,128]{2,1,0:T(8,128)(2,1)S(1)}, u32[]{:S(2)}, u32[]{:S(2)}) collective-permute-start(bf16[32,16,128]{2,1,0:T(8,128)(2,1)S(1)} %get-tuple-element.53), channel_id=1, source_target_pairs={{0,120},{8,0},{16,8},{24,16},{32,24},{40,32},{48,40},{56,48},{64,5... | collective-permute-start | bytes 393224 | tf_op jit(solution)/shard_map/ppermute | solution.py:312
  11.8 2.2 %collective-permute-done.1.right = bf16[32,16,128]{2,1,0:T(8,128)(2,1)S(1)} collective-permute-done((bf16[32,16,128]{2,1,0:T(8,128)(2,1)S(1)}, bf16[32,16,128]{2,1,0:T(8,128)(2,1)S(1)}, u32[]{:S(2)}, u32[]{:S(2)}) %collective-permute-start.1) | collective-permute-done | bytes 131104 | tf_op jit(solution)/shard_map/ppermute | solution.py:312
  14.0 5.0 %collective-permute-done.left = bf16[32,16,128]{2,1,0:T(8,128)(2,1)S(1)} collective-permute-done((bf16[32,16,128]{2,1,0:T(8,128)(2,1)S(1)}, bf16[32,16,128]{2,1,0:T(8,128)(2,1)S(1)}, u32[]{:S(2)}, u32[]{:S(2)}) %collective-permute-start) | collective-permute-done | bytes 131104 | tf_op jit(solution)/shard_map/ppermute | solution.py:312
  19.0 0.9 shard_map.66
  19.8 1.7 %collective-permute-start.2 = (bf16[80,16,128]{2,1,0:T(8,128)(2,1)S(1)}, bf16[80,16,128]{2,1,0:T(8,128)(2,1)S(1)}, u32[]{:S(2)}, u32[]{:S(2)}) collective-permute-start(bf16[80,16,128]{2,1,0:T(8,128)(2,1)S(1)} %get-tuple-element.32), channel_id=1, source_target_pairs={{0,2},{2,4},{4,6},{6,0},{1,3},{3,5},{5,7},{7,1},{8,10},{10,12},{12... | collective-permute-start | bytes 983048 | tf_op jit(solution)/shard_map/ppermute | solution.py:303
  21.5 3.3 %collective-permute-start.3 = (bf16[80,16,128]{2,1,0:T(8,128)(2,1)S(1)}, bf16[80,16,128]{2,1,0:T(8,128)(2,1)S(1)}, u32[]{:S(2)}, u32[]{:S(2)}) collective-permute-start(bf16[80,16,128]{2,1,0:T(8,128)(2,1)S(1)} %get-tuple-element.33), channel_id=1, source_target_pairs={{0,4},{2,6},{4,0},{6,2},{1,5},{3,7},{5,1},{7,3},{8,12},{10,14},{12... | collective-permute-start | bytes 983048 | tf_op jit(solution)/shard_map/ppermute | solution.py:303
  25.6 2.9 %collective-permute-start.5 = (bf16[80,16,128]{2,1,0:T(8,128)(2,1)S(1)}, bf16[80,16,128]{2,1,0:T(8,128)(2,1)S(1)}, u32[]{:S(2)}, u32[]{:S(2)}) collective-permute-start(bf16[80,16,128]{2,1,0:T(8,128)(2,1)S(1)} %get-tuple-element.31.refs_0_), channel_id=1, source_target_pairs={{0,1},{1,0},{2,3},{3,2},{4,5},{5,4},{6,7},{7,6},{8,9},{9,8},{10,11... | collective-permute-start | bytes 983048 | tf_op jit(solution)/shard_map/ppermute | solution.py:307
  28.5 1.1 %collective-permute-done.2.refs_1_ = bf16[80,16,128]{2,1,0:T(8,128)(2,1)S(1)} collective-permute-done((bf16[80,16,128]{2,1,0:T(8,128)(2,1)S(1)}, bf16[80,16,128]{2,1,0:T(8,128)(2,1)S(1)}, u32[]{:S(2)}, u32[]{:S(2)}) %collective-permute-start.2) | collective-permute-done | bytes 327712 | tf_op jit(solution)/shard_map/ppermute | solution.py:303
  29.6 4.1 %collective-permute-start.6 = (bf16[80,16,128]{2,1,0:T(8,128)(2,1)S(1)}, bf16[80,16,128]{2,1,0:T(8,128)(2,1)S(1)}, u32[]{:S(2)}, u32[]{:S(2)}) collective-permute-start(bf16[80,16,128]{2,1,0:T(8,128)(2,1)S(1)} %collective-permute-done.2.refs_1_), channel_id=1, source_target_pairs={{0,1},{1,0},{2,3},{3,2},{4,5},{5,4},{6,7},{7,6},{8,9},{9,8},{10,11... | collective-permute-start | bytes 983048 | tf_op jit(solution)/shard_map/ppermute | solution.py:307
  33.7 3.9 %collective-permute-done.3.refs_2_ = bf16[80,16,128]{2,1,0:T(8,128)(2,1)S(1)} collective-permute-done((bf16[80,16,128]{2,1,0:T(8,128)(2,1)S(1)}, bf16[80,16,128]{2,1,0:T(8,128)(2,1)S(1)}, u32[]{:S(2)}, u32[]{:S(2)}) %collective-permute-start.3) | collective-permute-done | bytes 327712 | tf_op jit(solution)/shard_map/ppermute | solution.py:303
  37.6 3.0 %collective-permute-start.7 = (bf16[80,16,128]{2,1,0:T(8,128)(2,1)S(1)}, bf16[80,16,128]{2,1,0:T(8,128)(2,1)S(1)}, u32[]{:S(2)}, u32[]{:S(2)}) collective-permute-start(bf16[80,16,128]{2,1,0:T(8,128)(2,1)S(1)} %collective-permute-done.3.refs_2_), channel_id=1, source_target_pairs={{0,1},{1,0},{2,3},{3,2},{4,5},{5,4},{6,7},{7,6},{8,9},{9,8},{10,11... | collective-permute-start | bytes 983048 | tf_op jit(solution)/shard_map/ppermute | solution.py:307
  41.6 1.7 %shard_map.64 = (f32[2,64,128]{2,1,0:T(8,128)S(1)}, f32[2,32,128]{2,1,0:T(8,128)S(1)}, s32[32,4]{1,0:T(8,128)S(1)}) custom-call(s32[4]{0:T(128)S(1)} %pad_add_fusion.info, s32[256,128]{1,0:T(8,128)S(1)} %copy-done.1, f32[256,128]{1,0:T(8,128)S(1)} %divide_select_fusion.w2, f32[256,128]{1,0:T(8,128)S(1)} %copy-done.2, s32[256,4]{1,0:T(8,128)S(1)} %copy.7.nbr), custom_call_target="tpu_custom_call" | custom-call | tf_op jit(solution)/shard_map/pallas_call | solution.py:292
  43.4 6.1 %collective-permute-done.9.refs_9_ = f32[2,32,128]{2,1,0:T(8,128)S(1)} collective-permute-done((f32[2,32,128]{2,1,0:T(8,128)S(1)}, f32[2,32,128]{2,1,0:T(8,128)S(1)}, u32[]{:S(2)}, u32[]{:S(2)}) %collective-permute-start.9) | collective-permute-done | bytes 32800 | tf_op jit(solution)/shard_map/ppermute | solution.py:323
  49.4 0.9 collective-permute-start.10
  50.4 4.3 %collective-permute-done.10.refs_1_ = bf16[32,16,128]{2,1,0:T(8,128)(2,1)S(1)} collective-permute-done((bf16[32,16,128]{2,1,0:T(8,128)(2,1)}, bf16[32,16,128]{2,1,0:T(8,128)(2,1)S(1)}, u32[]{:S(2)}, u32[]{:S(2)}) %collective-permute-start.10) | collective-permute-done | bytes 131104 | tf_op jit(solution)/shard_map/ppermute | solution.py:328
  55.1 4.9 %collective-permute-done.11.refs_2_ = bf16[32,16,128]{2,1,0:T(8,128)(2,1)S(1)} collective-permute-done((bf16[32,16,128]{2,1,0:T(8,128)(2,1)S(1)}, bf16[32,16,128]{2,1,0:T(8,128)(2,1)S(1)}, u32[]{:S(2)}, u32[]{:S(2)}) %collective-permute-start.11) | collective-permute-done | bytes 131104 | tf_op jit(solution)/shard_map/ppermute | solution.py:328
  60.0 4.0 %collective-permute-start.13 = (bf16[32,16,128]{2,1,0:T(8,128)(2,1)S(1)}, bf16[32,16,128]{2,1,0:T(8,128)(2,1)S(1)}, u32[]{:S(2)}, u32[]{:S(2)}) collective-permute-start(bf16[32,16,128]{2,1,0:T(8,128)(2,1)S(1)} %copy-done.6), channel_id=1, source_target_pairs={{0,1},{1,0},{2,3},{3,2},{4,5},{5,4},{6,7},{7,6},{8,9},{9,8},{10,11... | collective-permute-start | bytes 393224 | tf_op jit(solution)/shard_map/ppermute | solution.py:328
  64.0 1.6 %collective-permute-start.14 = (bf16[32,16,128]{2,1,0:T(8,128)(2,1)S(1)}, bf16[32,16,128]{2,1,0:T(8,128)(2,1)S(1)}, u32[]{:S(2)}, u32[]{:S(2)}) collective-permute-start(bf16[32,16,128]{2,1,0:T(8,128)(2,1)S(1)} %copy-done.4), channel_id=1, source_target_pairs={{0,3},{1,2},{2,5},{3,4},{4,7},{5,6},{6,1},{7,0},{8,11},{9,10},{10,... | collective-permute-start | bytes 393224 | tf_op jit(solution)/shard_map/ppermute | solution.py:328
  65.7 2.8 %collective-permute-start.16 = (bf16[32,16,128]{2,1,0:T(8,128)(2,1)S(1)}, bf16[32,16,128]{2,1,0:T(8,128)(2,1)S(1)}, u32[]{:S(2)}, u32[]{:S(2)}) collective-permute-start(bf16[32,16,128]{2,1,0:T(8,128)(2,1)S(1)} %get-tuple-element.44), channel_id=1, source_target_pairs={{0,7},{1,6},{2,1},{3,0},{4,3},{5,2},{6,5},{7,4},{8,15},{9,14},{10,... | collective-permute-start | bytes 393224 | tf_op jit(solution)/shard_map/ppermute | solution.py:328
  68.5 11.4 %shard_map.67.tr = bf16[32,128,128]{2,1,0:T(8,128)(2,1)S(1)} custom-call(s32[4]{0:T(128)S(1)} %pad_add_fusion.info, s32[32,4]{1,0:T(8,128)S(1)} %get-tuple-element.29.nbr, bf16[80,16,128]{2,1,0:T(8,128)(2,1)S(1)} %get-tuple-element.31.refs_0_, bf16[80,16,128]{2,1,0:T(8,128)(2,1)S(1)} %collective-permute-done.2.refs_1_, ...), custom_call_target="tpu_custom_call" | custom-call | tf_op jit(solution)/shard_map/pallas_call | solution.py:292
  79.9 1.6 %shard_map.68 = (bf16[32,16,128]{2,1,0:T(8,128)(2,1)S(1)}, bf16[32,16,128]{2,1,0:T(8,128)(2,1)S(1)}, bf16[32,16,128]{2,1,0:T(8,128)(2,1)S(1)}, bf16[32,16,128]{2...) custom-call(s32[4]{0:T(128)S(1)} %pad_add_fusion.info, ...), custom_call_target="tpu_custom_call" | custom-call | tf_op jit(solution)/shard_map/pallas_call | solution.py:292
  83.4 1.2 %collective-permute-start.20 = (bf16[32,16,128]{2,1,0:T(8,128)(2,1)S(1)}, bf16[32,16,128]{2,1,0:T(8,128)(2,1)S(1)}, u32[]{:S(2)}, u32[]{:S(2)}) collective-permute-start(bf16[32,16,128]{2,1,0:T(8,128)(2,1)S(1)} %get-tuple-element.49), channel_id=1, source_target_pairs={{0,1},{1,0},{2,3},{3,2},{4,5},{5,4},{6,7},{7,6},{8,9},{9,8},{10,11... | collective-permute-start | bytes 393224 | tf_op jit(solution)/shard_map/ppermute | solution.py:333
  84.6 1.5 %collective-permute-start.21 = (bf16[32,16,128]{2,1,0:T(8,128)(2,1)S(1)}, bf16[32,16,128]{2,1,0:T(8,128)(2,1)S(1)}, u32[]{:S(2)}, u32[]{:S(2)}) collective-permute-start(bf16[32,16,128]{2,1,0:T(8,128)(2,1)S(1)} %get-tuple-element.50), channel_id=1, source_target_pairs={{0,7},{1,6},{2,1},{3,0},{4,3},{5,2},{6,5},{7,4},{8,15},{9,14},{10,... | collective-permute-start | bytes 393224 | tf_op jit(solution)/shard_map/ppermute | solution.py:333
  86.6 1.8 %collective-permute-start.22 = (bf16[32,16,128]{2,1,0:T(8,128)(2,1)S(1)}, bf16[32,16,128]{2,1,0:T(8,128)(2,1)S(1)}, u32[]{:S(2)}, u32[]{:S(2)}) collective-permute-start(bf16[32,16,128]{2,1,0:T(8,128)(2,1)S(1)} %get-tuple-element.51), channel_id=1, source_target_pairs={{0,5},{1,4},{2,7},{3,6},{4,1},{5,0},{6,3},{7,2},{8,13},{9,12},{10,... | collective-permute-start | bytes 393224 | tf_op jit(solution)/shard_map/ppermute | solution.py:333
  88.4 2.7 %collective-permute-start.23 = (bf16[32,16,128]{2,1,0:T(8,128)(2,1)S(1)}, bf16[32,16,128]{2,1,0:T(8,128)(2,1)S(1)}, u32[]{:S(2)}, u32[]{:S(2)}) collective-permute-start(bf16[32,16,128]{2,1,0:T(8,128)(2,1)S(1)} %get-tuple-element.52), channel_id=1, source_target_pairs={{0,3},{1,2},{2,5},{3,4},{4,7},{5,6},{6,1},{7,0},{8,11},{9,10},{10,... | collective-permute-start | bytes 393224 | tf_op jit(solution)/shard_map/ppermute | solution.py:333
  91.1 1.0 collective-permute-done.19.refs_3_
  92.1 1.2 %collective-permute-done.21.refs_5_ = bf16[32,16,128]{2,1,0:T(8,128)(2,1)S(1)} collective-permute-done((bf16[32,16,128]{2,1,0:T(8,128)(2,1)S(1)}, bf16[32,16,128]{2,1,0:T(8,128)(2,1)S(1)}, u32[]{:S(2)}, u32[]{:S(2)}) %collective-permute-start.21) | collective-permute-done | bytes 131104 | tf_op jit(solution)/shard_map/ppermute | solution.py:333
  93.3 1.6 %collective-permute-done.22.refs_6_ = bf16[32,16,128]{2,1,0:T(8,128)(2,1)S(1)} collective-permute-done((bf16[32,16,128]{2,1,0:T(8,128)(2,1)S(1)}, bf16[32,16,128]{2,1,0:T(8,128)(2,1)S(1)}, u32[]{:S(2)}, u32[]{:S(2)}) %collective-permute-start.22) | collective-permute-done | bytes 131104 | tf_op jit(solution)/shard_map/ppermute | solution.py:333
  95.0 2.8 %collective-permute-done.23.refs_7_ = bf16[32,16,128]{2,1,0:T(8,128)(2,1)S(1)} collective-permute-done((bf16[32,16,128]{2,1,0:T(8,128)(2,1)S(1)}, bf16[32,16,128]{2,1,0:T(8,128)(2,1)S(1)}, u32[]{:S(2)}, u32[]{:S(2)}) %collective-permute-start.23) | collective-permute-done | bytes 131104 | tf_op jit(solution)/shard_map/ppermute | solution.py:333
  97.8 1.8 %shard_map.69 = bf16[16,256,128]{2,1,0:T(8,128)(2,1)} custom-call(s32[4]{0:T(128)S(1)} %pad_add_fusion.info, bf16[32,16,128]{2,1,0:T(8,128)(2,1)S(1)} %get-tuple-element.45.refs_0_, bf16[32,16,128]{2,1,0:T(8,128)(2,1)S(1)} %collective-permute-done.17.refs_1_, bf16[32,16,128]{2,1,0:T(8,128)(2,1)S(1)} %collective-permute-done.18.refs_2_, ...), custom_call_target="tpu_custom_call" | custom-call | tf_op jit(solution)/shard_map/pallas_call | solution.py:292
  (56 shorter events, 6.1 us)
Async XLA Ops:
  0.1 1.2 %copy-start = (bf16[16,256,128]{2,1,0:T(8,128)(2,1)S(1)}, bf16[16,256,128]{2,1,0:T(8,128)(2,1)}, u32[]{:S(2)}) copy-start(bf16[16,256,128]{2,1,0:T(8,128)(2,1)} %bg.1) | copy-start | bytes 3145732
  6.1 7.9 %collective-permute-start.1 = (bf16[32,16,128]{2,1,0:T(8,128)(2,1)S(1)}, bf16[32,16,128]{2,1,0:T(8,128)(2,1)S(1)}, u32[]{:S(2)}, u32[]{:S(2)}) collective-permute-start(bf16[32,16,128]{2,1,0:T(8,128)(2,1)S(1)} %get-tuple-element.53), channel_id=1, source_target_pairs={{0,120},{8,0},{16,8},{24,16},{32,24},{40,32},{48,40},{56,48},{64,5... | collective-permute-start | bytes 393224 | tf_op jit(solution)/shard_map/ppermute | solution.py:312
  11.8 28.7 %copy-start.12 = (f32[256,128]{1,0:T(8,128)S(1)}, f32[256,128]{1,0:T(8,128)}, u32[]{:S(2)}) copy-start(f32[256,128]{1,0:T(8,128)} %param.8) | copy-start | bytes 393220
  11.8 7.1 %collective-permute-start = (bf16[32,16,128]{2,1,0:T(8,128)(2,1)S(1)}, bf16[32,16,128]{2,1,0:T(8,128)(2,1)S(1)}, u32[]{:S(2)}, u32[]{:S(2)}) collective-permute-start(bf16[32,16,128]{2,1,0:T(8,128)(2,1)S(1)} %get-tuple-element.54), channel_id=1, source_target_pairs={{0,8},{8,16},{16,24},{24,32},{32,40},{40,48},{48,56},{56,64},{64,7... | collective-permute-start | bytes 393224 | tf_op jit(solution)/shard_map/ppermute | solution.py:312
  19.8 9.8 %collective-permute-start.2 = (bf16[80,16,128]{2,1,0:T(8,128)(2,1)S(1)}, bf16[80,16,128]{2,1,0:T(8,128)(2,1)S(1)}, u32[]{:S(2)}, u32[]{:S(2)}) collective-permute-start(bf16[80,16,128]{2,1,0:T(8,128)(2,1)S(1)} %get-tuple-element.32), channel_id=1, source_target_pairs={{0,2},{2,4},{4,6},{6,0},{1,3},{3,5},{5,7},{7,1},{8,10},{10,12},{12... | collective-permute-start | bytes 983048 | tf_op jit(solution)/shard_map/ppermute | solution.py:303
  21.5 16.0 %collective-permute-start.3 = (bf16[80,16,128]{2,1,0:T(8,128)(2,1)S(1)}, bf16[80,16,128]{2,1,0:T(8,128)(2,1)S(1)}, u32[]{:S(2)}, u32[]{:S(2)}) collective-permute-start(bf16[80,16,128]{2,1,0:T(8,128)(2,1)S(1)} %get-tuple-element.33), channel_id=1, source_target_pairs={{0,4},{2,6},{4,0},{6,2},{1,5},{3,7},{5,1},{7,3},{8,12},{10,14},{12... | collective-permute-start | bytes 983048 | tf_op jit(solution)/shard_map/ppermute | solution.py:303
  24.8 15.7 %copy-start.14 = (s32[256]{0:T(256)S(1)}, s32[256]{0:T(256)}, u32[]{:S(2)}) copy-start(s32[256]{0:T(256)} %param.10) | copy-start | bytes 3076
  24.8 15.7 %collective-permute-start.4 = (bf16[80,16,128]{2,1,0:T(8,128)(2,1)S(1)}, bf16[80,16,128]{2,1,0:T(8,128)(2,1)S(1)}, u32[]{:S(2)}, u32[]{:S(2)}) collective-permute-start(bf16[80,16,128]{2,1,0:T(8,128)(2,1)S(1)} %get-tuple-element.34), channel_id=1, source_target_pairs={{0,6},{2,0},{4,2},{6,4},{1,7},{3,1},{5,3},{7,5},{8,14},{10,8},{12,... | collective-permute-start | bytes 983048 | tf_op jit(solution)/shard_map/ppermute | solution.py:303
  25.6 15.1 %copy-start.13 = (s32[256,4]{0,1:T(4,128)S(1)}, s32[256,4]{0,1:T(4,128)}, u32[]{:S(2)}) copy-start(s32[256,4]{0,1:T(4,128)} %param.11) | copy-start | bytes 12292
  25.6 34.4 %collective-permute-start.5 = (bf16[80,16,128]{2,1,0:T(8,128)(2,1)S(1)}, bf16[80,16,128]{2,1,0:T(8,128)(2,1)S(1)}, u32[]{:S(2)}, u32[]{:S(2)}) collective-permute-start(bf16[80,16,128]{2,1,0:T(8,128)(2,1)S(1)} %get-tuple-element.31.refs_0_), channel_id=1, source_target_pairs={{0,1},{1,0},{2,3},{3,2},{4,5},{5,4},{6,7},{7,6},{8,9},{9,8},{10,11... | collective-permute-start | bytes 983048 | tf_op jit(solution)/shard_map/ppermute | solution.py:307
  29.6 34.4 %collective-permute-start.6 = (bf16[80,16,128]{2,1,0:T(8,128)(2,1)S(1)}, bf16[80,16,128]{2,1,0:T(8,128)(2,1)S(1)}, u32[]{:S(2)}, u32[]{:S(2)}) collective-permute-start(bf16[80,16,128]{2,1,0:T(8,128)(2,1)S(1)} %collective-permute-done.2.refs_1_), channel_id=1, source_target_pairs={{0,1},{1,0},{2,3},{3,2},{4,5},{5,4},{6,7},{7,6},{8,9},{9,8},{10,11... | collective-permute-start | bytes 983048 | tf_op jit(solution)/shard_map/ppermute | solution.py:307
  37.6 28.1 %collective-permute-start.7 = (bf16[80,16,128]{2,1,0:T(8,128)(2,1)S(1)}, bf16[80,16,128]{2,1,0:T(8,128)(2,1)S(1)}, u32[]{:S(2)}, u32[]{:S(2)}) collective-permute-start(bf16[80,16,128]{2,1,0:T(8,128)(2,1)S(1)} %collective-permute-done.3.refs_2_), channel_id=1, source_target_pairs={{0,1},{1,0},{2,3},{3,2},{4,5},{5,4},{6,7},{7,6},{8,9},{9,8},{10,11... | collective-permute-start | bytes 983048 | tf_op jit(solution)/shard_map/ppermute | solution.py:307
  40.5 25.2 %collective-permute-start.8 = (bf16[80,16,128]{2,1,0:T(8,128)(2,1)S(1)}, bf16[80,16,128]{2,1,0:T(8,128)(2,1)S(1)}, u32[]{:S(2)}, u32[]{:S(2)}) collective-permute-start(bf16[80,16,128]{2,1,0:T(8,128)(2,1)S(1)} %collective-permute-done.4.refs_3_), channel_id=1, source_target_pairs={{0,1},{1,0},{2,3},{3,2},{4,5},{5,4},{6,7},{7,6},{8,9},{9,8},{10,11... | collective-permute-start | bytes 983048 | tf_op jit(solution)/shard_map/ppermute | solution.py:307
  41.6 13.1 %copy-start.10 = (bf16[32,16,128]{2,1,0:T(8,128)(2,1)S(1)}, bf16[32,16,128]{2,1,0:T(8,128)(2,1)}, u32[]{:S(2)}) copy-start(bf16[32,16,128]{2,1,0:T(8,128)(2,1)} %copy-done.9) | copy-start | bytes 393220
  41.6 18.4 %copy-start.8 = (bf16[32,16,128]{2,1,0:T(8,128)(2,1)S(1)}, bf16[32,16,128]{2,1,0:T(8,128)(2,1)}, u32[]{:S(2)}) copy-start(bf16[32,16,128]{2,1,0:T(8,128)(2,1)} %copy-done.7) | copy-start | bytes 393220
  41.6 18.4 %copy-start.6 = (bf16[32,16,128]{2,1,0:T(8,128)(2,1)S(1)}, bf16[32,16,128]{2,1,0:T(8,128)(2,1)}, u32[]{:S(2)}) copy-start(bf16[32,16,128]{2,1,0:T(8,128)(2,1)} %copy-done.5) | copy-start | bytes 393220
  41.6 22.4 %copy-start.4 = (bf16[32,16,128]{2,1,0:T(8,128)(2,1)S(1)}, bf16[32,16,128]{2,1,0:T(8,128)(2,1)}, u32[]{:S(2)}) copy-start(bf16[32,16,128]{2,1,0:T(8,128)(2,1)} %copy-done.3) | copy-start | bytes 393220
  43.3 6.2 %collective-permute-start.9 = (f32[2,32,128]{2,1,0:T(8,128)S(1)}, f32[2,32,128]{2,1,0:T(8,128)S(1)}, u32[]{:S(2)}, u32[]{:S(2)}) collective-permute-start(f32[2,32,128]{2,1,0:T(8,128)S(1)} %get-tuple-element.36), channel_id=1, source_target_pairs={{0,8},{1,9},{2,10},{3,11},{4,124},{5,125},{6,126},{7,127},{8,16},{... | collective-permute-start | bytes 98312 | tf_op jit(solution)/shard_map/ppermute | solution.py:323
  49.4 5.2 %collective-permute-start.10 = (bf16[32,16,128]{2,1,0:T(8,128)(2,1)}, bf16[32,16,128]{2,1,0:T(8,128)(2,1)S(1)}, u32[]{:S(2)}, u32[]{:S(2)}) collective-permute-start(bf16[32,16,128]{2,1,0:T(8,128)(2,1)} %copy-done.11), channel_id=1, source_target_pairs={{0,2},{1,3},{2,4},{3,5},{4,6},{5,7},{6,0},{7,1},{8,10},{9,11},{10,... | collective-permute-start | bytes 393224 | tf_op jit(solution)/shard_map/ppermute | solution.py:328
  54.7 5.3 %collective-permute-start.11 = (bf16[32,16,128]{2,1,0:T(8,128)(2,1)S(1)}, bf16[32,16,128]{2,1,0:T(8,128)(2,1)S(1)}, u32[]{:S(2)}, u32[]{:S(2)}) collective-permute-start(bf16[32,16,128]{2,1,0:T(8,128)(2,1)S(1)} %copy-done.10), channel_id=1, source_target_pairs={{0,4},{1,5},{2,6},{3,7},{4,0},{5,1},{6,2},{7,3},{8,12},{9,13},{10,... | collective-permute-start | bytes 393224 | tf_op jit(solution)/shard_map/ppermute | solution.py:328
  60.0 19.9 %collective-permute-start.12 = (bf16[32,16,128]{2,1,0:T(8,128)(2,1)S(1)}, bf16[32,16,128]{2,1,0:T(8,128)(2,1)S(1)}, u32[]{:S(2)}, u32[]{:S(2)}) collective-permute-start(bf16[32,16,128]{2,1,0:T(8,128)(2,1)S(1)} %copy-done.8), channel_id=1, source_target_pairs={{0,6},{1,7},{2,0},{3,1},{4,2},{5,3},{6,4},{7,5},{8,14},{9,15},{10,... | collective-permute-start | bytes 393224 | tf_op jit(solution)/shard_map/ppermute | solution.py:328
  60.0 19.9 %collective-permute-start.13 = (bf16[32,16,128]{2,1,0:T(8,128)(2,1)S(1)}, bf16[32,16,128]{2,1,0:T(8,128)(2,1)S(1)}, u32[]{:S(2)}, u32[]{:S(2)}) collective-permute-start(bf16[32,16,128]{2,1,0:T(8,128)(2,1)S(1)} %copy-done.6), channel_id=1, source_target_pairs={{0,1},{1,0},{2,3},{3,2},{4,5},{5,4},{6,7},{7,6},{8,9},{9,8},{10,11... | collective-permute-start | bytes 393224 | tf_op jit(solution)/shard_map/ppermute | solution.py:328
  64.0 15.9 %collective-permute-start.14 = (bf16[32,16,128]{2,1,0:T(8,128)(2,1)S(1)}, bf16[32,16,128]{2,1,0:T(8,128)(2,1)S(1)}, u32[]{:S(2)}, u32[]{:S(2)}) collective-permute-start(bf16[32,16,128]{2,1,0:T(8,128)(2,1)S(1)} %copy-done.4), channel_id=1, source_target_pairs={{0,3},{1,2},{2,5},{3,4},{4,7},{5,6},{6,1},{7,0},{8,11},{9,10},{10,... | collective-permute-start | bytes 393224 | tf_op jit(solution)/shard_map/ppermute | solution.py:328
  65.7 14.3 %collective-permute-start.15 = (bf16[32,16,128]{2,1,0:T(8,128)(2,1)S(1)}, bf16[32,16,128]{2,1,0:T(8,128)(2,1)S(1)}, u32[]{:S(2)}, u32[]{:S(2)}) collective-permute-start(bf16[32,16,128]{2,1,0:T(8,128)(2,1)S(1)} %get-tuple-element.43), channel_id=1, source_target_pairs={{0,5},{1,4},{2,7},{3,6},{4,1},{5,0},{6,3},{7,2},{8,13},{9,12},{10,... | collective-permute-start | bytes 393224 | tf_op jit(solution)/shard_map/ppermute | solution.py:328
  65.7 14.2 %collective-permute-start.16 = (bf16[32,16,128]{2,1,0:T(8,128)(2,1)S(1)}, bf16[32,16,128]{2,1,0:T(8,128)(2,1)S(1)}, u32[]{:S(2)}, u32[]{:S(2)}) collective-permute-start(bf16[32,16,128]{2,1,0:T(8,128)(2,1)S(1)} %get-tuple-element.44), channel_id=1, source_target_pairs={{0,7},{1,6},{2,1},{3,0},{4,3},{5,2},{6,5},{7,4},{8,15},{9,14},{10,... | collective-permute-start | bytes 393224 | tf_op jit(solution)/shard_map/ppermute | solution.py:328
  81.5 5.0 %collective-permute-start.17 = (bf16[32,16,128]{2,1,0:T(8,128)(2,1)S(1)}, bf16[32,16,128]{2,1,0:T(8,128)(2,1)S(1)}, u32[]{:S(2)}, u32[]{:S(2)}) collective-permute-start(bf16[32,16,128]{2,1,0:T(8,128)(2,1)S(1)} %get-tuple-element.46), channel_id=1, source_target_pairs={{0,6},{1,7},{2,0},{3,1},{4,2},{5,3},{6,4},{7,5},{8,14},{9,15},{10,... | collective-permute-start | bytes 393224 | tf_op jit(solution)/shard_map/ppermute | solution.py:333
  82.3 6.1 %collective-permute-start.18 = (bf16[32,16,128]{2,1,0:T(8,128)(2,1)S(1)}, bf16[32,16,128]{2,1,0:T(8,128)(2,1)S(1)}, u32[]{:S(2)}, u32[]{:S(2)}) collective-permute-start(bf16[32,16,128]{2,1,0:T(8,128)(2,1)S(1)} %get-tuple-element.47), channel_id=1, source_target_pairs={{0,4},{1,5},{2,6},{3,7},{4,0},{5,1},{6,2},{7,3},{8,12},{9,13},{10,... | collective-permute-start | bytes 393224 | tf_op jit(solution)/shard_map/ppermute | solution.py:333
  82.6 9.5 %collective-permute-start.19 = (bf16[32,16,128]{2,1,0:T(8,128)(2,1)S(1)}, bf16[32,16,128]{2,1,0:T(8,128)(2,1)S(1)}, u32[]{:S(2)}, u32[]{:S(2)}) collective-permute-start(bf16[32,16,128]{2,1,0:T(8,128)(2,1)S(1)} %get-tuple-element.48), channel_id=1, source_target_pairs={{0,2},{1,3},{2,4},{3,5},{4,6},{5,7},{6,0},{7,1},{8,10},{9,11},{10,... | collective-permute-start | bytes 393224 | tf_op jit(solution)/shard_map/ppermute | solution.py:333
  83.4 8.7 %collective-permute-start.20 = (bf16[32,16,128]{2,1,0:T(8,128)(2,1)S(1)}, bf16[32,16,128]{2,1,0:T(8,128)(2,1)S(1)}, u32[]{:S(2)}, u32[]{:S(2)}) collective-permute-start(bf16[32,16,128]{2,1,0:T(8,128)(2,1)S(1)} %get-tuple-element.49), channel_id=1, source_target_pairs={{0,1},{1,0},{2,3},{3,2},{4,5},{5,4},{6,7},{7,6},{8,9},{9,8},{10,11... | collective-permute-start | bytes 393224 | tf_op jit(solution)/shard_map/ppermute | solution.py:333
  84.6 8.7 %collective-permute-start.21 = (bf16[32,16,128]{2,1,0:T(8,128)(2,1)S(1)}, bf16[32,16,128]{2,1,0:T(8,128)(2,1)S(1)}, u32[]{:S(2)}, u32[]{:S(2)}) collective-permute-start(bf16[32,16,128]{2,1,0:T(8,128)(2,1)S(1)} %get-tuple-element.50), channel_id=1, source_target_pairs={{0,7},{1,6},{2,1},{3,0},{4,3},{5,2},{6,5},{7,4},{8,15},{9,14},{10,... | collective-permute-start | bytes 393224 | tf_op jit(solution)/shard_map/ppermute | solution.py:333
  86.6 8.4 %collective-permute-start.22 = (bf16[32,16,128]{2,1,0:T(8,128)(2,1)S(1)}, bf16[32,16,128]{2,1,0:T(8,128)(2,1)S(1)}, u32[]{:S(2)}, u32[]{:S(2)}) collective-permute-start(bf16[32,16,128]{2,1,0:T(8,128)(2,1)S(1)} %get-tuple-element.51), channel_id=1, source_target_pairs={{0,5},{1,4},{2,7},{3,6},{4,1},{5,0},{6,3},{7,2},{8,13},{9,12},{10,... | collective-permute-start | bytes 393224 | tf_op jit(solution)/shard_map/ppermute | solution.py:333
  88.4 9.4 %collective-permute-start.23 = (bf16[32,16,128]{2,1,0:T(8,128)(2,1)S(1)}, bf16[32,16,128]{2,1,0:T(8,128)(2,1)S(1)}, u32[]{:S(2)}, u32[]{:S(2)}) collective-permute-start(bf16[32,16,128]{2,1,0:T(8,128)(2,1)S(1)} %get-tuple-element.52), channel_id=1, source_target_pairs={{0,3},{1,2},{2,5},{3,4},{4,7},{5,6},{6,1},{7,0},{8,11},{9,10},{10,... | collective-permute-start | bytes 393224 | tf_op jit(solution)/shard_map/ppermute | solution.py:333
  (7 other events, 5.3 us)
where the time goes:
time: 99.8 us; the launch traced here: 99.6 us
  starting transfers between devices  40.4 us (40%)
  waiting for transfers between devices  34.6 us (35%)
  Pallas kernels  20.7 us (21%)
  local copies, waits for them, and re-layouts  3.58 us (4%)
    pallas_call x6, Pallas kernels, call(): pl.pallas_call(kernel, in_specs=[smem()] * n_smem + [vmem()] * (len(args)...  20.7 us
    ppermute x4, starting transfers between devices, to_core(): return lax.ppermute(x, 'k', [(0, 1), (1, 0)])  9.98 us
    ppermute x7, starting transfers between devices, away(): return lax.ppermute(x, MEM, pairs)  9.76 us
    ppermute x7, waiting for transfers between devices, away(): return lax.ppermute(x, MEM, pairs)  9.25 us
    ppermute x7, starting transfers between devices, home(): return lax.ppermute(x, MEM, pairs)  9.12 us
    ppermute x2, waiting for transfers between devices, to_cells(): return lax.ppermute(x, 'cells', [(i, (i + by) % n) for i in range(n)])  7.13 us
    ppermute x7, waiting for transfers between devices, home(): return lax.ppermute(x, MEM, pairs)  7.12 us
    ppermute x1, waiting for transfers between devices, to_side(): return lax.ppermute(x, ('cells', 'z', 'k'), pairs)  6.07 us
  transfers between devices with their start and end apart: 24, of which 12 were waited for; matrix products, arithmetic and copies ran while one was open for 0% of the time, Pallas kernels for 13%

commit v1 on v0

--- a/solution.py
+++ b/solution.py
@@ -18,29 +18,43 @@
 
 
 def sense_kernel(info, bg, sg, *refs):
-    states, buf = refs[:8], refs[8]
+    keeps, (give, buf) = refs[:4], refs[4:]
     members, tiles, _ = bg.shape
     z, k = info[0], info[1]
     pitch = tiles + 1
+    row = lax.broadcasted_iota(jnp.int32, (128 * PACK, 128), 0)
+    lane, q = row & 127, row >> 7
+    goal = lane_id(128 * PACK) - 32 * q
+    pick = jnp.where((lane == goal) & (lane < 32), 1.0, 0.0)
+    pick = pick + jnp.where((lane - 32 == goal) & (lane >= 32) & (lane < 64), 0.5, 0.0)
+    pick = pick.astype(BF16)
     for m in range(members):
         buf[pl.ds(m * pitch, tiles), :] = bg[m].astype(F32)
-    quarter = lane_id(members) >> 5
     chunk = tiles // 8
-    for n, xd in enumerate(states):
+    for n in range(8):
         zone = 2 * ((z + n) % 4) + (k if n < 4 else 1 - k)
-
-        def group(i, carry, xd=xd, zone=zone):
-            row = None
+        xd, skip = (keeps[n], 0) if n < 4 else (give, chunk * (n - 4))
+        rows = []
+        for i in range(chunk // PACK):
+            group = []
             for q in range(PACK):
-                x = buf[pl.ds(chunk * zone + PACK * i + q, members, stride=pitch), :]
-                xd[PACK * i + q] = x.astype(BF16)
-                s = x + 0.5 * pltpu.roll(x, 96, 1)
-                s = s if q == 0 else pltpu.roll(s, 32 * q, 1)
-                row = s if q == 0 else jnp.where(quarter == q, s, row)
-            sg[(chunk // PACK) * zone + i] = row.astype(BF16)
-            return carry
-
-        lax.fori_loop(0, chunk // PACK, group, 0, unroll=4)
+                at = chunk * zone + PACK * i + q
+                x = buf[pl.ds(at, members, stride=pitch), :].astype(BF16)
+                xd[skip + PACK * i + q] = x
+                group.append(x)
+            rows.append(jnp.concatenate(group, axis=1))
+        sensed = jnp.dot(jnp.concatenate(rows, axis=0), pick, preferred_element_type=F32)
+        sensed = sensed.astype(BF16)
+        for i in range(chunk // PACK):
+            sg[(chunk // PACK) * zone + i] = sensed[members * i : members * (i + 1)]
+
+
+def both_kernel(k1, k2, k3, given, *outs):
+    for d, (keep, both) in enumerate(zip((k1, k2, k3), outs), 1):
+        n = keep.shape[0]
+        for i in range(n):
+            both[i] = keep[i]
+            both[n + i] = given[n * d + i]
 
 
 def window_kernel(info, sg, left, right, *outs):
@@ -82,31 +96,47 @@
                         w[16 * j + i] = right[src - 2 * half + i]
 
 
-def cell_kernel(info, pix, w2, y, nbr, out, near, own_nbr):
+def obs_kernel(info, pix, spread, y, active, w2, side):
+    half = pix.shape[0] // 2
+    counts = jnp.concatenate([active[...]] * 4, axis=0).astype(F32).T
+    slot = lane_id(half).astype(F32)
+    for h in range(2):
+        rows = pl.ds(half * h, half)
+        w2[rows, :] = jnp.where(slot < counts[:, h : h + 1], 1.0 / spread[rows, :], 0.0)
+    rows = pl.ds(pl.multiple_of(jnp.where(info[0] < 2, half, 0), half), half)
+    side[0] = pix[rows, :].astype(F32)
+    side[1] = w2[rows, :]
+    side[2] = y[rows, :]
+
+
+def cell_kernel(info, pix, w2, y, side, nbr, out, near, own_nbr):
     groups = pix.shape[0] // PACK
 
-    def packed(ref, p):
-        parts = [ref[pl.ds(2 * p + h, groups, stride=PACK), :] for h in range(2)]
-        return jnp.concatenate(parts, axis=0).astype(F32).T
-
-    cols = [[], []]
-    for p in range(2):
-        pt = packed(pix, p)
-        wt = packed(w2, p)
-        yt = packed(y, p) * wt
+    def sums(pt, wt, yt):
+        yt = yt * wt
         d, e = [], []
         for c in range(32):
             hit = pt == float(c)
             d.append(jnp.sum(jnp.where(hit, wt, 0.0), axis=0, keepdims=True))
             e.append(jnp.sum(jnp.where(hit, yt, 0.0), axis=0, keepdims=True))
-        for i, rows in enumerate((d, e)):
-            block = jnp.concatenate(rows, axis=0)
+        return jnp.concatenate(d, axis=0), jnp.concatenate(e, axis=0)
+
+    def packed(ref, n, qs):
+        parts = [ref[pl.ds(q, n, stride=PACK), :] for q in qs]
+        return jnp.concatenate(parts, axis=0).astype(F32).T
+
+    cols = [[], []]
+    for p in range(2):
+        qs = (2 * p, 2 * p + 1)
+        for i, block in enumerate(sums(*[packed(r, groups, qs) for r in (pix, w2, y)])):
             cols[i] += [block, pltpu.roll(block, 64, 1)]
-    own_nbr[...] = nbr[pl.ds(pl.multiple_of(64 * info[0] + 32 * info[1], 32), 32), :]
-    at = pl.multiple_of(jnp.where(info[0] < 2, 32, 0), 32)
     for i in range(2):
         out[i] = jnp.concatenate(cols[i], axis=0).T[:groups]
-        near[i] = out[i, pl.ds(at, 32), :]
+    some = sums(*[packed(side.at[i], groups // 2, range(PACK)) for i in range(3)])
+    for i, block in enumerate(some):
+        turned = [block] + [pltpu.roll(block, 128 - 32 * q, 1) for q in range(1, PACK)]
+        near[i] = jnp.concatenate(turned, axis=0).T[: groups // 2]
+    own_nbr[...] = nbr[pl.ds(pl.multiple_of(64 * info[0] + 32 * info[1], 32), 32), :]
 
 
 def pair_dot(left, right):
@@ -250,11 +280,12 @@
     lax.fori_loop(0, out.shape[0] // UNROLL, tiles, 0)
 
 
-def update_kernel(info, tr, *refs):
-    parts, outs = refs[:8], refs[8:]
+def update_kernel(info, tr, keep, given, s1, s2, s3, *outs):
+    n = tr.shape[0]
 
     def tile(t, carry):
-        x = jnp.concatenate([r[t] for r in parts], axis=0).astype(F32)
+        parts = [keep[t], s1[t], s2[t], s3[t], given[t], s1[n + t], s2[n + t], s3[n + t]]
+        x = jnp.concatenate(parts, axis=0).astype(F32)
         mean = jnp.sum(x, axis=0, keepdims=True) * (1.0 / 128.0)
         anomaly = (x - mean).astype(BF16)
         new = jnp.dot(tr[t], anomaly, preferred_element_type=F32) + mean
@@ -263,7 +294,7 @@
             o[t] = new[16 * i : 16 * i + 16]
         return carry
 
-    lax.fori_loop(0, tr.shape[0], tile, 0, unroll=8)
+    lax.fori_loop(0, n, tile, 0, unroll=8)
 
 
 def place_kernel(info, *refs):
@@ -288,10 +319,10 @@
     return pl.BlockSpec(memory_space=pltpu.SMEM)
 
 
-def call(kernel, n_smem, args, outs, scratch=(), mib=12):
+def call(kernel, n_smem, args, outs, scratch=(), mib=12, specs=None):
     return pl.pallas_call(
         kernel,
-        in_specs=[smem()] * n_smem + [vmem()] * (len(args) - n_smem),
+        in_specs=[smem()] * n_smem + list(specs or [vmem()] * (len(args) - n_smem)),
         out_specs=jax.tree.map(lambda _: vmem(), outs),
         out_shape=outs,
         scratch_shapes=list(scratch),
@@ -321,11 +352,6 @@
             cc = (c + 1) % n if zz < 2 else (c - 1) % n
             pairs += [(8 * c + 2 * z + k, 8 * cc + 2 * zz + k) for k in range(2)]
     return lax.ppermute(x, ("cells", "z", "k"), pairs)
-
-
-def away(x, d, o):
-    pairs = [(2 * z + k, 2 * ((z + d) % 4) + (k ^ o)) for z in range(4) for k in range(2)]
-    return lax.ppermute(x, MEM, pairs)
 
 
 def home(x, d, o):
@@ -345,32 +371,44 @@
         sense_kernel,
         1,
         (info, bg),
-        (shape(groups),) + (shape(tiles // 8),) * 8,
+        (shape(groups),) + (shape(tiles // 8),) * 4 + (shape(tiles // 2),),
         [pltpu.VMEM((members * (tiles + 1) + 7, width), F32)],
     )
     left = to_cells(sg[half:], 1)
     right = to_cells(sg[:half], -1)
-    windows = call(window_kernel, 1, (info, sg, left, right), (shape(80),) * 4)
+    keep, give = rest[:4], rest[4]
+    given = to_core(give)
+    windows = call(
+        window_kernel,
+        1,
+        (info, sg, left, right),
+        (shape(80),) * 4,
+    )
     own = [windows[0]] + [to_z(windows[d], d) for d in (1, 2, 3)]
-    state = [rest[i] if i == 0 else away(rest[i], i % 4, i // 4) for i in range(8)]
-    live = jnp.arange(128, dtype=jnp.int32)[None, :] < active[:, None]
-    w2 = jnp.where(live, 1.0 / spread, 0.0)
+    both = call(both_kernel, 0, (*keep[1:], given), (shape(tiles // 4),) * 3)
+    state = [to_z(both[d - 1], d) for d in (1, 2, 3)]
+    w2, side = call(
+        obs_kernel,
+        1,
+        (info, pixel, spread, figures, active.reshape(2, tiles // 2)),
+        (jax.ShapeDtypeStruct((tiles, 128), F32), jax.ShapeDtypeStruct((3, tiles // 2, 128), F32)),
+    )
+    side = to_side(side, 0)
     de, near, own_nbr = call(
         cell_kernel,
         1,
-        (info, pixel, w2, figures, nbr),
+        (info, pixel, w2, figures, side, nbr),
         (
             jax.ShapeDtypeStruct((2, groups, 128), F32),
             jax.ShapeDtypeStruct((2, half, 128), F32),
             jax.ShapeDtypeStruct((32, 4), jnp.int32),
         ),
     )
-    dn = to_side(near, 0)
     own += [to_core(r) for r in own]
     transform = call(
         solve_kernel,
         2,
-        (info, own_nbr, *own, de, dn),
+        (info, own_nbr, *own, de, near),
         jax.ShapeDtypeStruct((32, 128, 128), BF16),
         [
             pltpu.VMEM((72, 128, 128), BF16),
@@ -379,7 +417,7 @@
         ],
         40,
     )
-    outs = call(update_kernel, 1, (info, transform, *state), (shape(32),) * 8)
+    outs = call(update_kernel, 1, (info, transform, keep[0], given, *state), (shape(32),) * 8)
     back = [
         outs[i] if i == 0 else home(outs[i], i % 4, i // 4) for i in range(8)
     ]

time: 99.8 us -> 82.5 us (0.83)
  waiting for transfers between devices: 34.6 us -> 22.4 us
  starting transfers between devices: 40.4 us -> 33.8 us
    ppermute x7 -> x0, starting transfers between devices: 9.76 us -> none  [away(): return lax.ppermute(x, MEM, pairs)]
    ppermute x7 -> x0, waiting for transfers between devices: 9.25 us -> none  [away(): return lax.ppermute(x, MEM, pairs)]
    ppermute x3 -> x6, starting transfers between devices: 5.74 us -> 12 us  [to_z(): return lax.ppermute(x, 'z', [(i, (i + by) % 4) for i in range(4)])]
    ppermute x3 -> x6, waiting for transfers between devices: 4.98 us -> 9.28 us  [to_z(): return lax.ppermute(x, 'z', [(i, (i + by) % 4) for i in range(4)])]
    ppermute x4 -> x5, starting transfers between devices: 9.98 us -> 5.81 us  [to_core(): return lax.ppermute(x, 'k', [(0, 1), (1, 0)])]
    ppermute x2, waiting for transfers between devices: 7.13 us -> 3.09 us  [to_cells(): return lax.ppermute(x, 'cells', [(i, (i + by) % n) for i in range(n)])]
    ppermute x1, waiting for transfers between devices: 6.07 us -> 3.75 us  [to_side(): return lax.ppermute(x, ('cells', 'z', 'k'), pairs)]
    ppermute x7, starting transfers between devices: 9.12 us -> 10.1 us  [home(): return lax.ppermute(x, MEM, pairs)]
  transfers between devices with their start and end apart: 24 -> 21, of which waited for: 12 -> 8; matrix products, arithmetic and copies ran while one was open for 0% -> 0% of each run, Pallas kernels for 13% -> 19%
where the time goes in v1:
time: 82.5 us; the launch traced here: 82.3 us
  starting transfers between devices  33.8 us (41%)
  waiting for transfers between devices  22.4 us (27%)
  Pallas kernels  21.3 us (26%)
  local copies, waits for them, and re-layouts  4.52 us (5%)
    pallas_call x8, Pallas kernels, call(): pl.pallas_call(kernel, in_specs=[smem()] * n_smem + list(specs or [vmem()...  21.3 us
    ppermute x6, starting transfers between devices, to_z(): return lax.ppermute(x, 'z', [(i, (i + by) % 4) for i in range(4)])  12 us
    ppermute x7, starting transfers between devices, home(): return lax.ppermute(x, MEM, pairs)  10.1 us
    ppermute x6, waiting for transfers between devices, to_z(): return lax.ppermute(x, 'z', [(i, (i + by) % 4) for i in range(4)])  9.28 us
    ppermute x7, waiting for transfers between devices, home(): return lax.ppermute(x, MEM, pairs)  6.3 us
    ppermute x2, starting transfers between devices, to_cells(): return lax.ppermute(x, 'cells', [(i, (i + by) % n) for i in range(n)])  5.82 us
    ppermute x5, starting transfers between devices, to_core(): return lax.ppermute(x, 'k', [(0, 1), (1, 0)])  5.81 us
    unnamed x25, local copies, waits for them, and re-layouts  4.5 us
  transfers between devices with their start and end apart: 21, of which 8 were waited for; matrix products, arithmetic and copies ran while one was open for 0% of the time, Pallas kernels for 19%

profile of v1, /device:TPU:1, one launch (start us, length us, event | category | flops | bytes accessed | tf_op | source)
XLA Modules:
  0.0 82.3 jit_solution(7725425206298833440)
XLA Ops:
  0.1 1.2 %copy-done = bf16[16,256,128]{2,1,0:T(8,128)(2,1)S(1)} copy-done((bf16[16,256,128]{2,1,0:T(8,128)(2,1)S(1)}, bf16[16,256,128]{2,1,0:T(8,128)(2,1)}, u32[]{:S(2)}) %copy-start) | copy-done | bytes 1048600
  1.3 1.1 %shard_map.66 = (bf16[64,16,128]{2,1,0:T(8,128)(2,1)S(1)}, bf16[32,16,128]{2,1,0:T(8,128)(2,1)S(1)}, bf16[32,16,128]{2,1,0:T(8,128)(2,1)S(1)}, bf16[32,16,128]{2...) custom-call(s32[4]{0:T(128)S(1)} %pad_add_fusion.info, ...), custom_call_target="tpu_custom_call" | custom-call | tf_op jit(solution)/shard_map/pallas_call | solution.py:323
  3.1 2.0 %collective-permute-start.1 = (bf16[32,16,128]{2,1,0:T(8,128)(2,1)S(1)}, bf16[32,16,128]{2,1,0:T(8,128)(2,1)S(1)}, u32[]{:S(2)}, u32[]{:S(2)}) collective-permute-start(bf16[32,16,128]{2,1,0:T(8,128)(2,1)S(1)} %get-tuple-element.58), channel_id=1, source_target_pairs={{0,8},{8,16},{16,24},{24,32},{32,40},{40,48},{48,56},{56,64},{64,7... | collective-permute-start | bytes 393224 | tf_op jit(solution)/shard_map/ppermute | solution.py:343
  5.1 3.8 %collective-permute-start.2 = (bf16[32,16,128]{2,1,0:T(8,128)(2,1)S(1)}, bf16[32,16,128]{2,1,0:T(8,128)(2,1)S(1)}, u32[]{:S(2)}, u32[]{:S(2)}) collective-permute-start(bf16[32,16,128]{2,1,0:T(8,128)(2,1)S(1)} %get-tuple-element.57), channel_id=1, source_target_pairs={{0,120},{8,0},{16,8},{24,16},{32,24},{40,32},{48,40},{56,48},{64,5... | collective-permute-start | bytes 393224 | tf_op jit(solution)/shard_map/ppermute | solution.py:343
  8.9 3.1 %collective-permute-done.1.left = bf16[32,16,128]{2,1,0:T(8,128)(2,1)S(1)} collective-permute-done((bf16[32,16,128]{2,1,0:T(8,128)(2,1)S(1)}, bf16[32,16,128]{2,1,0:T(8,128)(2,1)S(1)}, u32[]{:S(2)}, u32[]{:S(2)}) %collective-permute-start.1) | collective-permute-done | bytes 131104 | tf_op jit(solution)/shard_map/ppermute | solution.py:343
  12.9 1.6 %collective-permute-start.3 = (bf16[80,16,128]{2,1,0:T(8,128)(2,1)S(1)}, bf16[80,16,128]{2,1,0:T(8,128)(2,1)S(1)}, u32[]{:S(2)}, u32[]{:S(2)}) collective-permute-start(bf16[80,16,128]{2,1,0:T(8,128)(2,1)S(1)} %get-tuple-element.36), channel_id=1, source_target_pairs={{0,2},{2,4},{4,6},{6,0},{1,3},{3,5},{5,7},{7,1},{8,10},{10,12},{12... | collective-permute-start | bytes 983048 | tf_op jit(solution)/shard_map/ppermute | solution.py:334
  14.5 1.7 %collective-permute-start.10 = (bf16[128,16,128]{2,1,0:T(8,128)(2,1)S(1)}, bf16[128,16,128]{2,1,0:T(8,128)(2,1)S(1)}, u32[]{:S(2)}, u32[]{:S(2)}) collective-permute-start(bf16[128,16,128]{2,1,0:T(8,128)(2,1)S(1)} %get-tuple-element.42), channel_id=1, source_target_pairs={{0,1},{1,0},{2,3},{3,2},{4,5},{5,4},{6,7},{7,6},{8,9},{9,8},{10,11... | collective-permute-start | bytes 1572872 | tf_op jit(solution)/shard_map/ppermute | solution.py:338
  16.1 3.3 %collective-permute-start.4 = (bf16[80,16,128]{2,1,0:T(8,128)(2,1)S(1)}, bf16[80,16,128]{2,1,0:T(8,128)(2,1)S(1)}, u32[]{:S(2)}, u32[]{:S(2)}) collective-permute-start(bf16[80,16,128]{2,1,0:T(8,128)(2,1)S(1)} %get-tuple-element.37), channel_id=1, source_target_pairs={{0,4},{2,6},{4,0},{6,2},{1,5},{3,7},{5,1},{7,3},{8,12},{10,14},{12... | collective-permute-start | bytes 983048 | tf_op jit(solution)/shard_map/ppermute | solution.py:334
  20.7 2.6 %collective-permute-done.3.refs_1_ = bf16[80,16,128]{2,1,0:T(8,128)(2,1)S(1)} collective-permute-done((bf16[80,16,128]{2,1,0:T(8,128)(2,1)S(1)}, bf16[80,16,128]{2,1,0:T(8,128)(2,1)S(1)}, u32[]{:S(2)}, u32[]{:S(2)}) %collective-permute-start.3) | collective-permute-done | bytes 327712 | tf_op jit(solution)/shard_map/ppermute | solution.py:334
  23.3 2.6 %collective-permute-start.7 = (bf16[80,16,128]{2,1,0:T(8,128)(2,1)S(1)}, bf16[80,16,128]{2,1,0:T(8,128)(2,1)S(1)}, u32[]{:S(2)}, u32[]{:S(2)}) collective-permute-start(bf16[80,16,128]{2,1,0:T(8,128)(2,1)S(1)} %collective-permute-done.3.refs_1_), channel_id=1, source_target_pairs={{0,1},{1,0},{2,3},{3,2},{4,5},{5,4},{6,7},{7,6},{8,9},{9,8},{10,11... | collective-permute-start | bytes 983048 | tf_op jit(solution)/shard_map/ppermute | solution.py:338
  26.7 4.5 %collective-permute-done.4.refs_2_ = bf16[80,16,128]{2,1,0:T(8,128)(2,1)S(1)} collective-permute-done((bf16[80,16,128]{2,1,0:T(8,128)(2,1)S(1)}, bf16[80,16,128]{2,1,0:T(8,128)(2,1)S(1)}, u32[]{:S(2)}, u32[]{:S(2)}) %collective-permute-start.4) | collective-permute-done | bytes 327712 | tf_op jit(solution)/shard_map/ppermute | solution.py:334
  31.2 2.2 %collective-permute-done.5.refs_3_ = bf16[80,16,128]{2,1,0:T(8,128)(2,1)S(1)} collective-permute-done((bf16[80,16,128]{2,1,0:T(8,128)(2,1)S(1)}, bf16[80,16,128]{2,1,0:T(8,128)(2,1)S(1)}, u32[]{:S(2)}, u32[]{:S(2)}) %collective-permute-start.5) | collective-permute-done | bytes 327712 | tf_op jit(solution)/shard_map/ppermute | solution.py:334
  33.4 0.9 %collective-permute-start.8 = (bf16[80,16,128]{2,1,0:T(8,128)(2,1)S(1)}, bf16[80,16,128]{2,1,0:T(8,128)(2,1)S(1)}, u32[]{:S(2)}, u32[]{:S(2)}) collective-permute-start(bf16[80,16,128]{2,1,0:T(8,128)(2,1)S(1)} %collective-permute-done.4.refs_2_), channel_id=1, source_target_pairs={{0,1},{1,0},{2,3},{3,2},{4,5},{5,4},{6,7},{7,6},{8,9},{9,8},{10,11... | collective-permute-start | bytes 983048 | tf_op jit(solution)/shard_map/ppermute | solution.py:338
  34.4 0.9 %shard_map.69 = (bf16[64,16,128]{2,1,0:T(8,128)(2,1)}, bf16[64,16,128]{2,1,0:T(8,128)(2,1)}, bf16[64,16,128]{2,1,0:T(8,128)(2,1)}) custom-call(bf16[32,16,128]{2,1,0:T(8,128)(2,1)S(1)} %get-tuple-element.43.k1, bf16[32,16,128]{2,1,0:T(8,128)(2,1)S(1)} %get-tuple-element.44.k2, bf16[32,16,128]{2,1,0:T(8,128)(2,1)S(1)} %get-tuple-element.45.k3, ...), custom_call_target="tpu_custom_call" | custom-call | tf_op jit(solution)/shard_map/pallas_call | solution.py:323
  35.3 3.7 %collective-permute-done.side = f32[3,128,128]{2,1,0:T(8,128)S(1)} collective-permute-done((f32[3,128,128]{2,1,0:T(8,128)S(1)}, f32[3,128,128]{2,1,0:T(8,128)S(1)}, u32[]{:S(2)}, u32[]{:S(2)}) %collective-permute-start) | collective-permute-done | bytes 196640 | tf_op jit(solution)/shard_map/ppermute | solution.py:354
  39.7 2.7 %collective-permute-start.11 = (bf16[64,16,128]{2,1,0:T(8,128)(2,1)}, bf16[64,16,128]{2,1,0:T(8,128)(2,1)}, u32[]{:S(2)}, u32[]{:S(2)}) collective-permute-start(bf16[64,16,128]{2,1,0:T(8,128)(2,1)} %get-tuple-element.46), channel_id=1, source_target_pairs={{0,2},{2,4},{4,6},{6,0},{1,3},{3,5},{5,7},{7,1},{8,10},{10,12},{12... | collective-permute-start | bytes 786440 | tf_op jit(solution)/shard_map/ppermute | solution.py:334
  42.4 1.6 %collective-permute-start.12 = (bf16[64,16,128]{2,1,0:T(8,128)(2,1)}, bf16[64,16,128]{2,1,0:T(8,128)(2,1)}, u32[]{:S(2)}, u32[]{:S(2)}) collective-permute-start(bf16[64,16,128]{2,1,0:T(8,128)(2,1)} %get-tuple-element.47), channel_id=1, source_target_pairs={{0,4},{2,6},{4,0},{6,2},{1,5},{3,7},{5,1},{7,3},{8,12},{10,14},{12... | collective-permute-start | bytes 786440 | tf_op jit(solution)/shard_map/ppermute | solution.py:334
  44.0 2.1 %collective-permute-start.13 = (bf16[64,16,128]{2,1,0:T(8,128)(2,1)}, bf16[64,16,128]{2,1,0:T(8,128)(2,1)}, u32[]{:S(2)}, u32[]{:S(2)}) collective-permute-start(bf16[64,16,128]{2,1,0:T(8,128)(2,1)} %get-tuple-element.48), channel_id=1, source_target_pairs={{0,6},{2,0},{4,2},{6,4},{1,7},{3,1},{5,3},{7,5},{8,14},{10,8},{12,... | collective-permute-start | bytes 786440 | tf_op jit(solution)/shard_map/ppermute | solution.py:334
  46.2 0.9 %copy-done.4 = f32[3,128,128]{2,1,0:T(8,128)S(1)} copy-done((f32[3,128,128]{2,1,0:T(8,128)S(1)}, f32[3,128,128]{2,1,0:T(8,128)}, u32[]{:S(2)}) %copy-start.4) | copy-done | bytes 196632
  47.2 0.9 %copy-done.6 = f32[256,128]{1,0:T(8,128)S(1)} copy-done((f32[256,128]{1,0:T(8,128)S(1)}, f32[256,128]{1,0:T(8,128)}, u32[]{:S(2)}) %copy-start.6) | copy-done | bytes 131096
  48.1 2.2 %shard_map.65 = (f32[2,64,128]{2,1,0:T(8,128)S(1)}, f32[2,32,128]{2,1,0:T(8,128)S(1)}, s32[32,4]{1,0:T(8,128)S(1)}) custom-call(s32[4]{0:T(128)S(1)} %pad_add_fusion.info, s32[256,128]{1,0:T(8,128)S(1)} %copy-done.1, f32[256,128]{1,0:T(8,128)S(1)} %copy-done.6, f32[256,128]{1,0:T(8,128)S(1)} %copy-done.2, f32[3,128,128]{2,1,0:T(8,128)S(1)} %copy-done.4, ...), custom_call_target="tpu_custom_call" | custom-call | tf_op jit(solution)/shard_map/pallas_call | solution.py:323
  50.3 11.4 %shard_map.68.tr = bf16[32,128,128]{2,1,0:T(8,128)(2,1)S(1)} custom-call(s32[4]{0:T(128)S(1)} %pad_add_fusion.info, s32[32,4]{1,0:T(8,128)S(1)} %get-tuple-element.33.nbr, bf16[80,16,128]{2,1,0:T(8,128)(2,1)S(1)} %get-tuple-element.35.refs_0_, bf16[80,16,128]{2,1,0:T(8,128)(2,1)S(1)} %collective-permute-done.3.refs_1_, ...), custom_call_target="tpu_custom_call" | custom-call | tf_op jit(solution)/shard_map/pallas_call | solution.py:323
  61.8 2.2 %shard_map.70 = (bf16[32,16,128]{2,1,0:T(8,128)(2,1)S(1)}, bf16[32,16,128]{2,1,0:T(8,128)(2,1)S(1)}, bf16[32,16,128]{2,1,0:T(8,128)(2,1)S(1)}, bf16[32,16,128]{2...) custom-call(s32[4]{0:T(128)S(1)} %pad_add_fusion.info, ...), custom_call_target="tpu_custom_call" | custom-call | tf_op jit(solution)/shard_map/pallas_call | solution.py:323
  64.1 1.2 %collective-permute-start.15 = (bf16[32,16,128]{2,1,0:T(8,128)(2,1)S(1)}, bf16[32,16,128]{2,1,0:T(8,128)(2,1)S(1)}, u32[]{:S(2)}, u32[]{:S(2)}) collective-permute-start(bf16[32,16,128]{2,1,0:T(8,128)(2,1)S(1)} %get-tuple-element.51), channel_id=1, source_target_pairs={{0,4},{1,5},{2,6},{3,7},{4,0},{5,1},{6,2},{7,3},{8,12},{9,13},{10,... | collective-permute-start | bytes 393224 | tf_op jit(solution)/shard_map/ppermute | solution.py:359
  65.5 3.2 %collective-permute-start.17 = (bf16[32,16,128]{2,1,0:T(8,128)(2,1)S(1)}, bf16[32,16,128]{2,1,0:T(8,128)(2,1)S(1)}, u32[]{:S(2)}, u32[]{:S(2)}) collective-permute-start(bf16[32,16,128]{2,1,0:T(8,128)(2,1)S(1)} %get-tuple-element.53), channel_id=1, source_target_pairs={{0,1},{1,0},{2,3},{3,2},{4,5},{5,4},{6,7},{7,6},{8,9},{9,8},{10,11... | collective-permute-start | bytes 393224 | tf_op jit(solution)/shard_map/ppermute | solution.py:359
  68.7 1.5 %collective-permute-start.18 = (bf16[32,16,128]{2,1,0:T(8,128)(2,1)S(1)}, bf16[32,16,128]{2,1,0:T(8,128)(2,1)S(1)}, u32[]{:S(2)}, u32[]{:S(2)}) collective-permute-start(bf16[32,16,128]{2,1,0:T(8,128)(2,1)S(1)} %get-tuple-element.54), channel_id=1, source_target_pairs={{0,7},{1,6},{2,1},{3,0},{4,3},{5,2},{6,5},{7,4},{8,15},{9,14},{10,... | collective-permute-start | bytes 393224 | tf_op jit(solution)/shard_map/ppermute | solution.py:359
  70.2 2.8 %collective-permute-start.19 = (bf16[32,16,128]{2,1,0:T(8,128)(2,1)S(1)}, bf16[32,16,128]{2,1,0:T(8,128)(2,1)S(1)}, u32[]{:S(2)}, u32[]{:S(2)}) collective-permute-start(bf16[32,16,128]{2,1,0:T(8,128)(2,1)S(1)} %get-tuple-element.55), channel_id=1, source_target_pairs={{0,5},{1,4},{2,7},{3,6},{4,1},{5,0},{6,3},{7,2},{8,13},{9,12},{10,... | collective-permute-start | bytes 393224 | tf_op jit(solution)/shard_map/ppermute | solution.py:359
  73.1 1.1 %collective-permute-start.20 = (bf16[32,16,128]{2,1,0:T(8,128)(2,1)S(1)}, bf16[32,16,128]{2,1,0:T(8,128)(2,1)S(1)}, u32[]{:S(2)}, u32[]{:S(2)}) collective-permute-start(bf16[32,16,128]{2,1,0:T(8,128)(2,1)S(1)} %get-tuple-element.56), channel_id=1, source_target_pairs={{0,3},{1,2},{2,5},{3,4},{4,7},{5,6},{6,1},{7,0},{8,11},{9,10},{10,... | collective-permute-start | bytes 393224 | tf_op jit(solution)/shard_map/ppermute | solution.py:359
  74.2 1.4 %collective-permute-done.18.refs_5_ = bf16[32,16,128]{2,1,0:T(8,128)(2,1)S(1)} collective-permute-done((bf16[32,16,128]{2,1,0:T(8,128)(2,1)S(1)}, bf16[32,16,128]{2,1,0:T(8,128)(2,1)S(1)}, u32[]{:S(2)}, u32[]{:S(2)}) %collective-permute-start.18) | collective-permute-done | bytes 131104 | tf_op jit(solution)/shard_map/ppermute | solution.py:359
  75.6 1.7 %collective-permute-done.19.refs_6_ = bf16[32,16,128]{2,1,0:T(8,128)(2,1)S(1)} collective-permute-done((bf16[32,16,128]{2,1,0:T(8,128)(2,1)S(1)}, bf16[32,16,128]{2,1,0:T(8,128)(2,1)S(1)}, u32[]{:S(2)}, u32[]{:S(2)}) %collective-permute-start.19) | collective-permute-done | bytes 131104 | tf_op jit(solution)/shard_map/ppermute | solution.py:359
  77.3 3.1 %collective-permute-done.20.refs_7_ = bf16[32,16,128]{2,1,0:T(8,128)(2,1)S(1)} collective-permute-done((bf16[32,16,128]{2,1,0:T(8,128)(2,1)S(1)}, bf16[32,16,128]{2,1,0:T(8,128)(2,1)S(1)}, u32[]{:S(2)}, u32[]{:S(2)}) %collective-permute-start.20) | collective-permute-done | bytes 131104 | tf_op jit(solution)/shard_map/ppermute | solution.py:359
  80.5 1.8 %shard_map.71 = bf16[16,256,128]{2,1,0:T(8,128)(2,1)} custom-call(s32[4]{0:T(128)S(1)} %pad_add_fusion.info, bf16[32,16,128]{2,1,0:T(8,128)(2,1)S(1)} %get-tuple-element.49.refs_0_, bf16[32,16,128]{2,1,0:T(8,128)(2,1)S(1)} %collective-permute-done.14.refs_1_, bf16[32,16,128]{2,1,0:T(8,128)(2,1)S(1)} %collective-permute-done.15.refs_2_, ...), custom_call_target="tpu_custom_call" | custom-call | tf_op jit(solution)/shard_map/pallas_call | solution.py:323
  (45 shorter events, 4.9 us)
Async XLA Ops:
  0.1 1.2 %copy-start = (bf16[16,256,128]{2,1,0:T(8,128)(2,1)S(1)}, bf16[16,256,128]{2,1,0:T(8,128)(2,1)}, u32[]{:S(2)}) copy-start(bf16[16,256,128]{2,1,0:T(8,128)(2,1)} %bg.1) | copy-start | bytes 3145732
  3.1 8.9 %collective-permute-start.1 = (bf16[32,16,128]{2,1,0:T(8,128)(2,1)S(1)}, bf16[32,16,128]{2,1,0:T(8,128)(2,1)S(1)}, u32[]{:S(2)}, u32[]{:S(2)}) collective-permute-start(bf16[32,16,128]{2,1,0:T(8,128)(2,1)S(1)} %get-tuple-element.58), channel_id=1, source_target_pairs={{0,8},{8,16},{16,24},{24,32},{32,40},{40,48},{48,56},{56,64},{64,7... | collective-permute-start | bytes 393224 | tf_op jit(solution)/shard_map/ppermute | solution.py:343
  5.1 20.8 %copy-start.1 = (s32[256,128]{1,0:T(8,128)S(1)}, s32[256,128]{1,0:T(8,128)}, u32[]{:S(2)}) copy-start(s32[256,128]{1,0:T(8,128)} %pix.3) | copy-start | bytes 393220
  5.1 20.8 %copy-start.2 = (f32[256,128]{1,0:T(8,128)S(1)}, f32[256,128]{1,0:T(8,128)}, u32[]{:S(2)}) copy-start(f32[256,128]{1,0:T(8,128)} %y.3) | copy-start | bytes 393220
  5.1 20.8 %copy-start.7 = (f32[256,128]{1,0:T(8,128)S(1)}, f32[256,128]{1,0:T(8,128)}, u32[]{:S(2)}) copy-start(f32[256,128]{1,0:T(8,128)} %spread.1) | copy-start | bytes 393220
  5.1 6.9 %collective-permute-start.2 = (bf16[32,16,128]{2,1,0:T(8,128)(2,1)S(1)}, bf16[32,16,128]{2,1,0:T(8,128)(2,1)S(1)}, u32[]{:S(2)}, u32[]{:S(2)}) collective-permute-start(bf16[32,16,128]{2,1,0:T(8,128)(2,1)S(1)} %get-tuple-element.57), channel_id=1, source_target_pairs={{0,120},{8,0},{16,8},{24,16},{32,24},{40,32},{48,40},{56,48},{64,5... | collective-permute-start | bytes 393224 | tf_op jit(solution)/shard_map/ppermute | solution.py:343
  12.9 10.4 %collective-permute-start.3 = (bf16[80,16,128]{2,1,0:T(8,128)(2,1)S(1)}, bf16[80,16,128]{2,1,0:T(8,128)(2,1)S(1)}, u32[]{:S(2)}, u32[]{:S(2)}) collective-permute-start(bf16[80,16,128]{2,1,0:T(8,128)(2,1)S(1)} %get-tuple-element.36), channel_id=1, source_target_pairs={{0,2},{2,4},{4,6},{6,0},{1,3},{3,5},{5,7},{7,1},{8,10},{10,12},{12... | collective-permute-start | bytes 983048 | tf_op jit(solution)/shard_map/ppermute | solution.py:334
  14.5 19.9 %collective-permute-start.10 = (bf16[128,16,128]{2,1,0:T(8,128)(2,1)S(1)}, bf16[128,16,128]{2,1,0:T(8,128)(2,1)S(1)}, u32[]{:S(2)}, u32[]{:S(2)}) collective-permute-start(bf16[128,16,128]{2,1,0:T(8,128)(2,1)S(1)} %get-tuple-element.42), channel_id=1, source_target_pairs={{0,1},{1,0},{2,3},{3,2},{4,5},{5,4},{6,7},{7,6},{8,9},{9,8},{10,11... | collective-permute-start | bytes 1572872 | tf_op jit(solution)/shard_map/ppermute | solution.py:338
  16.1 15.1 %collective-permute-start.4 = (bf16[80,16,128]{2,1,0:T(8,128)(2,1)S(1)}, bf16[80,16,128]{2,1,0:T(8,128)(2,1)S(1)}, u32[]{:S(2)}, u32[]{:S(2)}) collective-permute-start(bf16[80,16,128]{2,1,0:T(8,128)(2,1)S(1)} %get-tuple-element.37), channel_id=1, source_target_pairs={{0,4},{2,6},{4,0},{6,2},{1,5},{3,7},{5,1},{7,3},{8,12},{10,14},{12... | collective-permute-start | bytes 983048 | tf_op jit(solution)/shard_map/ppermute | solution.py:334
  19.4 14.0 %collective-permute-start.5 = (bf16[80,16,128]{2,1,0:T(8,128)(2,1)S(1)}, bf16[80,16,128]{2,1,0:T(8,128)(2,1)S(1)}, u32[]{:S(2)}, u32[]{:S(2)}) collective-permute-start(bf16[80,16,128]{2,1,0:T(8,128)(2,1)S(1)} %get-tuple-element.38), channel_id=1, source_target_pairs={{0,6},{2,0},{4,2},{6,4},{1,7},{3,1},{5,3},{7,5},{8,14},{10,8},{12,... | collective-permute-start | bytes 983048 | tf_op jit(solution)/shard_map/ppermute | solution.py:334
  20.2 5.8 %copy-start.10 = (s32[256]{0:T(256)S(1)}, s32[256]{0:T(256)}, u32[]{:S(2)}) copy-start(s32[256]{0:T(256)} %param.10) | copy-start | bytes 3076
  20.2 22.2 %collective-permute-start.6 = (bf16[80,16,128]{2,1,0:T(8,128)(2,1)S(1)}, bf16[80,16,128]{2,1,0:T(8,128)(2,1)S(1)}, u32[]{:S(2)}, u32[]{:S(2)}) collective-permute-start(bf16[80,16,128]{2,1,0:T(8,128)(2,1)S(1)} %get-tuple-element.35.refs_0_), channel_id=1, source_target_pairs={{0,1},{1,0},{2,3},{3,2},{4,5},{5,4},{6,7},{7,6},{8,9},{9,8},{10,11... | collective-permute-start | bytes 983048 | tf_op jit(solution)/shard_map/ppermute | solution.py:338
  23.3 20.7 %collective-permute-start.7 = (bf16[80,16,128]{2,1,0:T(8,128)(2,1)S(1)}, bf16[80,16,128]{2,1,0:T(8,128)(2,1)S(1)}, u32[]{:S(2)}, u32[]{:S(2)}) collective-permute-start(bf16[80,16,128]{2,1,0:T(8,128)(2,1)S(1)} %collective-permute-done.3.refs_1_), channel_id=1, source_target_pairs={{0,1},{1,0},{2,3},{3,2},{4,5},{5,4},{6,7},{7,6},{8,9},{9,8},{10,11... | collective-permute-start | bytes 983048 | tf_op jit(solution)/shard_map/ppermute | solution.py:338
  26.7 8.6 %copy-start.5 = (f32[256,128]{1,0:T(8,128)}, f32[256,128]{1,0:T(8,128)S(1)}, u32[]{:S(2)}) copy-start(f32[256,128]{1,0:T(8,128)S(1)} %get-tuple-element.31.w2) | copy-start | bytes 393220
  31.2 7.8 %collective-permute-start = (f32[3,128,128]{2,1,0:T(8,128)S(1)}, f32[3,128,128]{2,1,0:T(8,128)S(1)}, u32[]{:S(2)}, u32[]{:S(2)}) collective-permute-start(f32[3,128,128]{2,1,0:T(8,128)S(1)} %get-tuple-element.32), channel_id=1, source_target_pairs={{0,8},{1,9},{2,10},{3,11},{4,124},{5,125},{6,126},{7,127},{8,16},{... | collective-permute-start | bytes 589832 | tf_op jit(solution)/shard_map/ppermute | solution.py:354
  33.4 16.9 %collective-permute-start.8 = (bf16[80,16,128]{2,1,0:T(8,128)(2,1)S(1)}, bf16[80,16,128]{2,1,0:T(8,128)(2,1)S(1)}, u32[]{:S(2)}, u32[]{:S(2)}) collective-permute-start(bf16[80,16,128]{2,1,0:T(8,128)(2,1)S(1)} %collective-permute-done.4.refs_2_), channel_id=1, source_target_pairs={{0,1},{1,0},{2,3},{3,2},{4,5},{5,4},{6,7},{7,6},{8,9},{9,8},{10,11... | collective-permute-start | bytes 983048 | tf_op jit(solution)/shard_map/ppermute | solution.py:338
  34.4 16.0 %collective-permute-start.9 = (bf16[80,16,128]{2,1,0:T(8,128)(2,1)S(1)}, bf16[80,16,128]{2,1,0:T(8,128)(2,1)S(1)}, u32[]{:S(2)}, u32[]{:S(2)}) collective-permute-start(bf16[80,16,128]{2,1,0:T(8,128)(2,1)S(1)} %collective-permute-done.5.refs_3_), channel_id=1, source_target_pairs={{0,1},{1,0},{2,3},{3,2},{4,5},{5,4},{6,7},{7,6},{8,9},{9,8},{10,11... | collective-permute-start | bytes 983048 | tf_op jit(solution)/shard_map/ppermute | solution.py:338
  35.3 10.8 %copy-start.11 = (s32[256,4]{0,1:T(4,128)S(1)}, s32[256,4]{0,1:T(4,128)}, u32[]{:S(2)}) copy-start(s32[256,4]{0,1:T(4,128)} %param.11) | copy-start | bytes 12292
  39.0 0.7 copy-start.3
  39.7 22.1 %collective-permute-start.11 = (bf16[64,16,128]{2,1,0:T(8,128)(2,1)}, bf16[64,16,128]{2,1,0:T(8,128)(2,1)}, u32[]{:S(2)}, u32[]{:S(2)}) collective-permute-start(bf16[64,16,128]{2,1,0:T(8,128)(2,1)} %get-tuple-element.46), channel_id=1, source_target_pairs={{0,2},{2,4},{4,6},{6,0},{1,3},{3,5},{5,7},{7,1},{8,10},{10,12},{12... | collective-permute-start | bytes 786440 | tf_op jit(solution)/shard_map/ppermute | solution.py:334
  42.4 19.4 %collective-permute-start.12 = (bf16[64,16,128]{2,1,0:T(8,128)(2,1)}, bf16[64,16,128]{2,1,0:T(8,128)(2,1)}, u32[]{:S(2)}, u32[]{:S(2)}) collective-permute-start(bf16[64,16,128]{2,1,0:T(8,128)(2,1)} %get-tuple-element.47), channel_id=1, source_target_pairs={{0,4},{2,6},{4,0},{6,2},{1,5},{3,7},{5,1},{7,3},{8,12},{10,14},{12... | collective-permute-start | bytes 786440 | tf_op jit(solution)/shard_map/ppermute | solution.py:334
  44.0 17.8 %collective-permute-start.13 = (bf16[64,16,128]{2,1,0:T(8,128)(2,1)}, bf16[64,16,128]{2,1,0:T(8,128)(2,1)}, u32[]{:S(2)}, u32[]{:S(2)}) collective-permute-start(bf16[64,16,128]{2,1,0:T(8,128)(2,1)} %get-tuple-element.48), channel_id=1, source_target_pairs={{0,6},{2,0},{4,2},{6,4},{1,7},{3,1},{5,3},{7,5},{8,14},{10,8},{12,... | collective-permute-start | bytes 786440 | tf_op jit(solution)/shard_map/ppermute | solution.py:334
  46.2 0.9 %copy-start.4 = (f32[3,128,128]{2,1,0:T(8,128)S(1)}, f32[3,128,128]{2,1,0:T(8,128)}, u32[]{:S(2)}) copy-start(f32[3,128,128]{2,1,0:T(8,128)} %copy-done.3) | copy-start | bytes 589828
  47.1 0.9 %copy-start.6 = (f32[256,128]{1,0:T(8,128)S(1)}, f32[256,128]{1,0:T(8,128)}, u32[]{:S(2)}) copy-start(f32[256,128]{1,0:T(8,128)} %copy-done.5) | copy-start | bytes 393220
  50.3 11.5 %copy-start.9 = (bf16[32,16,128]{2,1,0:T(8,128)(2,1)S(1)}, bf16[32,16,128]{2,1,0:T(8,128)(2,1)}, u32[]{:S(2)}) copy-start(bf16[32,16,128]{2,1,0:T(8,128)(2,1)} %copy-done.8) | copy-start | bytes 393220
  64.0 6.2 %collective-permute-start.14 = (bf16[32,16,128]{2,1,0:T(8,128)(2,1)S(1)}, bf16[32,16,128]{2,1,0:T(8,128)(2,1)S(1)}, u32[]{:S(2)}, u32[]{:S(2)}) collective-permute-start(bf16[32,16,128]{2,1,0:T(8,128)(2,1)S(1)} %get-tuple-element.50), channel_id=1, source_target_pairs={{0,6},{1,7},{2,0},{3,1},{4,2},{5,3},{6,4},{7,5},{8,14},{9,15},{10,... | collective-permute-start | bytes 393224 | tf_op jit(solution)/shard_map/ppermute | solution.py:359
  64.1 9.0 %collective-permute-start.15 = (bf16[32,16,128]{2,1,0:T(8,128)(2,1)S(1)}, bf16[32,16,128]{2,1,0:T(8,128)(2,1)S(1)}, u32[]{:S(2)}, u32[]{:S(2)}) collective-permute-start(bf16[32,16,128]{2,1,0:T(8,128)(2,1)S(1)} %get-tuple-element.51), channel_id=1, source_target_pairs={{0,4},{1,5},{2,6},{3,7},{4,0},{5,1},{6,2},{7,3},{8,12},{9,13},{10,... | collective-permute-start | bytes 393224 | tf_op jit(solution)/shard_map/ppermute | solution.py:359
  65.3 8.9 %collective-permute-start.16 = (bf16[32,16,128]{2,1,0:T(8,128)(2,1)S(1)}, bf16[32,16,128]{2,1,0:T(8,128)(2,1)S(1)}, u32[]{:S(2)}, u32[]{:S(2)}) collective-permute-start(bf16[32,16,128]{2,1,0:T(8,128)(2,1)S(1)} %get-tuple-element.52), channel_id=1, source_target_pairs={{0,2},{1,3},{2,4},{3,5},{4,6},{5,7},{6,0},{7,1},{8,10},{9,11},{10,... | collective-permute-start | bytes 393224 | tf_op jit(solution)/shard_map/ppermute | solution.py:359
  65.5 8.6 %collective-permute-start.17 = (bf16[32,16,128]{2,1,0:T(8,128)(2,1)S(1)}, bf16[32,16,128]{2,1,0:T(8,128)(2,1)S(1)}, u32[]{:S(2)}, u32[]{:S(2)}) collective-permute-start(bf16[32,16,128]{2,1,0:T(8,128)(2,1)S(1)} %get-tuple-element.53), channel_id=1, source_target_pairs={{0,1},{1,0},{2,3},{3,2},{4,5},{5,4},{6,7},{7,6},{8,9},{9,8},{10,11... | collective-permute-start | bytes 393224 | tf_op jit(solution)/shard_map/ppermute | solution.py:359
  68.7 6.9 %collective-permute-start.18 = (bf16[32,16,128]{2,1,0:T(8,128)(2,1)S(1)}, bf16[32,16,128]{2,1,0:T(8,128)(2,1)S(1)}, u32[]{:S(2)}, u32[]{:S(2)}) collective-permute-start(bf16[32,16,128]{2,1,0:T(8,128)(2,1)S(1)} %get-tuple-element.54), channel_id=1, source_target_pairs={{0,7},{1,6},{2,1},{3,0},{4,3},{5,2},{6,5},{7,4},{8,15},{9,14},{10,... | collective-permute-start | bytes 393224 | tf_op jit(solution)/shard_map/ppermute | solution.py:359
  70.2 7.1 %collective-permute-start.19 = (bf16[32,16,128]{2,1,0:T(8,128)(2,1)S(1)}, bf16[32,16,128]{2,1,0:T(8,128)(2,1)S(1)}, u32[]{:S(2)}, u32[]{:S(2)}) collective-permute-start(bf16[32,16,128]{2,1,0:T(8,128)(2,1)S(1)} %get-tuple-element.55), channel_id=1, source_target_pairs={{0,5},{1,4},{2,7},{3,6},{4,1},{5,0},{6,3},{7,2},{8,13},{9,12},{10,... | collective-permute-start | bytes 393224 | tf_op jit(solution)/shard_map/ppermute | solution.py:359
  73.1 7.4 %collective-permute-start.20 = (bf16[32,16,128]{2,1,0:T(8,128)(2,1)S(1)}, bf16[32,16,128]{2,1,0:T(8,128)(2,1)S(1)}, u32[]{:S(2)}, u32[]{:S(2)}) collective-permute-start(bf16[32,16,128]{2,1,0:T(8,128)(2,1)S(1)} %get-tuple-element.56), channel_id=1, source_target_pairs={{0,3},{1,2},{2,5},{3,4},{4,7},{5,6},{6,1},{7,0},{8,11},{9,10},{10,... | collective-permute-start | bytes 393224 | tf_op jit(solution)/shard_map/ppermute | solution.py:359
  (1 other events, 0.6 us)

commit v2 on v1

--- a/solution.py
+++ b/solution.py
@@ -57,85 +57,51 @@
             both[n + i] = given[n * d + i]
 
 
-def window_kernel(info, sg, left, right, *outs):
-    half = left.shape[0]
-    z = info[0]
-    for d, w in enumerate(outs):
-        zz = (z + d) % 4
-
-        @pl.when(zz < 2)
+def pick_kernel(info, left, right, *outs):
+    for d, end in enumerate(outs):
+        low = (info[0] + d) % 4 < 2
+
+        @pl.when(low)
         def _():
-            for i in range(16):
-                w[i] = left[16 * zz + i]
-            for j in range(4):
-                src = 16 * zz + 16 * (j + 1) - half
-
-                @pl.when(src < 0)
-                def _():
-                    for i in range(16):
-                        w[16 * (j + 1) + i] = left[src + half + i]
-
-                @pl.when(src >= 0)
-                def _():
-                    for i in range(16):
-                        w[16 * (j + 1) + i] = sg[src + i]
-
-        @pl.when(zz >= 2)
+            for i in range(left.shape[0]):
+                end[i] = left[i]
+
+        @pl.when(jnp.logical_not(low))
         def _():
-            for j in range(5):
-                src = 16 * zz + 16 * j - half
-
-                @pl.when(src < 2 * half)
-                def _():
-                    for i in range(16):
-                        w[16 * j + i] = sg[src + i]
-
-                @pl.when(src >= 2 * half)
-                def _():
-                    for i in range(16):
-                        w[16 * j + i] = right[src - 2 * half + i]
-
-
-def obs_kernel(info, pix, spread, y, active, w2, side):
+            for i in range(left.shape[0]):
+                end[i] = right[i]
+
+
+def cell_kernel(info, pix, spread, y, active, nbr, out, near, own_nbr, w2):
+    groups = pix.shape[0] // PACK
     half = pix.shape[0] // 2
     counts = jnp.concatenate([active[...]] * 4, axis=0).astype(F32).T
     slot = lane_id(half).astype(F32)
     for h in range(2):
         rows = pl.ds(half * h, half)
         w2[rows, :] = jnp.where(slot < counts[:, h : h + 1], 1.0 / spread[rows, :], 0.0)
-    rows = pl.ds(pl.multiple_of(jnp.where(info[0] < 2, half, 0), half), half)
-    side[0] = pix[rows, :].astype(F32)
-    side[1] = w2[rows, :]
-    side[2] = y[rows, :]
-
-
-def cell_kernel(info, pix, w2, y, side, nbr, out, near, own_nbr):
-    groups = pix.shape[0] // PACK
-
-    def sums(pt, wt, yt):
-        yt = yt * wt
+
+    def packed(ref, p):
+        parts = [ref[pl.ds(2 * p + h, groups, stride=PACK), :] for h in range(2)]
+        return jnp.concatenate(parts, axis=0).astype(F32).T
+
+    cols = [[], []]
+    for p in range(2):
+        pt = packed(pix, p)
+        wt = packed(w2, p)
+        yt = packed(y, p) * wt
         d, e = [], []
         for c in range(32):
             hit = pt == float(c)
             d.append(jnp.sum(jnp.where(hit, wt, 0.0), axis=0, keepdims=True))
             e.append(jnp.sum(jnp.where(hit, yt, 0.0), axis=0, keepdims=True))
-        return jnp.concatenate(d, axis=0), jnp.concatenate(e, axis=0)
-
-    def packed(ref, n, qs):
-        parts = [ref[pl.ds(q, n, stride=PACK), :] for q in qs]
-        return jnp.concatenate(parts, axis=0).astype(F32).T
-
-    cols = [[], []]
-    for p in range(2):
-        qs = (2 * p, 2 * p + 1)
-        for i, block in enumerate(sums(*[packed(r, groups, qs) for r in (pix, w2, y)])):
+        for i, rows in enumerate((d, e)):
+            block = jnp.concatenate(rows, axis=0)
             cols[i] += [block, pltpu.roll(block, 64, 1)]
+    at = pl.multiple_of(jnp.where(info[0] < 2, 32, 0), 32)
     for i in range(2):
         out[i] = jnp.concatenate(cols[i], axis=0).T[:groups]
-    some = sums(*[packed(side.at[i], groups // 2, range(PACK)) for i in range(3)])
-    for i, block in enumerate(some):
-        turned = [block] + [pltpu.roll(block, 128 - 32 * q, 1) for q in range(1, PACK)]
-        near[i] = jnp.concatenate(turned, axis=0).T[: groups // 2]
+        near[i] = out[i, pl.ds(at, 32), :]
     own_nbr[...] = nbr[pl.ds(pl.multiple_of(64 * info[0] + 32 * info[1], 32), 32), :]
 
 
@@ -156,7 +122,7 @@
 
 
 def solve_kernel(info, nbr, *refs):
-    parts, (de, dn, out, gt, lt, ks) = refs[:8], refs[8:]
+    own, ends, (de, dn, out, gt, lt, ks) = refs[:8], refs[8:16], refs[16:]
     z, k, first, total = info[0], info[1], info[2], info[3]
     reach = 128
     start = 16 * z - 32 + 8 * k
@@ -168,8 +134,8 @@
     own_to = jnp.where(low, -start, 0)
     mine = lax.broadcasted_iota(jnp.int32, (8, 128), 0) == (lane_id(8) >> 5)
 
-    def center(table, b, g):
-        x = jnp.concatenate([r[8 * k + g] for r in parts], axis=0).astype(F32)
+    def center(src, table, b, g):
+        x = jnp.concatenate([r[b] for r in src], axis=0).astype(F32)
         mean = jnp.sum(x, axis=0, keepdims=True) * (1.0 / 128.0)
         d = table[0, pl.ds(b, 1), :]
         e = table[1, pl.ds(b, 1), :] - d * mean
@@ -183,12 +149,12 @@
 
     def own_eight(j, carry):
         for i in range(8):
-            center(de, own_at + 8 * j + i, own_to + 8 * j + i)
+            center(own, de, own_at + 8 * j + i, own_to + 8 * j + i)
         return carry
 
     def end_eight(j, carry):
         for i in range(8):
-            center(dn, end_at + 8 * j + i, end_to + 8 * j + i)
+            center(ends, dn, end_at + 8 * j + i, end_to + 8 * j + i)
         return carry
 
     lax.fori_loop(0, (gt.shape[0] - n_end) // 8, own_eight, 0)
@@ -378,37 +344,30 @@
     right = to_cells(sg[:half], -1)
     keep, give = rest[:4], rest[4]
     given = to_core(give)
-    windows = call(
-        window_kernel,
-        1,
-        (info, sg, left, right),
-        (shape(80),) * 4,
-    )
-    own = [windows[0]] + [to_z(windows[d], d) for d in (1, 2, 3)]
+    ends = list(call(pick_kernel, 1, (info, left, right), (shape(half),) * 4))
+    own = [sg] + [to_z(sg, d) for d in (1, 2, 3)]
+    for d in (1, 2, 3):
+        ends[d] = to_z(ends[d], d)
     both = call(both_kernel, 0, (*keep[1:], given), (shape(tiles // 4),) * 3)
     state = [to_z(both[d - 1], d) for d in (1, 2, 3)]
-    w2, side = call(
-        obs_kernel,
-        1,
-        (info, pixel, spread, figures, active.reshape(2, tiles // 2)),
-        (jax.ShapeDtypeStruct((tiles, 128), F32), jax.ShapeDtypeStruct((3, tiles // 2, 128), F32)),
-    )
-    side = to_side(side, 0)
     de, near, own_nbr = call(
         cell_kernel,
         1,
-        (info, pixel, w2, figures, side, nbr),
+        (info, pixel, spread, figures, active.reshape(2, tiles // 2), nbr),
         (
             jax.ShapeDtypeStruct((2, groups, 128), F32),
             jax.ShapeDtypeStruct((2, half, 128), F32),
             jax.ShapeDtypeStruct((32, 4), jnp.int32),
         ),
-    )
+        [pltpu.VMEM((tiles, 128), F32)],
+    )
+    dn = to_side(near, 0)
     own += [to_core(r) for r in own]
+    ends += [to_core(r) for r in ends]
     transform = call(
         solve_kernel,
         2,
-        (info, own_nbr, *own, de, near),
+        (info, own_nbr, *own, *ends, de, dn),
         jax.ShapeDtypeStruct((32, 128, 128), BF16),
         [
             pltpu.VMEM((72, 128, 128), BF16),

time: 82.5 us -> 82.7 us (level)
  starting transfers between devices: 33.8 us -> 37.8 us
  Pallas kernels: 21.3 us -> 18.4 us
  local copies, waits for them, and re-layouts: 4.52 us -> 2.05 us
  waiting for transfers between devices: 22.4 us -> 24 us
    ppermute x6 -> x9, waiting for transfers between devices: 9.28 us -> 14.4 us  [to_z(): return lax.ppermute(x, 'z', [(i, (i + by) % 4) for i in range(4)])]
    ppermute x1, waiting for transfers between devices: 3.75 us -> 0.01 us  [to_side(): return lax.ppermute(x, ('cells', 'z', 'k'), pairs)]
    pallas_call x8 -> x7, Pallas kernels: 21.3 us -> 18.4 us  [call(): pl.pallas_call(kernel, in_specs=[smem()] * n_smem + list(specs or [vmem()...]
    unnamed x25 -> x13, local copies, waits for them, and re-layouts: 4.5 us -> 2.03 us
    ppermute x7, starting transfers between devices: 10.1 us -> 12.4 us  [home(): return lax.ppermute(x, MEM, pairs)]
    ppermute x5 -> x9, starting transfers between devices: 5.81 us -> 7.8 us  [to_core(): return lax.ppermute(x, 'k', [(0, 1), (1, 0)])]
    ppermute x6 -> x9, starting transfers between devices: 12 us -> 11.8 us  [to_z(): return lax.ppermute(x, 'z', [(i, (i + by) % 4) for i in range(4)])]
  transfers between devices with their start and end apart: 21 -> 28, of which waited for: 8 -> 10; matrix products, arithmetic and copies ran while one was open for 0% -> 0% of each run, Pallas kernels for 19% -> 17%
where the time goes in v2:
time: 82.7 us; the launch traced here: 82.5 us
  starting transfers between devices  37.8 us (46%)
  waiting for transfers between devices  24 us (29%)
  Pallas kernels  18.4 us (22%)
  local copies, waits for them, and re-layouts  2.05 us (2%)
    pallas_call x7, Pallas kernels, call(): pl.pallas_call(kernel, in_specs=[smem()] * n_smem + list(specs or [vmem()...  18.4 us
    ppermute x9, waiting for transfers between devices, to_z(): return lax.ppermute(x, 'z', [(i, (i + by) % 4) for i in range(4)])  14.4 us
    ppermute x7, starting transfers between devices, home(): return lax.ppermute(x, MEM, pairs)  12.4 us
    ppermute x9, starting transfers between devices, to_z(): return lax.ppermute(x, 'z', [(i, (i + by) % 4) for i in range(4)])  11.8 us
    ppermute x9, starting transfers between devices, to_core(): return lax.ppermute(x, 'k', [(0, 1), (1, 0)])  7.8 us
    ppermute x7, waiting for transfers between devices, home(): return lax.ppermute(x, MEM, pairs)  6.14 us
    ppermute x2, starting transfers between devices, to_cells(): return lax.ppermute(x, 'cells', [(i, (i + by) % n) for i in range(n)])  5.82 us
    ppermute x2, waiting for transfers between devices, to_cells(): return lax.ppermute(x, 'cells', [(i, (i + by) % n) for i in range(n)])  3.39 us
  transfers between devices with their start and end apart: 28, of which 10 were waited for; matrix products, arithmetic and copies ran while one was open for 0% of the time, Pallas kernels for 17%

profile of v2, /device:TPU:1, one launch (start us, length us, event | category | flops | bytes accessed | tf_op | source)
XLA Modules:
  0.0 82.5 jit_solution(16148075609153710250)
XLA Ops:
  0.1 1.2 %copy-done = bf16[16,256,128]{2,1,0:T(8,128)(2,1)S(1)} copy-done((bf16[16,256,128]{2,1,0:T(8,128)(2,1)S(1)}, bf16[16,256,128]{2,1,0:T(8,128)(2,1)}, u32[]{:S(2)}) %copy-start) | copy-done | bytes 1048600
  1.3 1.1 %shard_map.65 = (bf16[64,16,128]{2,1,0:T(8,128)(2,1)S(1)}, bf16[32,16,128]{2,1,0:T(8,128)(2,1)S(1)}, bf16[32,16,128]{2,1,0:T(8,128)(2,1)S(1)}, bf16[32,16,128]{2...) custom-call(s32[4]{0:T(128)S(1)} %pad_add_fusion.info, ...), custom_call_target="tpu_custom_call" | custom-call | tf_op jit(solution)/shard_map/pallas_call | solution.py:289
  2.5 5.8 %collective-permute-start.8 = (bf16[32,16,128]{2,1,0:T(8,128)(2,1)S(1)}, bf16[32,16,128]{2,1,0:T(8,128)(2,1)S(1)}, u32[]{:S(2)}, u32[]{:S(2)}) collective-permute-start(bf16[32,16,128]{2,1,0:T(8,128)(2,1)S(1)} %get-tuple-element.53), channel_id=1, source_target_pairs={{0,120},{8,0},{16,8},{24,16},{32,24},{40,32},{48,40},{56,48},{64,5... | collective-permute-start | bytes 393224 | tf_op jit(solution)/shard_map/ppermute | solution.py:309
  8.3 1.0 %collective-permute-start.17 = (bf16[128,16,128]{2,1,0:T(8,128)(2,1)S(1)}, bf16[128,16,128]{2,1,0:T(8,128)(2,1)S(1)}, u32[]{:S(2)}, u32[]{:S(2)}) collective-permute-start(bf16[128,16,128]{2,1,0:T(8,128)(2,1)S(1)} %get-tuple-element.38), channel_id=1, source_target_pairs={{0,1},{1,0},{2,3},{3,2},{4,5},{5,4},{6,7},{7,6},{8,9},{9,8},{10,11... | collective-permute-start | bytes 1572872 | tf_op jit(solution)/shard_map/ppermute | solution.py:304
  10.1 1.9 %shard_map.64 = (f32[2,64,128]{2,1,0:T(8,128)S(1)}, f32[2,32,128]{2,1,0:T(8,128)S(1)}, s32[32,4]{1,0:T(8,128)S(1)}) custom-call(s32[4]{0:T(128)S(1)} %pad_add_fusion.info, s32[256,128]{1,0:T(8,128)S(1)} %copy-done.1, f32[256,128]{1,0:T(8,128)S(1)} %copy-done.2, f32[256,128]{1,0:T(8,128)S(1)} %copy-done.3, s32[2,128]{1,0:T(2,128)S(1)} %bitcast.4, ...), custom_call_target="tpu_custom_call" | custom-call | tf_op jit(solution)/shard_map/pallas_call | solution.py:289
  12.1 3.4 %collective-permute-done.7.left = bf16[32,16,128]{2,1,0:T(8,128)(2,1)S(1)} collective-permute-done((bf16[32,16,128]{2,1,0:T(8,128)(2,1)S(1)}, bf16[32,16,128]{2,1,0:T(8,128)(2,1)S(1)}, u32[]{:S(2)}, u32[]{:S(2)}) %collective-permute-start.7) | collective-permute-done | bytes 131104 | tf_op jit(solution)/shard_map/ppermute | solution.py:309
  16.1 1.7 %collective-permute-start.9 = (bf16[32,16,128]{2,1,0:T(8,128)(2,1)S(1)}, bf16[32,16,128]{2,1,0:T(8,128)(2,1)S(1)}, u32[]{:S(2)}, u32[]{:S(2)}) collective-permute-start(bf16[32,16,128]{2,1,0:T(8,128)(2,1)S(1)} %get-tuple-element.32), channel_id=1, source_target_pairs={{0,2},{2,4},{4,6},{6,0},{1,3},{3,5},{5,7},{7,1},{8,10},{10,12},{12... | collective-permute-start | bytes 393224 | tf_op jit(solution)/shard_map/ppermute | solution.py:300
  17.8 5.0 %collective-permute-start.10 = (bf16[32,16,128]{2,1,0:T(8,128)(2,1)S(1)}, bf16[32,16,128]{2,1,0:T(8,128)(2,1)S(1)}, u32[]{:S(2)}, u32[]{:S(2)}) collective-permute-start(bf16[32,16,128]{2,1,0:T(8,128)(2,1)S(1)} %get-tuple-element.33), channel_id=1, source_target_pairs={{0,4},{2,6},{4,0},{6,2},{1,5},{3,7},{5,1},{7,3},{8,12},{10,14},{12... | collective-permute-start | bytes 393224 | tf_op jit(solution)/shard_map/ppermute | solution.py:300
  22.8 0.7 collective-permute-start.11
  23.5 1.5 %collective-permute-done.9.refs_9_ = bf16[32,16,128]{2,1,0:T(8,128)(2,1)S(1)} collective-permute-done((bf16[32,16,128]{2,1,0:T(8,128)(2,1)S(1)}, bf16[32,16,128]{2,1,0:T(8,128)(2,1)S(1)}, u32[]{:S(2)}, u32[]{:S(2)}) %collective-permute-start.9) | collective-permute-done | bytes 131104 | tf_op jit(solution)/shard_map/ppermute | solution.py:300
  25.0 1.0 %collective-permute-start.12 = (bf16[32,16,128]{2,1,0:T(8,128)(2,1)S(1)}, bf16[32,16,128]{2,1,0:T(8,128)(2,1)S(1)}, u32[]{:S(2)}, u32[]{:S(2)}) collective-permute-start(bf16[32,16,128]{2,1,0:T(8,128)(2,1)S(1)} %get-tuple-element.31.refs_8_), channel_id=1, source_target_pairs={{0,1},{1,0},{2,3},{3,2},{4,5},{5,4},{6,7},{7,6},{8,9},{9,8},{10,11... | collective-permute-start | bytes 393224 | tf_op jit(solution)/shard_map/ppermute | solution.py:304
  26.0 2.7 %collective-permute-done.10.refs_10_ = bf16[32,16,128]{2,1,0:T(8,128)(2,1)S(1)} collective-permute-done((bf16[32,16,128]{2,1,0:T(8,128)(2,1)S(1)}, bf16[32,16,128]{2,1,0:T(8,128)(2,1)S(1)}, u32[]{:S(2)}, u32[]{:S(2)}) %collective-permute-start.10) | collective-permute-done | bytes 131104 | tf_op jit(solution)/shard_map/ppermute | solution.py:300
  28.7 1.3 %collective-permute-start.3 = (bf16[64,16,128]{2,1,0:T(8,128)(2,1)S(1)}, bf16[64,16,128]{2,1,0:T(8,128)(2,1)S(1)}, u32[]{:S(2)}, u32[]{:S(2)}) collective-permute-start(bf16[64,16,128]{2,1,0:T(8,128)(2,1)S(1)} %get-tuple-element.30.refs_0_), channel_id=1, source_target_pairs={{0,1},{1,0},{2,3},{3,2},{4,5},{5,4},{6,7},{7,6},{8,9},{9,8},{10,11... | collective-permute-start | bytes 786440 | tf_op jit(solution)/shard_map/ppermute | solution.py:304
  30.4 1.1 %collective-permute-start = (bf16[64,16,128]{2,1,0:T(8,128)(2,1)S(1)}, bf16[64,16,128]{2,1,0:T(8,128)(2,1)S(1)}, u32[]{:S(2)}, u32[]{:S(2)}) collective-permute-start(bf16[64,16,128]{2,1,0:T(8,128)(2,1)S(1)} %get-tuple-element.30.refs_0_), channel_id=1, source_target_pairs={{0,2},{2,4},{4,6},{6,0},{1,3},{3,5},{5,7},{7,1},{8,10},{10,12},{12... | collective-permute-start | bytes 786440 | tf_op jit(solution)/shard_map/ppermute | solution.py:300
  31.6 2.3 %collective-permute-done.2.refs_3_ = bf16[64,16,128]{2,1,0:T(8,128)(2,1)S(1)} collective-permute-done((bf16[64,16,128]{2,1,0:T(8,128)(2,1)S(1)}, bf16[64,16,128]{2,1,0:T(8,128)(2,1)S(1)}, u32[]{:S(2)}, u32[]{:S(2)}) %collective-permute-start.2) | collective-permute-done | bytes 262176 | tf_op jit(solution)/shard_map/ppermute | solution.py:300
  33.9 2.1 %collective-permute-start.6 = (bf16[64,16,128]{2,1,0:T(8,128)(2,1)S(1)}, bf16[64,16,128]{2,1,0:T(8,128)(2,1)S(1)}, u32[]{:S(2)}, u32[]{:S(2)}) collective-permute-start(bf16[64,16,128]{2,1,0:T(8,128)(2,1)S(1)} %collective-permute-done.2.refs_3_), channel_id=1, source_target_pairs={{0,1},{1,0},{2,3},{3,2},{4,5},{5,4},{6,7},{7,6},{8,9},{9,8},{10,11... | collective-permute-start | bytes 786440 | tf_op jit(solution)/shard_map/ppermute | solution.py:304
  36.0 3.2 %collective-permute-done.1.refs_2_ = bf16[64,16,128]{2,1,0:T(8,128)(2,1)S(1)} collective-permute-done((bf16[64,16,128]{2,1,0:T(8,128)(2,1)S(1)}, bf16[64,16,128]{2,1,0:T(8,128)(2,1)S(1)}, u32[]{:S(2)}, u32[]{:S(2)}) %collective-permute-start.1) | collective-permute-done | bytes 262176 | tf_op jit(solution)/shard_map/ppermute | solution.py:300
  39.1 1.9 %collective-permute-start.14 = (bf16[32,16,128]{2,1,0:T(8,128)(2,1)S(1)}, bf16[32,16,128]{2,1,0:T(8,128)(2,1)S(1)}, u32[]{:S(2)}, u32[]{:S(2)}) collective-permute-start(bf16[32,16,128]{2,1,0:T(8,128)(2,1)S(1)} %collective-permute-done.10.refs_10_), channel_id=1, source_target_pairs={{0,1},{1,0},{2,3},{3,2},{4,5},{5,4},{6,7},{7,6},{8,9},{9,8},{10,11... | collective-permute-start | bytes 393224 | tf_op jit(solution)/shard_map/ppermute | solution.py:304
  41.1 4.2 %collective-permute-done.refs_1_ = bf16[64,16,128]{2,1,0:T(8,128)(2,1)S(1)} collective-permute-done((bf16[64,16,128]{2,1,0:T(8,128)(2,1)S(1)}, bf16[64,16,128]{2,1,0:T(8,128)(2,1)S(1)}, u32[]{:S(2)}, u32[]{:S(2)}) %collective-permute-start) | collective-permute-done | bytes 262176 | tf_op jit(solution)/shard_map/ppermute | solution.py:300
  46.0 1.5 %collective-permute-start.19 = (bf16[64,16,128]{2,1,0:T(8,128)(2,1)S(1)}, bf16[64,16,128]{2,1,0:T(8,128)(2,1)S(1)}, u32[]{:S(2)}, u32[]{:S(2)}) collective-permute-start(bf16[64,16,128]{2,1,0:T(8,128)(2,1)S(1)} %get-tuple-element.43), channel_id=1, source_target_pairs={{0,4},{2,6},{4,0},{6,2},{1,5},{3,7},{5,1},{7,3},{8,12},{10,14},{12... | collective-permute-start | bytes 786440 | tf_op jit(solution)/shard_map/ppermute | solution.py:300
  47.5 1.2 %collective-permute-start.20 = (bf16[64,16,128]{2,1,0:T(8,128)(2,1)S(1)}, bf16[64,16,128]{2,1,0:T(8,128)(2,1)S(1)}, u32[]{:S(2)}, u32[]{:S(2)}) collective-permute-start(bf16[64,16,128]{2,1,0:T(8,128)(2,1)S(1)} %get-tuple-element.44), channel_id=1, source_target_pairs={{0,6},{2,0},{4,2},{6,4},{1,7},{3,1},{5,3},{7,5},{8,14},{10,8},{12,... | collective-permute-start | bytes 786440 | tf_op jit(solution)/shard_map/ppermute | solution.py:300
  48.7 11.4 %shard_map.67.tr = bf16[32,128,128]{2,1,0:T(8,128)(2,1)S(1)} custom-call(s32[4]{0:T(128)S(1)} %pad_add_fusion.info, s32[32,4]{1,0:T(8,128)S(1)} %get-tuple-element.29.nbr, bf16[64,16,128]{2,1,0:T(8,128)(2,1)S(1)} %get-tuple-element.30.refs_0_, bf16[64,16,128]{2,1,0:T(8,128)(2,1)S(1)} %collective-permute-done.refs_1_, ...), custom_call_target="tpu_custom_call" | custom-call | tf_op jit(solution)/shard_map/pallas_call | solution.py:289
  60.6 1.6 %shard_map.69 = (bf16[32,16,128]{2,1,0:T(8,128)(2,1)S(1)}, bf16[32,16,128]{2,1,0:T(8,128)(2,1)S(1)}, bf16[32,16,128]{2,1,0:T(8,128)(2,1)S(1)}, bf16[32,16,128]{2...) custom-call(s32[4]{0:T(128)S(1)} %pad_add_fusion.info, ...), custom_call_target="tpu_custom_call" | custom-call | tf_op jit(solution)/shard_map/pallas_call | solution.py:289
  62.2 3.0 %collective-permute-start.21 = (bf16[32,16,128]{2,1,0:T(8,128)(2,1)S(1)}, bf16[32,16,128]{2,1,0:T(8,128)(2,1)S(1)}, u32[]{:S(2)}, u32[]{:S(2)}) collective-permute-start(bf16[32,16,128]{2,1,0:T(8,128)(2,1)S(1)} %get-tuple-element.46), channel_id=1, source_target_pairs={{0,6},{1,7},{2,0},{3,1},{4,2},{5,3},{6,4},{7,5},{8,14},{9,15},{10,... | collective-permute-start | bytes 393224 | tf_op jit(solution)/shard_map/ppermute | solution.py:325
  65.2 0.7 collective-permute-start.23
  65.9 1.3 %collective-permute-start.24 = (bf16[32,16,128]{2,1,0:T(8,128)(2,1)S(1)}, bf16[32,16,128]{2,1,0:T(8,128)(2,1)S(1)}, u32[]{:S(2)}, u32[]{:S(2)}) collective-permute-start(bf16[32,16,128]{2,1,0:T(8,128)(2,1)S(1)} %get-tuple-element.49), channel_id=1, source_target_pairs={{0,1},{1,0},{2,3},{3,2},{4,5},{5,4},{6,7},{7,6},{8,9},{9,8},{10,11... | collective-permute-start | bytes 393224 | tf_op jit(solution)/shard_map/ppermute | solution.py:325
  67.1 1.9 %collective-permute-start.25 = (bf16[32,16,128]{2,1,0:T(8,128)(2,1)S(1)}, bf16[32,16,128]{2,1,0:T(8,128)(2,1)S(1)}, u32[]{:S(2)}, u32[]{:S(2)}) collective-permute-start(bf16[32,16,128]{2,1,0:T(8,128)(2,1)S(1)} %get-tuple-element.50), channel_id=1, source_target_pairs={{0,7},{1,6},{2,1},{3,0},{4,3},{5,2},{6,5},{7,4},{8,15},{9,14},{10,... | collective-permute-start | bytes 393224 | tf_op jit(solution)/shard_map/ppermute | solution.py:325
  69.0 2.6 %collective-permute-start.26 = (bf16[32,16,128]{2,1,0:T(8,128)(2,1)S(1)}, bf16[32,16,128]{2,1,0:T(8,128)(2,1)S(1)}, u32[]{:S(2)}, u32[]{:S(2)}) collective-permute-start(bf16[32,16,128]{2,1,0:T(8,128)(2,1)S(1)} %get-tuple-element.51), channel_id=1, source_target_pairs={{0,5},{1,4},{2,7},{3,6},{4,1},{5,0},{6,3},{7,2},{8,13},{9,12},{10,... | collective-permute-start | bytes 393224 | tf_op jit(solution)/shard_map/ppermute | solution.py:325
  71.6 3.0 %collective-permute-start.27 = (bf16[32,16,128]{2,1,0:T(8,128)(2,1)S(1)}, bf16[32,16,128]{2,1,0:T(8,128)(2,1)S(1)}, u32[]{:S(2)}, u32[]{:S(2)}) collective-permute-start(bf16[32,16,128]{2,1,0:T(8,128)(2,1)S(1)} %get-tuple-element.52), channel_id=1, source_target_pairs={{0,3},{1,2},{2,5},{3,4},{4,7},{5,6},{6,1},{7,0},{8,11},{9,10},{10,... | collective-permute-start | bytes 393224 | tf_op jit(solution)/shard_map/ppermute | solution.py:325
  74.6 1.9 %collective-permute-done.26.refs_6_ = bf16[32,16,128]{2,1,0:T(8,128)(2,1)S(1)} collective-permute-done((bf16[32,16,128]{2,1,0:T(8,128)(2,1)S(1)}, bf16[32,16,128]{2,1,0:T(8,128)(2,1)S(1)}, u32[]{:S(2)}, u32[]{:S(2)}) %collective-permute-start.26) | collective-permute-done | bytes 131104 | tf_op jit(solution)/shard_map/ppermute | solution.py:325
  76.5 4.2 %collective-permute-done.27.refs_7_ = bf16[32,16,128]{2,1,0:T(8,128)(2,1)S(1)} collective-permute-done((bf16[32,16,128]{2,1,0:T(8,128)(2,1)S(1)}, bf16[32,16,128]{2,1,0:T(8,128)(2,1)S(1)}, u32[]{:S(2)}, u32[]{:S(2)}) %collective-permute-start.27) | collective-permute-done | bytes 131104 | tf_op jit(solution)/shard_map/ppermute | solution.py:325
  80.7 1.8 %shard_map.70 = bf16[16,256,128]{2,1,0:T(8,128)(2,1)} custom-call(s32[4]{0:T(128)S(1)} %pad_add_fusion.info, bf16[32,16,128]{2,1,0:T(8,128)(2,1)S(1)} %get-tuple-element.45.refs_0_, bf16[32,16,128]{2,1,0:T(8,128)(2,1)S(1)} %collective-permute-done.21.refs_1_, bf16[32,16,128]{2,1,0:T(8,128)(2,1)S(1)} %collective-permute-done.22.refs_2_, ...), custom_call_target="tpu_custom_call" | custom-call | tf_op jit(solution)/shard_map/pallas_call | solution.py:289
  (46 shorter events, 3.2 us)
Async XLA Ops:
  2.4 6.9 %copy-start.5 = (s32[256,4]{0,1:T(4,128)S(1)}, s32[256,4]{0,1:T(4,128)}, u32[]{:S(2)}) copy-start(s32[256,4]{0,1:T(4,128)} %param.11) | copy-start | bytes 12292
  2.4 7.0 %copy-start.2 = (f32[256,128]{1,0:T(8,128)S(1)}, f32[256,128]{1,0:T(8,128)}, u32[]{:S(2)}) copy-start(f32[256,128]{1,0:T(8,128)} %spread.1) | copy-start | bytes 393220
  2.4 7.0 %copy-start.3 = (f32[256,128]{1,0:T(8,128)S(1)}, f32[256,128]{1,0:T(8,128)}, u32[]{:S(2)}) copy-start(f32[256,128]{1,0:T(8,128)} %y.1) | copy-start | bytes 393220
  2.5 7.0 %copy-start.1 = (s32[256,128]{1,0:T(8,128)S(1)}, s32[256,128]{1,0:T(8,128)}, u32[]{:S(2)}) copy-start(s32[256,128]{1,0:T(8,128)} %pix.1) | copy-start | bytes 393220
  2.5 9.6 %collective-permute-start.8 = (bf16[32,16,128]{2,1,0:T(8,128)(2,1)S(1)}, bf16[32,16,128]{2,1,0:T(8,128)(2,1)S(1)}, u32[]{:S(2)}, u32[]{:S(2)}) collective-permute-start(bf16[32,16,128]{2,1,0:T(8,128)(2,1)S(1)} %get-tuple-element.53), channel_id=1, source_target_pairs={{0,120},{8,0},{16,8},{24,16},{32,24},{40,32},{48,40},{56,48},{64,5... | collective-permute-start | bytes 393224 | tf_op jit(solution)/shard_map/ppermute | solution.py:309
  8.3 7.1 %collective-permute-start.7 = (bf16[32,16,128]{2,1,0:T(8,128)(2,1)S(1)}, bf16[32,16,128]{2,1,0:T(8,128)(2,1)S(1)}, u32[]{:S(2)}, u32[]{:S(2)}) collective-permute-start(bf16[32,16,128]{2,1,0:T(8,128)(2,1)S(1)} %get-tuple-element.54), channel_id=1, source_target_pairs={{0,8},{8,16},{16,24},{24,32},{32,40},{40,48},{48,56},{56,64},{64,7... | collective-permute-start | bytes 393224 | tf_op jit(solution)/shard_map/ppermute | solution.py:309
  8.3 32.7 %collective-permute-start.17 = (bf16[128,16,128]{2,1,0:T(8,128)(2,1)S(1)}, bf16[128,16,128]{2,1,0:T(8,128)(2,1)S(1)}, u32[]{:S(2)}, u32[]{:S(2)}) collective-permute-start(bf16[128,16,128]{2,1,0:T(8,128)(2,1)S(1)} %get-tuple-element.38), channel_id=1, source_target_pairs={{0,1},{1,0},{2,3},{3,2},{4,5},{5,4},{6,7},{7,6},{8,9},{9,8},{10,11... | collective-permute-start | bytes 1572872 | tf_op jit(solution)/shard_map/ppermute | solution.py:304
  12.0 11.5 %collective-permute-start.16 = (f32[2,32,128]{2,1,0:T(8,128)S(1)}, f32[2,32,128]{2,1,0:T(8,128)S(1)}, u32[]{:S(2)}, u32[]{:S(2)}) collective-permute-start(f32[2,32,128]{2,1,0:T(8,128)S(1)} %get-tuple-element.36), channel_id=1, source_target_pairs={{0,8},{1,9},{2,10},{3,11},{4,124},{5,125},{6,126},{7,127},{8,16},{... | collective-permute-start | bytes 98312 | tf_op jit(solution)/shard_map/ppermute | solution.py:320
  16.1 8.9 %collective-permute-start.9 = (bf16[32,16,128]{2,1,0:T(8,128)(2,1)S(1)}, bf16[32,16,128]{2,1,0:T(8,128)(2,1)S(1)}, u32[]{:S(2)}, u32[]{:S(2)}) collective-permute-start(bf16[32,16,128]{2,1,0:T(8,128)(2,1)S(1)} %get-tuple-element.32), channel_id=1, source_target_pairs={{0,2},{2,4},{4,6},{6,0},{1,3},{3,5},{5,7},{7,1},{8,10},{10,12},{12... | collective-permute-start | bytes 393224 | tf_op jit(solution)/shard_map/ppermute | solution.py:300
  17.8 10.9 %collective-permute-start.10 = (bf16[32,16,128]{2,1,0:T(8,128)(2,1)S(1)}, bf16[32,16,128]{2,1,0:T(8,128)(2,1)S(1)}, u32[]{:S(2)}, u32[]{:S(2)}) collective-permute-start(bf16[32,16,128]{2,1,0:T(8,128)(2,1)S(1)} %get-tuple-element.33), channel_id=1, source_target_pairs={{0,4},{2,6},{4,0},{6,2},{1,5},{3,7},{5,1},{7,3},{8,12},{10,14},{12... | collective-permute-start | bytes 393224 | tf_op jit(solution)/shard_map/ppermute | solution.py:300
  22.8 7.3 %collective-permute-start.11 = (bf16[32,16,128]{2,1,0:T(8,128)(2,1)S(1)}, bf16[32,16,128]{2,1,0:T(8,128)(2,1)S(1)}, u32[]{:S(2)}, u32[]{:S(2)}) collective-permute-start(bf16[32,16,128]{2,1,0:T(8,128)(2,1)S(1)} %get-tuple-element.34), channel_id=1, source_target_pairs={{0,6},{2,0},{4,2},{6,4},{1,7},{3,1},{5,3},{7,5},{8,14},{10,8},{12,... | collective-permute-start | bytes 393224 | tf_op jit(solution)/shard_map/ppermute | solution.py:300
  23.5 10.4 %collective-permute-start.2 = (bf16[64,16,128]{2,1,0:T(8,128)(2,1)S(1)}, bf16[64,16,128]{2,1,0:T(8,128)(2,1)S(1)}, u32[]{:S(2)}, u32[]{:S(2)}) collective-permute-start(bf16[64,16,128]{2,1,0:T(8,128)(2,1)S(1)} %get-tuple-element.30.refs_0_), channel_id=1, source_target_pairs={{0,6},{2,0},{4,2},{6,4},{1,7},{3,1},{5,3},{7,5},{8,14},{10,8},{12,... | collective-permute-start | bytes 786440 | tf_op jit(solution)/shard_map/ppermute | solution.py:300
  25.0 5.4 %collective-permute-start.12 = (bf16[32,16,128]{2,1,0:T(8,128)(2,1)S(1)}, bf16[32,16,128]{2,1,0:T(8,128)(2,1)S(1)}, u32[]{:S(2)}, u32[]{:S(2)}) collective-permute-start(bf16[32,16,128]{2,1,0:T(8,128)(2,1)S(1)} %get-tuple-element.31.refs_8_), channel_id=1, source_target_pairs={{0,1},{1,0},{2,3},{3,2},{4,5},{5,4},{6,7},{7,6},{8,9},{9,8},{10,11... | collective-permute-start | bytes 393224 | tf_op jit(solution)/shard_map/ppermute | solution.py:304
  28.7 7.2 %collective-permute-start.3 = (bf16[64,16,128]{2,1,0:T(8,128)(2,1)S(1)}, bf16[64,16,128]{2,1,0:T(8,128)(2,1)S(1)}, u32[]{:S(2)}, u32[]{:S(2)}) collective-permute-start(bf16[64,16,128]{2,1,0:T(8,128)(2,1)S(1)} %get-tuple-element.30.refs_0_), channel_id=1, source_target_pairs={{0,1},{1,0},{2,3},{3,2},{4,5},{5,4},{6,7},{7,6},{8,9},{9,8},{10,11... | collective-permute-start | bytes 786440 | tf_op jit(solution)/shard_map/ppermute | solution.py:304
  30.0 9.1 %collective-permute-start.1 = (bf16[64,16,128]{2,1,0:T(8,128)(2,1)S(1)}, bf16[64,16,128]{2,1,0:T(8,128)(2,1)S(1)}, u32[]{:S(2)}, u32[]{:S(2)}) collective-permute-start(bf16[64,16,128]{2,1,0:T(8,128)(2,1)S(1)} %get-tuple-element.30.refs_0_), channel_id=1, source_target_pairs={{0,4},{2,6},{4,0},{6,2},{1,5},{3,7},{5,1},{7,3},{8,12},{10,14},{12... | collective-permute-start | bytes 786440 | tf_op jit(solution)/shard_map/ppermute | solution.py:300
  30.4 14.9 %collective-permute-start = (bf16[64,16,128]{2,1,0:T(8,128)(2,1)S(1)}, bf16[64,16,128]{2,1,0:T(8,128)(2,1)S(1)}, u32[]{:S(2)}, u32[]{:S(2)}) collective-permute-start(bf16[64,16,128]{2,1,0:T(8,128)(2,1)S(1)} %get-tuple-element.30.refs_0_), channel_id=1, source_target_pairs={{0,2},{2,4},{4,6},{6,0},{1,3},{3,5},{5,7},{7,1},{8,10},{10,12},{12... | collective-permute-start | bytes 786440 | tf_op jit(solution)/shard_map/ppermute | solution.py:300
  33.9 13.6 %collective-permute-start.6 = (bf16[64,16,128]{2,1,0:T(8,128)(2,1)S(1)}, bf16[64,16,128]{2,1,0:T(8,128)(2,1)S(1)}, u32[]{:S(2)}, u32[]{:S(2)}) collective-permute-start(bf16[64,16,128]{2,1,0:T(8,128)(2,1)S(1)} %collective-permute-done.2.refs_3_), channel_id=1, source_target_pairs={{0,1},{1,0},{2,3},{3,2},{4,5},{5,4},{6,7},{7,6},{8,9},{9,8},{10,11... | collective-permute-start | bytes 786440 | tf_op jit(solution)/shard_map/ppermute | solution.py:304
  35.9 9.9 %collective-permute-start.13 = (bf16[32,16,128]{2,1,0:T(8,128)(2,1)S(1)}, bf16[32,16,128]{2,1,0:T(8,128)(2,1)S(1)}, u32[]{:S(2)}, u32[]{:S(2)}) collective-permute-start(bf16[32,16,128]{2,1,0:T(8,128)(2,1)S(1)} %collective-permute-done.9.refs_9_), channel_id=1, source_target_pairs={{0,1},{1,0},{2,3},{3,2},{4,5},{5,4},{6,7},{7,6},{8,9},{9,8},{10,11... | collective-permute-start | bytes 393224 | tf_op jit(solution)/shard_map/ppermute | solution.py:304
  39.1 6.8 %collective-permute-start.14 = (bf16[32,16,128]{2,1,0:T(8,128)(2,1)S(1)}, bf16[32,16,128]{2,1,0:T(8,128)(2,1)S(1)}, u32[]{:S(2)}, u32[]{:S(2)}) collective-permute-start(bf16[32,16,128]{2,1,0:T(8,128)(2,1)S(1)} %collective-permute-done.10.refs_10_), channel_id=1, source_target_pairs={{0,1},{1,0},{2,3},{3,2},{4,5},{5,4},{6,7},{7,6},{8,9},{9,8},{10,11... | collective-permute-start | bytes 393224 | tf_op jit(solution)/shard_map/ppermute | solution.py:304
  41.1 4.9 %collective-permute-start.15 = (bf16[32,16,128]{2,1,0:T(8,128)(2,1)S(1)}, bf16[32,16,128]{2,1,0:T(8,128)(2,1)S(1)}, u32[]{:S(2)}, u32[]{:S(2)}) collective-permute-start(bf16[32,16,128]{2,1,0:T(8,128)(2,1)S(1)} %collective-permute-done.11.refs_11_), channel_id=1, source_target_pairs={{0,1},{1,0},{2,3},{3,2},{4,5},{5,4},{6,7},{7,6},{8,9},{9,8},{10,11... | collective-permute-start | bytes 393224 | tf_op jit(solution)/shard_map/ppermute | solution.py:304
  45.4 3.3 %collective-permute-start.5 = (bf16[64,16,128]{2,1,0:T(8,128)(2,1)S(1)}, bf16[64,16,128]{2,1,0:T(8,128)(2,1)S(1)}, u32[]{:S(2)}, u32[]{:S(2)}) collective-permute-start(bf16[64,16,128]{2,1,0:T(8,128)(2,1)S(1)} %collective-permute-done.1.refs_2_), channel_id=1, source_target_pairs={{0,1},{1,0},{2,3},{3,2},{4,5},{5,4},{6,7},{7,6},{8,9},{9,8},{10,11... | collective-permute-start | bytes 786440 | tf_op jit(solution)/shard_map/ppermute | solution.py:304
  45.9 2.8 %collective-permute-start.4 = (bf16[64,16,128]{2,1,0:T(8,128)(2,1)S(1)}, bf16[64,16,128]{2,1,0:T(8,128)(2,1)S(1)}, u32[]{:S(2)}, u32[]{:S(2)}) collective-permute-start(bf16[64,16,128]{2,1,0:T(8,128)(2,1)S(1)} %collective-permute-done.refs_1_), channel_id=1, source_target_pairs={{0,1},{1,0},{2,3},{3,2},{4,5},{5,4},{6,7},{7,6},{8,9},{9,8},{10,11... | collective-permute-start | bytes 786440 | tf_op jit(solution)/shard_map/ppermute | solution.py:304
  45.9 14.3 %collective-permute-start.18 = (bf16[64,16,128]{2,1,0:T(8,128)(2,1)S(1)}, bf16[64,16,128]{2,1,0:T(8,128)(2,1)S(1)}, u32[]{:S(2)}, u32[]{:S(2)}) collective-permute-start(bf16[64,16,128]{2,1,0:T(8,128)(2,1)S(1)} %get-tuple-element.42), channel_id=1, source_target_pairs={{0,2},{2,4},{4,6},{6,0},{1,3},{3,5},{5,7},{7,1},{8,10},{10,12},{12... | collective-permute-start | bytes 786440 | tf_op jit(solution)/shard_map/ppermute | solution.py:300
  46.0 14.2 %collective-permute-start.19 = (bf16[64,16,128]{2,1,0:T(8,128)(2,1)S(1)}, bf16[64,16,128]{2,1,0:T(8,128)(2,1)S(1)}, u32[]{:S(2)}, u32[]{:S(2)}) collective-permute-start(bf16[64,16,128]{2,1,0:T(8,128)(2,1)S(1)} %get-tuple-element.43), channel_id=1, source_target_pairs={{0,4},{2,6},{4,0},{6,2},{1,5},{3,7},{5,1},{7,3},{8,12},{10,14},{12... | collective-permute-start | bytes 786440 | tf_op jit(solution)/shard_map/ppermute | solution.py:300
  47.5 13.1 %collective-permute-start.20 = (bf16[64,16,128]{2,1,0:T(8,128)(2,1)S(1)}, bf16[64,16,128]{2,1,0:T(8,128)(2,1)S(1)}, u32[]{:S(2)}, u32[]{:S(2)}) collective-permute-start(bf16[64,16,128]{2,1,0:T(8,128)(2,1)S(1)} %get-tuple-element.44), channel_id=1, source_target_pairs={{0,6},{2,0},{4,2},{6,4},{1,7},{3,1},{5,3},{7,5},{8,14},{10,8},{12,... | collective-permute-start | bytes 786440 | tf_op jit(solution)/shard_map/ppermute | solution.py:300
  62.2 6.9 %collective-permute-start.21 = (bf16[32,16,128]{2,1,0:T(8,128)(2,1)S(1)}, bf16[32,16,128]{2,1,0:T(8,128)(2,1)S(1)}, u32[]{:S(2)}, u32[]{:S(2)}) collective-permute-start(bf16[32,16,128]{2,1,0:T(8,128)(2,1)S(1)} %get-tuple-element.46), channel_id=1, source_target_pairs={{0,6},{1,7},{2,0},{3,1},{4,2},{5,3},{6,4},{7,5},{8,14},{9,15},{10,... | collective-permute-start | bytes 393224 | tf_op jit(solution)/shard_map/ppermute | solution.py:325
  65.2 6.4 %collective-permute-start.22 = (bf16[32,16,128]{2,1,0:T(8,128)(2,1)S(1)}, bf16[32,16,128]{2,1,0:T(8,128)(2,1)S(1)}, u32[]{:S(2)}, u32[]{:S(2)}) collective-permute-start(bf16[32,16,128]{2,1,0:T(8,128)(2,1)S(1)} %get-tuple-element.47), channel_id=1, source_target_pairs={{0,4},{1,5},{2,6},{3,7},{4,0},{5,1},{6,2},{7,3},{8,12},{9,13},{10,... | collective-permute-start | bytes 393224 | tf_op jit(solution)/shard_map/ppermute | solution.py:325
  65.2 9.4 %collective-permute-start.23 = (bf16[32,16,128]{2,1,0:T(8,128)(2,1)S(1)}, bf16[32,16,128]{2,1,0:T(8,128)(2,1)S(1)}, u32[]{:S(2)}, u32[]{:S(2)}) collective-permute-start(bf16[32,16,128]{2,1,0:T(8,128)(2,1)S(1)} %get-tuple-element.48), channel_id=1, source_target_pairs={{0,2},{1,3},{2,4},{3,5},{4,6},{5,7},{6,0},{7,1},{8,10},{9,11},{10,... | collective-permute-start | bytes 393224 | tf_op jit(solution)/shard_map/ppermute | solution.py:325
  65.9 8.7 %collective-permute-start.24 = (bf16[32,16,128]{2,1,0:T(8,128)(2,1)S(1)}, bf16[32,16,128]{2,1,0:T(8,128)(2,1)S(1)}, u32[]{:S(2)}, u32[]{:S(2)}) collective-permute-start(bf16[32,16,128]{2,1,0:T(8,128)(2,1)S(1)} %get-tuple-element.49), channel_id=1, source_target_pairs={{0,1},{1,0},{2,3},{3,2},{4,5},{5,4},{6,7},{7,6},{8,9},{9,8},{10,11... | collective-permute-start | bytes 393224 | tf_op jit(solution)/shard_map/ppermute | solution.py:325
  67.1 7.5 %collective-permute-start.25 = (bf16[32,16,128]{2,1,0:T(8,128)(2,1)S(1)}, bf16[32,16,128]{2,1,0:T(8,128)(2,1)S(1)}, u32[]{:S(2)}, u32[]{:S(2)}) collective-permute-start(bf16[32,16,128]{2,1,0:T(8,128)(2,1)S(1)} %get-tuple-element.50), channel_id=1, source_target_pairs={{0,7},{1,6},{2,1},{3,0},{4,3},{5,2},{6,5},{7,4},{8,15},{9,14},{10,... | collective-permute-start | bytes 393224 | tf_op jit(solution)/shard_map/ppermute | solution.py:325
  69.0 7.5 %collective-permute-start.26 = (bf16[32,16,128]{2,1,0:T(8,128)(2,1)S(1)}, bf16[32,16,128]{2,1,0:T(8,128)(2,1)S(1)}, u32[]{:S(2)}, u32[]{:S(2)}) collective-permute-start(bf16[32,16,128]{2,1,0:T(8,128)(2,1)S(1)} %get-tuple-element.51), channel_id=1, source_target_pairs={{0,5},{1,4},{2,7},{3,6},{4,1},{5,0},{6,3},{7,2},{8,13},{9,12},{10,... | collective-permute-start | bytes 393224 | tf_op jit(solution)/shard_map/ppermute | solution.py:325
  71.6 9.1 %collective-permute-start.27 = (bf16[32,16,128]{2,1,0:T(8,128)(2,1)S(1)}, bf16[32,16,128]{2,1,0:T(8,128)(2,1)S(1)}, u32[]{:S(2)}, u32[]{:S(2)}) collective-permute-start(bf16[32,16,128]{2,1,0:T(8,128)(2,1)S(1)} %get-tuple-element.52), channel_id=1, source_target_pairs={{0,3},{1,2},{2,5},{3,4},{4,7},{5,6},{6,1},{7,0},{8,11},{9,10},{10,... | collective-permute-start | bytes 393224 | tf_op jit(solution)/shard_map/ppermute | solution.py:325
  (2 other events, 1.9 us)

commit v3 on v2

--- a/solution.py
+++ b/solution.py
@@ -18,7 +18,7 @@
 
 
 def sense_kernel(info, bg, sg, *refs):
-    keeps, (give, buf) = refs[:4], refs[4:]
+    keeps, (give,), cores, buf = refs[:4], refs[4:5], refs[5:9], refs[9]
     members, tiles, _ = bg.shape
     z, k = info[0], info[1]
     pitch = tiles + 1
@@ -47,6 +47,10 @@
         sensed = sensed.astype(BF16)
         for i in range(chunk // PACK):
             sg[(chunk // PACK) * zone + i] = sensed[members * i : members * (i + 1)]
+    for d, core in enumerate(cores):
+        at = jnp.where((z + d) % 4 < 2, 0, 16)
+        for i in range(core.shape[0]):
+            core[i] = sg[at + i]
 
 
 def both_kernel(k1, k2, k3, given, *outs):
@@ -57,19 +61,23 @@
             both[n + i] = given[n * d + i]
 
 
-def pick_kernel(info, left, right, *outs):
+def pick_kernel(info, sg, left, right, *outs):
     for d, end in enumerate(outs):
-        low = (info[0] + d) % 4 < 2
-
-        @pl.when(low)
-        def _():
-            for i in range(left.shape[0]):
-                end[i] = left[i]
-
-        @pl.when(jnp.logical_not(low))
-        def _():
-            for i in range(left.shape[0]):
-                end[i] = right[i]
+        zz = (info[0] + d) % 4
+        for to, pieces in enumerate(
+            (
+                ((left, 0), (left, 16)),
+                ((left, 16), (sg, 48)),
+                ((sg, 0), (right, 0)),
+                ((right, 0), (right, 16)),
+            )
+        ):
+
+            @pl.when(zz == to)
+            def _(pieces=pieces, end=end):
+                for h, (ref, at) in enumerate(pieces):
+                    for i in range(16):
+                        end[16 * h + i] = ref[at + i]
 
 
 def cell_kernel(info, pix, spread, y, active, nbr, out, near, own_nbr, w2):
@@ -122,23 +130,26 @@
 
 
 def solve_kernel(info, nbr, *refs):
-    own, ends, (de, dn, out, gt, lt, ks) = refs[:8], refs[8:16], refs[16:]
+    own, ends, (de, dn, out, gt, lt, ks, tab) = refs[:8], refs[8:16], refs[16:]
     z, k, first, total = info[0], info[1], info[2], info[3]
     reach = 128
-    start = 16 * z - 32 + 8 * k
-    low = z < 2
-    n_end = jnp.where(low, -start, start + 8)
-    end_at = jnp.where(low, 32 + start, 0)
-    end_to = jnp.where(low, 0, 64 - start)
-    own_at = jnp.where(low, 0, start)
-    own_to = jnp.where(low, -start, 0)
+    for i in range(2):
+        tab[i, 32:96, :] = de[i]
+        tab[i, pl.ds(pl.multiple_of(jnp.where(z < 2, 0, 96), 32), 32), :] = dn[i]
+    lead = jnp.where(z == 0, 32, jnp.where(z == 3, 0, 16))
+    here = 8 * k
+    own_lo = jnp.maximum(lead, here)
+    own_hi = jnp.minimum(lead + 48, here + 72)
+    n_first = (own_lo - here) // 8
+    n_last = (here + 72 - own_hi) // 8
     mine = lax.broadcasted_iota(jnp.int32, (8, 128), 0) == (lane_id(8) >> 5)
 
-    def center(src, table, b, g):
+    def center(src, b, w):
+        g = w - here
         x = jnp.concatenate([r[b] for r in src], axis=0).astype(F32)
         mean = jnp.sum(x, axis=0, keepdims=True) * (1.0 / 128.0)
-        d = table[0, pl.ds(b, 1), :]
-        e = table[1, pl.ds(b, 1), :] - d * mean
+        d = tab[0, pl.ds(16 * z + w, 1), :]
+        e = tab[1, pl.ds(16 * z + w, 1), :] - d * mean
         a = x - mean
         turned = a.astype(BF16).T
         gt[g] = turned
@@ -149,16 +160,20 @@
 
     def own_eight(j, carry):
         for i in range(8):
-            center(own, de, own_at + 8 * j + i, own_to + 8 * j + i)
+            w = own_lo + 8 * j + i
+            center(own, w - lead, w)
         return carry
 
     def end_eight(j, carry):
+        early = j < n_first
+        w0 = jnp.where(early, here + 8 * j, own_hi + 8 * (j - n_first))
+        b0 = jnp.where(early, w0, w0 - 48)
         for i in range(8):
-            center(ends, dn, end_at + 8 * j + i, end_to + 8 * j + i)
+            center(ends, b0 + i, w0 + i)
         return carry
 
-    lax.fori_loop(0, (gt.shape[0] - n_end) // 8, own_eight, 0)
-    lax.fori_loop(0, n_end // 8, end_eight, 0)
+    lax.fori_loop(0, (own_hi - own_lo) // 8, own_eight, 0)
+    lax.fori_loop(0, n_first + n_last, end_eight, 0)
     eye = lax.broadcasted_iota(jnp.int32, (128, 128), 0) == lane_id(128)
 
     def gather(t):
@@ -337,15 +352,15 @@
         sense_kernel,
         1,
         (info, bg),
-        (shape(groups),) + (shape(tiles // 8),) * 4 + (shape(tiles // 2),),
-        [pltpu.VMEM((members * (tiles + 1) + 7, width), F32)],
+        (shape(groups),) + (shape(tiles // 8),) * 4 + (shape(tiles // 2),) + (shape(48),) * 4,
+        [pltpu.VMEM(((members + 1) * (tiles + 1) + 7, width), F32)],
     )
     left = to_cells(sg[half:], 1)
     right = to_cells(sg[:half], -1)
     keep, give = rest[:4], rest[4]
     given = to_core(give)
-    ends = list(call(pick_kernel, 1, (info, left, right), (shape(half),) * 4))
-    own = [sg] + [to_z(sg, d) for d in (1, 2, 3)]
+    ends = list(call(pick_kernel, 1, (info, sg, left, right), (shape(half),) * 4))
+    own = [rest[5]] + [to_z(rest[5 + d], d) for d in (1, 2, 3)]
     for d in (1, 2, 3):
         ends[d] = to_z(ends[d], d)
     both = call(both_kernel, 0, (*keep[1:], given), (shape(tiles // 4),) * 3)
@@ -373,19 +388,18 @@
             pltpu.VMEM((72, 128, 128), BF16),
             pltpu.VMEM((72, 128, 128), BF16),
             pltpu.VMEM((8 * 72, 128), F32),
+            pltpu.VMEM((2, 128, 128), F32),
         ],
         40,
     )
     outs = call(update_kernel, 1, (info, transform, keep[0], given, *state), (shape(32),) * 8)
-    back = [
-        outs[i] if i == 0 else home(outs[i], i % 4, i // 4) for i in range(8)
-    ]
+    back = [outs[i] if i == 0 else home(outs[i], i % 4, i // 4) for i in range(8)]
     return call(
         place_kernel,
         1,
         (info, *back),
         jax.ShapeDtypeStruct((members, tiles, width), BF16),
-        [pltpu.VMEM((2, 16 * 33, 128), F32)],
+        [pltpu.VMEM((2, 17 * 33 + 7, 128), F32)],
     )
 
 

time: 82.7 us -> 76 us (0.919)
  waiting for transfers between devices: 24 us -> 13.7 us
  starting transfers between devices: 37.8 us -> 41.3 us
    ppermute x9, waiting for transfers between devices: 14.4 us -> 1.47 us  [to_z(): return lax.ppermute(x, 'z', [(i, (i + by) % 4) for i in range(4)])]
    ppermute x9, starting transfers between devices: 11.8 us -> 16 us  [to_z(): return lax.ppermute(x, 'z', [(i, (i + by) % 4) for i in range(4)])]
    ppermute x1, waiting for transfers between devices: 0.01 us -> 4.28 us  [to_side(): return lax.ppermute(x, ('cells', 'z', 'k'), pairs)]
    ppermute x7, starting transfers between devices: 12.4 us -> 8.91 us  [home(): return lax.ppermute(x, MEM, pairs)]
    ppermute x2, waiting for transfers between devices: 3.39 us -> 0.01 us  [to_cells(): return lax.ppermute(x, 'cells', [(i, (i + by) % n) for i in range(n)])]
    ppermute x9, starting transfers between devices: 7.8 us -> 11.1 us  [to_core(): return lax.ppermute(x, 'k', [(0, 1), (1, 0)])]
    ppermute x9, waiting for transfers between devices: 0.02 us -> 1.38 us  [to_core(): return lax.ppermute(x, 'k', [(0, 1), (1, 0)])]
  transfers between devices with their start and end apart: 28 -> 28, of which waited for: 10 -> 9; matrix products, arithmetic and copies ran while one was open for 0% -> 0% of each run, Pallas kernels for 17% -> 18%
where the time goes in v3:
time: 76 us; the launch traced here: 75.9 us
  starting transfers between devices  41.3 us (54%)
  Pallas kernels  18.5 us (24%)
  waiting for transfers between devices  13.7 us (18%)
  local copies, waits for them, and re-layouts  2.04 us (3%)
    pallas_call x7, Pallas kernels, call(): pl.pallas_call(kernel, in_specs=[smem()] * n_smem + list(specs or [vmem()...  18.5 us
    ppermute x9, starting transfers between devices, to_z(): return lax.ppermute(x, 'z', [(i, (i + by) % 4) for i in range(4)])  16 us
    ppermute x9, starting transfers between devices, to_core(): return lax.ppermute(x, 'k', [(0, 1), (1, 0)])  11.1 us
    ppermute x7, starting transfers between devices, home(): return lax.ppermute(x, MEM, pairs)  8.91 us
    ppermute x7, waiting for transfers between devices, home(): return lax.ppermute(x, MEM, pairs)  6.6 us
    ppermute x2, starting transfers between devices, to_cells(): return lax.ppermute(x, 'cells', [(i, (i + by) % n) for i in range(n)])  5.18 us
    ppermute x1, waiting for transfers between devices, to_side(): return lax.ppermute(x, ('cells', 'z', 'k'), pairs)  4.28 us
    unnamed x13, local copies, waits for them, and re-layouts  2.02 us
  transfers between devices with their start and end apart: 28, of which 9 were waited for; matrix products, arithmetic and copies ran while one was open for 0% of the time, Pallas kernels for 18%

profile of v3, /device:TPU:1, one launch (start us, length us, event | category | flops | bytes accessed | tf_op | source)
XLA Modules:
  0.0 75.9 jit_solution(11583189602648773808)
XLA Ops:
  0.1 1.2 %copy-done = bf16[16,256,128]{2,1,0:T(8,128)(2,1)S(1)} copy-done((bf16[16,256,128]{2,1,0:T(8,128)(2,1)S(1)}, bf16[16,256,128]{2,1,0:T(8,128)(2,1)}, u32[]{:S(2)}) %copy-start) | copy-done | bytes 1048600
  1.3 1.2 %shard_map.65 = (bf16[64,16,128]{2,1,0:T(8,128)(2,1)S(1)}, bf16[32,16,128]{2,1,0:T(8,128)(2,1)S(1)}, bf16[32,16,128]{2,1,0:T(8,128)(2,1)S(1)}, bf16[32,16,128]{2...) custom-call(s32[4]{0:T(128)S(1)} %pad_add_fusion.info, ...), custom_call_target="tpu_custom_call" | custom-call | tf_op jit(solution)/shard_map/pallas_call | solution.py:304
  2.5 1.5 %collective-permute-start.17 = (bf16[128,16,128]{2,1,0:T(8,128)(2,1)S(1)}, bf16[128,16,128]{2,1,0:T(8,128)(2,1)S(1)}, u32[]{:S(2)}, u32[]{:S(2)}) collective-permute-start(bf16[128,16,128]{2,1,0:T(8,128)(2,1)S(1)} %get-tuple-element.46), channel_id=1, source_target_pairs={{0,1},{1,0},{2,3},{3,2},{4,5},{5,4},{6,7},{7,6},{8,9},{9,8},{10,11... | collective-permute-start | bytes 1572872 | tf_op jit(solution)/shard_map/ppermute | solution.py:319
  4.0 5.1 %collective-permute-start.8 = (bf16[32,16,128]{2,1,0:T(8,128)(2,1)S(1)}, bf16[32,16,128]{2,1,0:T(8,128)(2,1)S(1)}, u32[]{:S(2)}, u32[]{:S(2)}) collective-permute-start(bf16[32,16,128]{2,1,0:T(8,128)(2,1)S(1)} %get-tuple-element.61), channel_id=1, source_target_pairs={{0,120},{8,0},{16,8},{24,16},{32,24},{40,32},{48,40},{56,48},{64,5... | collective-permute-start | bytes 393224 | tf_op jit(solution)/shard_map/ppermute | solution.py:324
  9.3 0.6 copy-done.4
  9.9 1.9 %shard_map.64 = (f32[2,64,128]{2,1,0:T(8,128)S(1)}, f32[2,32,128]{2,1,0:T(8,128)S(1)}, s32[32,4]{1,0:T(8,128)S(1)}) custom-call(s32[4]{0:T(128)S(1)} %pad_add_fusion.info, s32[256,128]{1,0:T(8,128)S(1)} %copy-done.1, f32[256,128]{1,0:T(8,128)S(1)} %copy-done.2, f32[256,128]{1,0:T(8,128)S(1)} %copy-done.3, s32[2,128]{1,0:T(2,128)S(1)} %bitcast.4, ...), custom_call_target="tpu_custom_call" | custom-call | tf_op jit(solution)/shard_map/pallas_call | solution.py:304
  11.9 1.7 %collective-permute-start = (bf16[48,16,128]{2,1,0:T(8,128)(2,1)S(1)}, bf16[48,16,128]{2,1,0:T(8,128)(2,1)S(1)}, u32[]{:S(2)}, u32[]{:S(2)}) collective-permute-start(bf16[48,16,128]{2,1,0:T(8,128)(2,1)S(1)} %get-tuple-element.35), channel_id=1, source_target_pairs={{0,2},{2,4},{4,6},{6,0},{1,3},{3,5},{5,7},{7,1},{8,10},{10,12},{12... | collective-permute-start | bytes 589832 | tf_op jit(solution)/shard_map/ppermute | solution.py:315
  13.7 4.3 %collective-permute-done.16.refs_17_ = f32[2,32,128]{2,1,0:T(8,128)S(1)} collective-permute-done((f32[2,32,128]{2,1,0:T(8,128)S(1)}, f32[2,32,128]{2,1,0:T(8,128)S(1)}, u32[]{:S(2)}, u32[]{:S(2)}) %collective-permute-start.16) | collective-permute-done | bytes 32800 | tf_op jit(solution)/shard_map/ppermute | solution.py:335
  18.3 3.7 %collective-permute-start.2 = (bf16[48,16,128]{2,1,0:T(8,128)(2,1)S(1)}, bf16[48,16,128]{2,1,0:T(8,128)(2,1)S(1)}, u32[]{:S(2)}, u32[]{:S(2)}) collective-permute-start(bf16[48,16,128]{2,1,0:T(8,128)(2,1)S(1)} %get-tuple-element.37), channel_id=1, source_target_pairs={{0,6},{2,0},{4,2},{6,4},{1,7},{3,1},{5,3},{7,5},{8,14},{10,8},{12,... | collective-permute-start | bytes 589832 | tf_op jit(solution)/shard_map/ppermute | solution.py:315
  22.0 2.4 %collective-permute-start.3 = (bf16[48,16,128]{2,1,0:T(8,128)(2,1)S(1)}, bf16[48,16,128]{2,1,0:T(8,128)(2,1)S(1)}, u32[]{:S(2)}, u32[]{:S(2)}) collective-permute-start(bf16[48,16,128]{2,1,0:T(8,128)(2,1)S(1)} %get-tuple-element.34.refs_0_), channel_id=1, source_target_pairs={{0,1},{1,0},{2,3},{3,2},{4,5},{5,4},{6,7},{7,6},{8,9},{9,8},{10,11... | collective-permute-start | bytes 589832 | tf_op jit(solution)/shard_map/ppermute | solution.py:319
  24.4 0.7 shard_map.66
  25.1 1.5 %collective-permute-done.1.refs_2_ = bf16[48,16,128]{2,1,0:T(8,128)(2,1)S(1)} collective-permute-done((bf16[48,16,128]{2,1,0:T(8,128)(2,1)S(1)}, bf16[48,16,128]{2,1,0:T(8,128)(2,1)S(1)}, u32[]{:S(2)}, u32[]{:S(2)}) %collective-permute-start.1) | collective-permute-done | bytes 196640 | tf_op jit(solution)/shard_map/ppermute | solution.py:315
  26.6 0.8 %collective-permute-start.10 = (bf16[32,16,128]{2,1,0:T(8,128)(2,1)S(1)}, bf16[32,16,128]{2,1,0:T(8,128)(2,1)S(1)}, u32[]{:S(2)}, u32[]{:S(2)}) collective-permute-start(bf16[32,16,128]{2,1,0:T(8,128)(2,1)S(1)} %get-tuple-element.41), channel_id=1, source_target_pairs={{0,4},{2,6},{4,0},{6,2},{1,5},{3,7},{5,1},{7,3},{8,12},{10,14},{12... | collective-permute-start | bytes 393224 | tf_op jit(solution)/shard_map/ppermute | solution.py:315
  27.4 3.2 %collective-permute-start.11 = (bf16[32,16,128]{2,1,0:T(8,128)(2,1)S(1)}, bf16[32,16,128]{2,1,0:T(8,128)(2,1)S(1)}, u32[]{:S(2)}, u32[]{:S(2)}) collective-permute-start(bf16[32,16,128]{2,1,0:T(8,128)(2,1)S(1)} %get-tuple-element.42), channel_id=1, source_target_pairs={{0,6},{2,0},{4,2},{6,4},{1,7},{3,1},{5,3},{7,5},{8,14},{10,8},{12,... | collective-permute-start | bytes 393224 | tf_op jit(solution)/shard_map/ppermute | solution.py:315
  30.6 3.3 %collective-permute-start.12 = (bf16[32,16,128]{2,1,0:T(8,128)(2,1)S(1)}, bf16[32,16,128]{2,1,0:T(8,128)(2,1)S(1)}, u32[]{:S(2)}, u32[]{:S(2)}) collective-permute-start(bf16[32,16,128]{2,1,0:T(8,128)(2,1)S(1)} %get-tuple-element.39.refs_8_), channel_id=1, source_target_pairs={{0,1},{1,0},{2,3},{3,2},{4,5},{5,4},{6,7},{7,6},{8,9},{9,8},{10,11... | collective-permute-start | bytes 393224 | tf_op jit(solution)/shard_map/ppermute | solution.py:319
  33.9 1.2 %collective-permute-start.4 = (bf16[48,16,128]{2,1,0:T(8,128)(2,1)S(1)}, bf16[48,16,128]{2,1,0:T(8,128)(2,1)S(1)}, u32[]{:S(2)}, u32[]{:S(2)}) collective-permute-start(bf16[48,16,128]{2,1,0:T(8,128)(2,1)S(1)} %collective-permute-done.refs_1_), channel_id=1, source_target_pairs={{0,1},{1,0},{2,3},{3,2},{4,5},{5,4},{6,7},{7,6},{8,9},{9,8},{10,11... | collective-permute-start | bytes 589832 | tf_op jit(solution)/shard_map/ppermute | solution.py:319
  35.1 1.3 %collective-permute-start.14 = (bf16[32,16,128]{2,1,0:T(8,128)(2,1)S(1)}, bf16[32,16,128]{2,1,0:T(8,128)(2,1)S(1)}, u32[]{:S(2)}, u32[]{:S(2)}) collective-permute-start(bf16[32,16,128]{2,1,0:T(8,128)(2,1)S(1)} %collective-permute-done.10.refs_10_), channel_id=1, source_target_pairs={{0,1},{1,0},{2,3},{3,2},{4,5},{5,4},{6,7},{7,6},{8,9},{9,8},{10,11... | collective-permute-start | bytes 393224 | tf_op jit(solution)/shard_map/ppermute | solution.py:319
  36.5 2.2 %collective-permute-start.18 = (bf16[64,16,128]{2,1,0:T(8,128)(2,1)S(1)}, bf16[64,16,128]{2,1,0:T(8,128)(2,1)S(1)}, u32[]{:S(2)}, u32[]{:S(2)}) collective-permute-start(bf16[64,16,128]{2,1,0:T(8,128)(2,1)S(1)} %get-tuple-element.50), channel_id=1, source_target_pairs={{0,2},{2,4},{4,6},{6,0},{1,3},{3,5},{5,7},{7,1},{8,10},{10,12},{12... | collective-permute-start | bytes 786440 | tf_op jit(solution)/shard_map/ppermute | solution.py:315
  38.7 2.4 %collective-permute-start.19 = (bf16[64,16,128]{2,1,0:T(8,128)(2,1)S(1)}, bf16[64,16,128]{2,1,0:T(8,128)(2,1)S(1)}, u32[]{:S(2)}, u32[]{:S(2)}) collective-permute-start(bf16[64,16,128]{2,1,0:T(8,128)(2,1)S(1)} %get-tuple-element.51), channel_id=1, source_target_pairs={{0,4},{2,6},{4,0},{6,2},{1,5},{3,7},{5,1},{7,3},{8,12},{10,14},{12... | collective-permute-start | bytes 786440 | tf_op jit(solution)/shard_map/ppermute | solution.py:315
  41.1 1.6 %collective-permute-start.20 = (bf16[64,16,128]{2,1,0:T(8,128)(2,1)S(1)}, bf16[64,16,128]{2,1,0:T(8,128)(2,1)S(1)}, u32[]{:S(2)}, u32[]{:S(2)}) collective-permute-start(bf16[64,16,128]{2,1,0:T(8,128)(2,1)S(1)} %get-tuple-element.52), channel_id=1, source_target_pairs={{0,6},{2,0},{4,2},{6,4},{1,7},{3,1},{5,3},{7,5},{8,14},{10,8},{12,... | collective-permute-start | bytes 786440 | tf_op jit(solution)/shard_map/ppermute | solution.py:315
  42.7 1.3 %collective-permute-start.5 = (bf16[48,16,128]{2,1,0:T(8,128)(2,1)S(1)}, bf16[48,16,128]{2,1,0:T(8,128)(2,1)S(1)}, u32[]{:S(2)}, u32[]{:S(2)}) collective-permute-start(bf16[48,16,128]{2,1,0:T(8,128)(2,1)S(1)} %collective-permute-done.1.refs_2_), channel_id=1, source_target_pairs={{0,1},{1,0},{2,3},{3,2},{4,5},{5,4},{6,7},{7,6},{8,9},{9,8},{10,11... | collective-permute-start | bytes 589832 | tf_op jit(solution)/shard_map/ppermute | solution.py:319
  44.1 1.0 %collective-permute-done.5.refs_6_ = bf16[48,16,128]{2,1,0:T(8,128)(2,1)S(1)} collective-permute-done((bf16[48,16,128]{2,1,0:T(8,128)(2,1)S(1)}, bf16[48,16,128]{2,1,0:T(8,128)(2,1)S(1)}, u32[]{:S(2)}, u32[]{:S(2)}) %collective-permute-start.5) | collective-permute-done | bytes 196640 | tf_op jit(solution)/shard_map/ppermute | solution.py:319
  45.5 11.4 %shard_map.67.tr = bf16[32,128,128]{2,1,0:T(8,128)(2,1)S(1)} custom-call(s32[4]{0:T(128)S(1)} %pad_add_fusion.info, s32[32,4]{1,0:T(8,128)S(1)} %get-tuple-element.33.nbr, bf16[48,16,128]{2,1,0:T(8,128)(2,1)S(1)} %get-tuple-element.34.refs_0_, bf16[48,16,128]{2,1,0:T(8,128)(2,1)S(1)} %collective-permute-done.refs_1_, ...), custom_call_target="tpu_custom_call" | custom-call | tf_op jit(solution)/shard_map/pallas_call | solution.py:304
  56.9 1.6 %shard_map.69 = (bf16[32,16,128]{2,1,0:T(8,128)(2,1)S(1)}, bf16[32,16,128]{2,1,0:T(8,128)(2,1)S(1)}, bf16[32,16,128]{2,1,0:T(8,128)(2,1)S(1)}, bf16[32,16,128]{2...) custom-call(s32[4]{0:T(128)S(1)} %pad_add_fusion.info, ...), custom_call_target="tpu_custom_call" | custom-call | tf_op jit(solution)/shard_map/pallas_call | solution.py:304
  58.6 1.6 %collective-permute-start.22 = (bf16[32,16,128]{2,1,0:T(8,128)(2,1)S(1)}, bf16[32,16,128]{2,1,0:T(8,128)(2,1)S(1)}, u32[]{:S(2)}, u32[]{:S(2)}) collective-permute-start(bf16[32,16,128]{2,1,0:T(8,128)(2,1)S(1)} %get-tuple-element.55), channel_id=1, source_target_pairs={{0,4},{1,5},{2,6},{3,7},{4,0},{5,1},{6,2},{7,3},{8,12},{9,13},{10,... | collective-permute-start | bytes 393224 | tf_op jit(solution)/shard_map/ppermute | solution.py:340
  60.2 0.8 %collective-permute-start.24 = (bf16[32,16,128]{2,1,0:T(8,128)(2,1)S(1)}, bf16[32,16,128]{2,1,0:T(8,128)(2,1)S(1)}, u32[]{:S(2)}, u32[]{:S(2)}) collective-permute-start(bf16[32,16,128]{2,1,0:T(8,128)(2,1)S(1)} %get-tuple-element.57), channel_id=1, source_target_pairs={{0,1},{1,0},{2,3},{3,2},{4,5},{5,4},{6,7},{7,6},{8,9},{9,8},{10,11... | collective-permute-start | bytes 393224 | tf_op jit(solution)/shard_map/ppermute | solution.py:340
  61.1 2.8 %collective-permute-start.25 = (bf16[32,16,128]{2,1,0:T(8,128)(2,1)S(1)}, bf16[32,16,128]{2,1,0:T(8,128)(2,1)S(1)}, u32[]{:S(2)}, u32[]{:S(2)}) collective-permute-start(bf16[32,16,128]{2,1,0:T(8,128)(2,1)S(1)} %get-tuple-element.58), channel_id=1, source_target_pairs={{0,7},{1,6},{2,1},{3,0},{4,3},{5,2},{6,5},{7,4},{8,15},{9,14},{10,... | collective-permute-start | bytes 393224 | tf_op jit(solution)/shard_map/ppermute | solution.py:340
  63.9 0.8 %collective-permute-start.26 = (bf16[32,16,128]{2,1,0:T(8,128)(2,1)S(1)}, bf16[32,16,128]{2,1,0:T(8,128)(2,1)S(1)}, u32[]{:S(2)}, u32[]{:S(2)}) collective-permute-start(bf16[32,16,128]{2,1,0:T(8,128)(2,1)S(1)} %get-tuple-element.59), channel_id=1, source_target_pairs={{0,5},{1,4},{2,7},{3,6},{4,1},{5,0},{6,3},{7,2},{8,13},{9,12},{10,... | collective-permute-start | bytes 393224 | tf_op jit(solution)/shard_map/ppermute | solution.py:340
  65.0 2.7 %collective-permute-start.27 = (bf16[32,16,128]{2,1,0:T(8,128)(2,1)S(1)}, bf16[32,16,128]{2,1,0:T(8,128)(2,1)S(1)}, u32[]{:S(2)}, u32[]{:S(2)}) collective-permute-start(bf16[32,16,128]{2,1,0:T(8,128)(2,1)S(1)} %get-tuple-element.60), channel_id=1, source_target_pairs={{0,3},{1,2},{2,5},{3,4},{4,7},{5,6},{6,1},{7,0},{8,11},{9,10},{10,... | collective-permute-start | bytes 393224 | tf_op jit(solution)/shard_map/ppermute | solution.py:340
  68.3 2.2 %collective-permute-done.25.refs_5_ = bf16[32,16,128]{2,1,0:T(8,128)(2,1)S(1)} collective-permute-done((bf16[32,16,128]{2,1,0:T(8,128)(2,1)S(1)}, bf16[32,16,128]{2,1,0:T(8,128)(2,1)S(1)}, u32[]{:S(2)}, u32[]{:S(2)}) %collective-permute-start.25) | collective-permute-done | bytes 131104 | tf_op jit(solution)/shard_map/ppermute | solution.py:340
  70.9 3.1 %collective-permute-done.27.refs_7_ = bf16[32,16,128]{2,1,0:T(8,128)(2,1)S(1)} collective-permute-done((bf16[32,16,128]{2,1,0:T(8,128)(2,1)S(1)}, bf16[32,16,128]{2,1,0:T(8,128)(2,1)S(1)}, u32[]{:S(2)}, u32[]{:S(2)}) %collective-permute-start.27) | collective-permute-done | bytes 131104 | tf_op jit(solution)/shard_map/ppermute | solution.py:340
  74.0 1.8 %shard_map.70 = bf16[16,256,128]{2,1,0:T(8,128)(2,1)} custom-call(s32[4]{0:T(128)S(1)} %pad_add_fusion.info, bf16[32,16,128]{2,1,0:T(8,128)(2,1)S(1)} %get-tuple-element.53.refs_0_, bf16[32,16,128]{2,1,0:T(8,128)(2,1)S(1)} %collective-permute-done.21.refs_1_, bf16[32,16,128]{2,1,0:T(8,128)(2,1)S(1)} %collective-permute-done.22.refs_2_, ...), custom_call_target="tpu_custom_call" | custom-call | tf_op jit(solution)/shard_map/pallas_call | solution.py:304
  (46 shorter events, 2.7 us)
Async XLA Ops:
  2.5 33.9 %collective-permute-start.17 = (bf16[128,16,128]{2,1,0:T(8,128)(2,1)S(1)}, bf16[128,16,128]{2,1,0:T(8,128)(2,1)S(1)}, u32[]{:S(2)}, u32[]{:S(2)}) collective-permute-start(bf16[128,16,128]{2,1,0:T(8,128)(2,1)S(1)} %get-tuple-element.46), channel_id=1, source_target_pairs={{0,1},{1,0},{2,3},{3,2},{4,5},{5,4},{6,7},{7,6},{8,9},{9,8},{10,11... | collective-permute-start | bytes 1572872 | tf_op jit(solution)/shard_map/ppermute | solution.py:319
  3.9 5.2 %copy-start.5 = (s32[256,4]{0,1:T(4,128)S(1)}, s32[256,4]{0,1:T(4,128)}, u32[]{:S(2)}) copy-start(s32[256,4]{0,1:T(4,128)} %param.11) | copy-start | bytes 12292
  3.9 5.3 %copy-start.2 = (f32[256,128]{1,0:T(8,128)S(1)}, f32[256,128]{1,0:T(8,128)}, u32[]{:S(2)}) copy-start(f32[256,128]{1,0:T(8,128)} %spread.1) | copy-start | bytes 393220
  3.9 5.3 %copy-start.3 = (f32[256,128]{1,0:T(8,128)S(1)}, f32[256,128]{1,0:T(8,128)}, u32[]{:S(2)}) copy-start(f32[256,128]{1,0:T(8,128)} %y.1) | copy-start | bytes 393220
  4.0 5.3 %copy-start.1 = (s32[256,128]{1,0:T(8,128)S(1)}, s32[256,128]{1,0:T(8,128)}, u32[]{:S(2)}) copy-start(s32[256,128]{1,0:T(8,128)} %pix.1) | copy-start | bytes 393220
  4.0 14.3 %collective-permute-start.8 = (bf16[32,16,128]{2,1,0:T(8,128)(2,1)S(1)}, bf16[32,16,128]{2,1,0:T(8,128)(2,1)S(1)}, u32[]{:S(2)}, u32[]{:S(2)}) collective-permute-start(bf16[32,16,128]{2,1,0:T(8,128)(2,1)S(1)} %get-tuple-element.61), channel_id=1, source_target_pairs={{0,120},{8,0},{16,8},{24,16},{32,24},{40,32},{48,40},{56,48},{64,5... | collective-permute-start | bytes 393224 | tf_op jit(solution)/shard_map/ppermute | solution.py:324
  11.8 6.2 %collective-permute-start.16 = (f32[2,32,128]{2,1,0:T(8,128)S(1)}, f32[2,32,128]{2,1,0:T(8,128)S(1)}, u32[]{:S(2)}, u32[]{:S(2)}) collective-permute-start(f32[2,32,128]{2,1,0:T(8,128)S(1)} %get-tuple-element.44), channel_id=1, source_target_pairs={{0,8},{1,9},{2,10},{3,11},{4,124},{5,125},{6,126},{7,127},{8,16},{... | collective-permute-start | bytes 98312 | tf_op jit(solution)/shard_map/ppermute | solution.py:335
  11.9 10.1 %collective-permute-start.7 = (bf16[32,16,128]{2,1,0:T(8,128)(2,1)S(1)}, bf16[32,16,128]{2,1,0:T(8,128)(2,1)S(1)}, u32[]{:S(2)}, u32[]{:S(2)}) collective-permute-start(bf16[32,16,128]{2,1,0:T(8,128)(2,1)S(1)} %get-tuple-element.62), channel_id=1, source_target_pairs={{0,8},{8,16},{16,24},{24,32},{32,40},{40,48},{48,56},{56,64},{64,7... | collective-permute-start | bytes 393224 | tf_op jit(solution)/shard_map/ppermute | solution.py:324
  11.9 13.1 %collective-permute-start = (bf16[48,16,128]{2,1,0:T(8,128)(2,1)S(1)}, bf16[48,16,128]{2,1,0:T(8,128)(2,1)S(1)}, u32[]{:S(2)}, u32[]{:S(2)}) collective-permute-start(bf16[48,16,128]{2,1,0:T(8,128)(2,1)S(1)} %get-tuple-element.35), channel_id=1, source_target_pairs={{0,2},{2,4},{4,6},{6,0},{1,3},{3,5},{5,7},{7,1},{8,10},{10,12},{12... | collective-permute-start | bytes 589832 | tf_op jit(solution)/shard_map/ppermute | solution.py:315
  17.9 8.6 %collective-permute-start.1 = (bf16[48,16,128]{2,1,0:T(8,128)(2,1)S(1)}, bf16[48,16,128]{2,1,0:T(8,128)(2,1)S(1)}, u32[]{:S(2)}, u32[]{:S(2)}) collective-permute-start(bf16[48,16,128]{2,1,0:T(8,128)(2,1)S(1)} %get-tuple-element.36), channel_id=1, source_target_pairs={{0,4},{2,6},{4,0},{6,2},{1,5},{3,7},{5,1},{7,3},{8,12},{10,14},{12... | collective-permute-start | bytes 589832 | tf_op jit(solution)/shard_map/ppermute | solution.py:315
  18.3 9.1 %collective-permute-start.2 = (bf16[48,16,128]{2,1,0:T(8,128)(2,1)S(1)}, bf16[48,16,128]{2,1,0:T(8,128)(2,1)S(1)}, u32[]{:S(2)}, u32[]{:S(2)}) collective-permute-start(bf16[48,16,128]{2,1,0:T(8,128)(2,1)S(1)} %get-tuple-element.37), channel_id=1, source_target_pairs={{0,6},{2,0},{4,2},{6,4},{1,7},{3,1},{5,3},{7,5},{8,14},{10,8},{12,... | collective-permute-start | bytes 589832 | tf_op jit(solution)/shard_map/ppermute | solution.py:315
  22.0 8.6 %collective-permute-start.3 = (bf16[48,16,128]{2,1,0:T(8,128)(2,1)S(1)}, bf16[48,16,128]{2,1,0:T(8,128)(2,1)S(1)}, u32[]{:S(2)}, u32[]{:S(2)}) collective-permute-start(bf16[48,16,128]{2,1,0:T(8,128)(2,1)S(1)} %get-tuple-element.34.refs_0_), channel_id=1, source_target_pairs={{0,1},{1,0},{2,3},{3,2},{4,5},{5,4},{6,7},{7,6},{8,9},{9,8},{10,11... | collective-permute-start | bytes 589832 | tf_op jit(solution)/shard_map/ppermute | solution.py:319
  25.0 8.8 %collective-permute-start.9 = (bf16[32,16,128]{2,1,0:T(8,128)(2,1)S(1)}, bf16[32,16,128]{2,1,0:T(8,128)(2,1)S(1)}, u32[]{:S(2)}, u32[]{:S(2)}) collective-permute-start(bf16[32,16,128]{2,1,0:T(8,128)(2,1)S(1)} %get-tuple-element.40), channel_id=1, source_target_pairs={{0,2},{2,4},{4,6},{6,0},{1,3},{3,5},{5,7},{7,1},{8,10},{10,12},{12... | collective-permute-start | bytes 393224 | tf_op jit(solution)/shard_map/ppermute | solution.py:315
  26.6 8.5 %collective-permute-start.10 = (bf16[32,16,128]{2,1,0:T(8,128)(2,1)S(1)}, bf16[32,16,128]{2,1,0:T(8,128)(2,1)S(1)}, u32[]{:S(2)}, u32[]{:S(2)}) collective-permute-start(bf16[32,16,128]{2,1,0:T(8,128)(2,1)S(1)} %get-tuple-element.41), channel_id=1, source_target_pairs={{0,4},{2,6},{4,0},{6,2},{1,5},{3,7},{5,1},{7,3},{8,12},{10,14},{12... | collective-permute-start | bytes 393224 | tf_op jit(solution)/shard_map/ppermute | solution.py:315
  27.4 7.6 %collective-permute-start.11 = (bf16[32,16,128]{2,1,0:T(8,128)(2,1)S(1)}, bf16[32,16,128]{2,1,0:T(8,128)(2,1)S(1)}, u32[]{:S(2)}, u32[]{:S(2)}) collective-permute-start(bf16[32,16,128]{2,1,0:T(8,128)(2,1)S(1)} %get-tuple-element.42), channel_id=1, source_target_pairs={{0,6},{2,0},{4,2},{6,4},{1,7},{3,1},{5,3},{7,5},{8,14},{10,8},{12,... | collective-permute-start | bytes 393224 | tf_op jit(solution)/shard_map/ppermute | solution.py:315
  30.6 5.9 %collective-permute-start.12 = (bf16[32,16,128]{2,1,0:T(8,128)(2,1)S(1)}, bf16[32,16,128]{2,1,0:T(8,128)(2,1)S(1)}, u32[]{:S(2)}, u32[]{:S(2)}) collective-permute-start(bf16[32,16,128]{2,1,0:T(8,128)(2,1)S(1)} %get-tuple-element.39.refs_8_), channel_id=1, source_target_pairs={{0,1},{1,0},{2,3},{3,2},{4,5},{5,4},{6,7},{7,6},{8,9},{9,8},{10,11... | collective-permute-start | bytes 393224 | tf_op jit(solution)/shard_map/ppermute | solution.py:319
  33.9 10.2 %collective-permute-start.4 = (bf16[48,16,128]{2,1,0:T(8,128)(2,1)S(1)}, bf16[48,16,128]{2,1,0:T(8,128)(2,1)S(1)}, u32[]{:S(2)}, u32[]{:S(2)}) collective-permute-start(bf16[48,16,128]{2,1,0:T(8,128)(2,1)S(1)} %collective-permute-done.refs_1_), channel_id=1, source_target_pairs={{0,1},{1,0},{2,3},{3,2},{4,5},{5,4},{6,7},{7,6},{8,9},{9,8},{10,11... | collective-permute-start | bytes 589832 | tf_op jit(solution)/shard_map/ppermute | solution.py:319
  35.0 3.7 %collective-permute-start.13 = (bf16[32,16,128]{2,1,0:T(8,128)(2,1)S(1)}, bf16[32,16,128]{2,1,0:T(8,128)(2,1)S(1)}, u32[]{:S(2)}, u32[]{:S(2)}) collective-permute-start(bf16[32,16,128]{2,1,0:T(8,128)(2,1)S(1)} %collective-permute-done.9.refs_9_), channel_id=1, source_target_pairs={{0,1},{1,0},{2,3},{3,2},{4,5},{5,4},{6,7},{7,6},{8,9},{9,8},{10,11... | collective-permute-start | bytes 393224 | tf_op jit(solution)/shard_map/ppermute | solution.py:319
  35.1 6.0 %collective-permute-start.14 = (bf16[32,16,128]{2,1,0:T(8,128)(2,1)S(1)}, bf16[32,16,128]{2,1,0:T(8,128)(2,1)S(1)}, u32[]{:S(2)}, u32[]{:S(2)}) collective-permute-start(bf16[32,16,128]{2,1,0:T(8,128)(2,1)S(1)} %collective-permute-done.10.refs_10_), channel_id=1, source_target_pairs={{0,1},{1,0},{2,3},{3,2},{4,5},{5,4},{6,7},{7,6},{8,9},{9,8},{10,11... | collective-permute-start | bytes 393224 | tf_op jit(solution)/shard_map/ppermute | solution.py:319
  36.4 6.3 %collective-permute-start.15 = (bf16[32,16,128]{2,1,0:T(8,128)(2,1)S(1)}, bf16[32,16,128]{2,1,0:T(8,128)(2,1)S(1)}, u32[]{:S(2)}, u32[]{:S(2)}) collective-permute-start(bf16[32,16,128]{2,1,0:T(8,128)(2,1)S(1)} %collective-permute-done.11.refs_11_), channel_id=1, source_target_pairs={{0,1},{1,0},{2,3},{3,2},{4,5},{5,4},{6,7},{7,6},{8,9},{9,8},{10,11... | collective-permute-start | bytes 393224 | tf_op jit(solution)/shard_map/ppermute | solution.py:319
  36.5 20.4 %collective-permute-start.18 = (bf16[64,16,128]{2,1,0:T(8,128)(2,1)S(1)}, bf16[64,16,128]{2,1,0:T(8,128)(2,1)S(1)}, u32[]{:S(2)}, u32[]{:S(2)}) collective-permute-start(bf16[64,16,128]{2,1,0:T(8,128)(2,1)S(1)} %get-tuple-element.50), channel_id=1, source_target_pairs={{0,2},{2,4},{4,6},{6,0},{1,3},{3,5},{5,7},{7,1},{8,10},{10,12},{12... | collective-permute-start | bytes 786440 | tf_op jit(solution)/shard_map/ppermute | solution.py:315
  38.7 18.2 %collective-permute-start.19 = (bf16[64,16,128]{2,1,0:T(8,128)(2,1)S(1)}, bf16[64,16,128]{2,1,0:T(8,128)(2,1)S(1)}, u32[]{:S(2)}, u32[]{:S(2)}) collective-permute-start(bf16[64,16,128]{2,1,0:T(8,128)(2,1)S(1)} %get-tuple-element.51), channel_id=1, source_target_pairs={{0,4},{2,6},{4,0},{6,2},{1,5},{3,7},{5,1},{7,3},{8,12},{10,14},{12... | collective-permute-start | bytes 786440 | tf_op jit(solution)/shard_map/ppermute | solution.py:315
  41.1 15.8 %collective-permute-start.20 = (bf16[64,16,128]{2,1,0:T(8,128)(2,1)S(1)}, bf16[64,16,128]{2,1,0:T(8,128)(2,1)S(1)}, u32[]{:S(2)}, u32[]{:S(2)}) collective-permute-start(bf16[64,16,128]{2,1,0:T(8,128)(2,1)S(1)} %get-tuple-element.52), channel_id=1, source_target_pairs={{0,6},{2,0},{4,2},{6,4},{1,7},{3,1},{5,3},{7,5},{8,14},{10,8},{12,... | collective-permute-start | bytes 786440 | tf_op jit(solution)/shard_map/ppermute | solution.py:315
  42.7 2.4 %collective-permute-start.5 = (bf16[48,16,128]{2,1,0:T(8,128)(2,1)S(1)}, bf16[48,16,128]{2,1,0:T(8,128)(2,1)S(1)}, u32[]{:S(2)}, u32[]{:S(2)}) collective-permute-start(bf16[48,16,128]{2,1,0:T(8,128)(2,1)S(1)} %collective-permute-done.1.refs_2_), channel_id=1, source_target_pairs={{0,1},{1,0},{2,3},{3,2},{4,5},{5,4},{6,7},{7,6},{8,9},{9,8},{10,11... | collective-permute-start | bytes 589832 | tf_op jit(solution)/shard_map/ppermute | solution.py:319
  44.0 1.4 %collective-permute-start.6 = (bf16[48,16,128]{2,1,0:T(8,128)(2,1)S(1)}, bf16[48,16,128]{2,1,0:T(8,128)(2,1)S(1)}, u32[]{:S(2)}, u32[]{:S(2)}) collective-permute-start(bf16[48,16,128]{2,1,0:T(8,128)(2,1)S(1)} %collective-permute-done.2.refs_3_), channel_id=1, source_target_pairs={{0,1},{1,0},{2,3},{3,2},{4,5},{5,4},{6,7},{7,6},{8,9},{9,8},{10,11... | collective-permute-start | bytes 589832 | tf_op jit(solution)/shard_map/ppermute | solution.py:319
  58.5 5.4 %collective-permute-start.21 = (bf16[32,16,128]{2,1,0:T(8,128)(2,1)S(1)}, bf16[32,16,128]{2,1,0:T(8,128)(2,1)S(1)}, u32[]{:S(2)}, u32[]{:S(2)}) collective-permute-start(bf16[32,16,128]{2,1,0:T(8,128)(2,1)S(1)} %get-tuple-element.54), channel_id=1, source_target_pairs={{0,6},{1,7},{2,0},{3,1},{4,2},{5,3},{6,4},{7,5},{8,14},{9,15},{10,... | collective-permute-start | bytes 393224 | tf_op jit(solution)/shard_map/ppermute | solution.py:340
  58.6 6.4 %collective-permute-start.22 = (bf16[32,16,128]{2,1,0:T(8,128)(2,1)S(1)}, bf16[32,16,128]{2,1,0:T(8,128)(2,1)S(1)}, u32[]{:S(2)}, u32[]{:S(2)}) collective-permute-start(bf16[32,16,128]{2,1,0:T(8,128)(2,1)S(1)} %get-tuple-element.55), channel_id=1, source_target_pairs={{0,4},{1,5},{2,6},{3,7},{4,0},{5,1},{6,2},{7,3},{8,12},{9,13},{10,... | collective-permute-start | bytes 393224 | tf_op jit(solution)/shard_map/ppermute | solution.py:340
  60.2 8.0 %collective-permute-start.23 = (bf16[32,16,128]{2,1,0:T(8,128)(2,1)S(1)}, bf16[32,16,128]{2,1,0:T(8,128)(2,1)S(1)}, u32[]{:S(2)}, u32[]{:S(2)}) collective-permute-start(bf16[32,16,128]{2,1,0:T(8,128)(2,1)S(1)} %get-tuple-element.56), channel_id=1, source_target_pairs={{0,2},{1,3},{2,4},{3,5},{4,6},{5,7},{6,0},{7,1},{8,10},{9,11},{10,... | collective-permute-start | bytes 393224 | tf_op jit(solution)/shard_map/ppermute | solution.py:340
  60.2 8.0 %collective-permute-start.24 = (bf16[32,16,128]{2,1,0:T(8,128)(2,1)S(1)}, bf16[32,16,128]{2,1,0:T(8,128)(2,1)S(1)}, u32[]{:S(2)}, u32[]{:S(2)}) collective-permute-start(bf16[32,16,128]{2,1,0:T(8,128)(2,1)S(1)} %get-tuple-element.57), channel_id=1, source_target_pairs={{0,1},{1,0},{2,3},{3,2},{4,5},{5,4},{6,7},{7,6},{8,9},{9,8},{10,11... | collective-permute-start | bytes 393224 | tf_op jit(solution)/shard_map/ppermute | solution.py:340
  61.1 9.4 %collective-permute-start.25 = (bf16[32,16,128]{2,1,0:T(8,128)(2,1)S(1)}, bf16[32,16,128]{2,1,0:T(8,128)(2,1)S(1)}, u32[]{:S(2)}, u32[]{:S(2)}) collective-permute-start(bf16[32,16,128]{2,1,0:T(8,128)(2,1)S(1)} %get-tuple-element.58), channel_id=1, source_target_pairs={{0,7},{1,6},{2,1},{3,0},{4,3},{5,2},{6,5},{7,4},{8,15},{9,14},{10,... | collective-permute-start | bytes 393224 | tf_op jit(solution)/shard_map/ppermute | solution.py:340
  63.9 7.0 %collective-permute-start.26 = (bf16[32,16,128]{2,1,0:T(8,128)(2,1)S(1)}, bf16[32,16,128]{2,1,0:T(8,128)(2,1)S(1)}, u32[]{:S(2)}, u32[]{:S(2)}) collective-permute-start(bf16[32,16,128]{2,1,0:T(8,128)(2,1)S(1)} %get-tuple-element.59), channel_id=1, source_target_pairs={{0,5},{1,4},{2,7},{3,6},{4,1},{5,0},{6,3},{7,2},{8,13},{9,12},{10,... | collective-permute-start | bytes 393224 | tf_op jit(solution)/shard_map/ppermute | solution.py:340
  65.0 9.1 %collective-permute-start.27 = (bf16[32,16,128]{2,1,0:T(8,128)(2,1)S(1)}, bf16[32,16,128]{2,1,0:T(8,128)(2,1)S(1)}, u32[]{:S(2)}, u32[]{:S(2)}) collective-permute-start(bf16[32,16,128]{2,1,0:T(8,128)(2,1)S(1)} %get-tuple-element.60), channel_id=1, source_target_pairs={{0,3},{1,2},{2,5},{3,4},{4,7},{5,6},{6,1},{7,0},{8,11},{9,10},{10,... | collective-permute-start | bytes 393224 | tf_op jit(solution)/shard_map/ppermute | solution.py:340
  (2 other events, 1.9 us)
